TPU v7x, 512 devices: a whole 4x4x16 slice. The times are simulated.
512 devices in a mesh: ep: 64 (over x, z), tp: 8 (over y, core).
Axes of the slice: x: 4, y: 4, z: 16, core: 2. Of those that a mesh axis runs over, the one named last changes fastest.
Arguments:
- tokens: bfloat16 [1024, 4096], P('ep', 'tp'), may hold values from -6 to 6
- expert_ids: int32 [1024, 8], P('ep'), may hold values from 0 to 63, as said below
- route_weight: float32 [1024, 8], P('ep'), may hold values from 0.05 to 0.6
- gate_weight: bfloat16 [64, 1536, 4096], P('ep', 'tp'), may hold values from -0.09375 to 0.09375
- up_weight: bfloat16 [64, 1536, 4096], P('ep', 'tp'), may hold values from -0.09375 to 0.09375
- down_weight: bfloat16 [64, 1536, 4096], P('ep', 'tp'), may hold values from -0.21875 to 0.21875
Outputs:
- moe_out: bfloat16 [1024, 4096], P('ep', 'tp')
- act_absmax: float32 [2, 64], P(None, 'ep')
Inputs may be any that keep to these rules, and one draw needn't show every extreme that they name: `expert_ids`: each row names 8 different experts. Exactly 2 experts are named more than 2 times among the rows of one index of ep, in every such block, and at most 8 times; one of them is named exactly 8 times in every block, the other reaches 8 in some block. Every other expert is named at most 2 times among the rows of one index of ep, and one of them exactly 2 times in every block.
All inputs are finite; a program needn't handle non-finite values.
Results may differ from a plain program's by a relative error of at most 0.015.
Values may be sent and summed in bfloat16 or wider, within the bound.
No kernel may reach another device: no remote copies, remote signals or barrier semaphores. Data moves between devices by JAX's collectives and lax.ppermute only.
A program may use at most 64 MiB of HBM per device.

v0:
```python
import jax
import jax.numpy as jnp
import numpy as np
from jax import lax
from jax.experimental import pallas as pl
from jax.experimental.pallas import tpu as pltpu
from jax.sharding import Mesh, PartitionSpec as P


TOP = 8
SLOTS = 8
CORES = 2
X = 4
LANES = 128
BF = jnp.bfloat16
F32 = jnp.float32


IN_VMEM = pl.BlockSpec(memory_space=pltpu.VMEM)
IN_PLACE = pl.BlockSpec(memory_space=pltpu.HBM)
IN_SMEM = pl.BlockSpec(memory_space=pltpu.SMEM)
ROOM = pltpu.CompilerParams(vmem_limit_bytes=24 << 20)


def local(array):
    return pltpu.with_memory_space_constraint(array, pltpu.VMEM)


def remote(array):
    return pltpu.with_memory_space_constraint(array, pltpu.HBM)


def dot_nt(a, b):
    return lax.dot_general(a, b, (((1,), (1,)), ((), ())), preferred_element_type=F32)


def dot_nn(a, b):
    return lax.dot_general(a, b, (((1,), (0,)), ((), ())), preferred_element_type=F32)


def iota(shape, axis):
    return lax.broadcasted_iota(jnp.int32, shape, axis)


def call(kernel, order, inputs, out_shape, scratch=(), cost=None):
    single = isinstance(out_shape, jax.ShapeDtypeStruct)
    specs = ([] if order is None else [IN_SMEM]) + [IN_VMEM] * len(inputs)
    run = pl.pallas_call(
        kernel,
        in_specs=specs,
        out_specs=IN_VMEM if single else [IN_VMEM] * len(out_shape),
        out_shape=out_shape,
        scratch_shapes=list(scratch),
        compiler_params=ROOM,
        cost_estimate=cost,
    )
    return run(*(() if order is None else (order,)), *inputs)


def pack_kernel(ids_hbm, route_hbm, tok_hbm, out_ref, ids_ref, route_ref, tok_ref, sems):
    copies = [
        pltpu.make_async_copy(source, target, sems.at[number])
        for number, (source, target) in enumerate(
            ((ids_hbm, ids_ref), (route_hbm, route_ref), (tok_hbm, tok_ref))
        )
    ]
    for copy in copies:
        copy.start()
    for copy in copies:
        copy.wait()
    planes, height, _ = out_ref.shape
    rows, width = tok_ref.shape
    for group in range(width // LANES):
        piece = tok_ref[:, group * LANES : (group + 1) * LANES]
        for plane in range(planes):
            out_ref[plane, pl.ds(group * rows, rows), :] = piece
    lines = planes * 2 * X
    line = iota((lines, rows), 0)
    expert = (line % X) * planes + line // (2 * X)
    scale = jnp.zeros((lines, rows), F32)
    for k in range(TOP):
        scale = jnp.where(ids_ref[k : k + 1, :] == expert, route_ref[k : k + 1, :], scale)
    high = scale.astype(BF).astype(F32)
    value = jnp.where((line // X) % 2 == 0, high, scale - high).astype(BF)
    spread = (iota((rows, LANES), 1) == iota((rows, LANES), 0)).astype(F32).astype(BF)
    info = dot_nn(value, spread).reshape(planes, 2 * X, LANES)
    out_ref[:, pl.ds(height - 2 * X, 2 * X), :] = info.astype(BF)


def pack_tokens(ids, route, tokens, planes):
    rows, width = tokens.shape
    height = width // LANES * rows + 2 * X
    return pl.pallas_call(
        pack_kernel,
        in_specs=[IN_PLACE] * 3,
        out_specs=IN_VMEM,
        out_shape=jax.ShapeDtypeStruct((planes, height, LANES), BF),
        scratch_shapes=[
            pltpu.VMEM(ids.shape, ids.dtype),
            pltpu.VMEM(route.shape, route.dtype),
            pltpu.VMEM(tokens.shape, tokens.dtype),
            pltpu.SemaphoreType.DMA((3,)),
        ],
        compiler_params=ROOM,
        name="pack_tokens",
    )(remote(ids), remote(route), remote(tokens))


def route_tables(got_ref, rows):
    planes, height, _ = got_ref.shape
    span = LANES // rows
    parts = []
    for start in range(0, planes, span):
        total = None
        for plane in range(start, start + span):
            part = got_ref[plane, pl.ds(height - 2 * X, 2 * X), :].astype(F32)
            if plane > start:
                part = pltpu.roll(part, (plane - start) * rows, 1)
            total = part if total is None else total + part
        parts.append(total)
    table = jnp.concatenate(parts, axis=1)
    tokens = planes * rows
    left, right = iota((tokens, tokens), 0), iota((tokens, tokens), 1)
    before = ((left // rows == right // rows) & (left < right)).astype(F32).astype(BF)
    rank = dot_nn((table > 0.0).astype(F32).astype(BF), before)
    return table, rank


def taken_rows(table, rank, j, rows):
    tokens = table.shape[1]
    count = tokens // rows * SLOTS
    row, token = iota((count, tokens), 0), iota((count, tokens), 1)
    return (
        (table[j : j + 1, :] > 0.0)
        & (row // SLOTS == token // rows)
        & (rank[j : j + 1, :] == (row % SLOTS).astype(F32))
    )


def pick_kernel(got_ref, out_ref, tok_ref, pick_ref):
    planes, height, _ = got_ref.shape
    groups = tok_ref.shape[1] // LANES
    rows = (height - 2 * X) // groups
    table, rank = route_tables(got_ref, rows)
    for plane in range(planes):
        for group in range(groups):
            tok_ref[pl.ds(plane * rows, rows), group * LANES : (group + 1) * LANES] = got_ref[
                plane, pl.ds(group * rows, rows), :
            ]
    count = planes * SLOTS
    for j in range(X):
        pick_ref[pl.ds(j * count, count), :] = (
            taken_rows(table, rank, j, rows).astype(F32).astype(BF)
        )
    out_ref[...] = dot_nn(pick_ref[...], tok_ref[...]).astype(BF).reshape(out_ref.shape)


def weigh_kernel(got_ref, high_ref, low_ref):
    planes = got_ref.shape[0]
    rows = high_ref.shape[0] // planes
    table, rank = route_tables(got_ref, rows)
    count = planes * SLOTS
    for j in range(X):
        taken = taken_rows(table, rank, j, rows)
        for ref, line in ((high_ref, j), (low_ref, X + j)):
            value = jnp.where(taken, table[line : line + 1, :], 0.0)
            ref[:, j * count : (j + 1) * count] = value.T.astype(BF)


def join_kernel(got_ref, top_ref, low_ref):
    _, rows, width = got_ref.shape
    half = X // 2
    for x in range(X):
        ref = top_ref if x < half else low_ref
        for core in range(CORES):
            ref[pl.ds((x % half) * rows, rows), core * width : (core + 1) * width] = got_ref[
                x * CORES + core
            ]


def arrange_kernel(order_ref, gate_own, gate_other, up_own, up_other, out_ref):
    core = order_ref[4]
    chips, _, width = out_ref.shape
    unit = gate_own.shape[0]
    own = pl.multiple_of(core * unit, unit)
    other = pl.multiple_of((1 - core) * unit, unit)
    for number in range(chips):
        lanes = pl.ds(pl.multiple_of(order_ref[number] * width, width), width)
        out_ref[number, pl.ds(own, unit), :] = gate_own[:, lanes]
        out_ref[number, pl.ds(other, unit), :] = gate_other[:, lanes]
        out_ref[number, pl.ds(own + CORES * unit, unit), :] = up_own[:, lanes]
        out_ref[number, pl.ds(other + CORES * unit, unit), :] = up_other[:, lanes]


def near_kernel(*refs):
    pieces, (table_hbm, acc_ref, peak_ref, last_ref, x_ref, w_ref, sems) = refs[:6], refs[6:]
    half = pieces[0].shape[0]
    copies = [
        pltpu.make_async_copy(
            table_hbm.at[number], w_ref.at[number] if number < 3 else last_ref, sems.at[number]
        )
        for number in range(4)
    ]
    for copy in copies:
        copy.start()
    peak = None
    total = None
    for number in range(3):
        x_ref[number, pl.ds(0, half), :] = pieces[2 * number][...]
        x_ref[number, pl.ds(half, half), :] = pieces[2 * number + 1][...]
        x = x_ref[number]
        copies[number].wait()
        value = dot_nt(x, w_ref[number])
        total = value if total is None else total + value
        high = jnp.max(jnp.abs(x).astype(F32), axis=0, keepdims=True)
        peak = high if peak is None else jnp.maximum(peak, high)
    acc_ref[...] = total
    peak_ref[...] = peak
    copies[3].wait()


def near_chunks(pieces, table):
    half, width = pieces[0].shape
    wide = table.shape[1]
    return pl.pallas_call(
        near_kernel,
        in_specs=[IN_VMEM] * 6 + [IN_PLACE],
        out_specs=[IN_VMEM] * 3,
        out_shape=[
            jax.ShapeDtypeStruct((2 * half, wide), F32),
            jax.ShapeDtypeStruct((1, width), F32),
            jax.ShapeDtypeStruct((wide, width), BF),
        ],
        scratch_shapes=[
            pltpu.VMEM((3, 2 * half, width), BF),
            pltpu.VMEM((3, wide, width), BF),
            pltpu.SemaphoreType.DMA((4,)),
        ],
        compiler_params=ROOM,
        cost_estimate=pl.CostEstimate(
            flops=12 * half * width * wide, transcendentals=0, bytes_accessed=8 * width * wide
        ),
        name="near_chunks",
    )(*(local(piece) for piece in pieces), remote(table))


def far_kernel(top_ref, low_ref, table_ref, acc_ref, peak_in, hid_ref, peak_ref, x_ref):
    half = top_ref.shape[0]
    units = hid_ref.shape[1]
    x_ref[pl.ds(0, half), :] = top_ref[...]
    x_ref[pl.ds(half, half), :] = low_ref[...]
    x = x_ref[...]
    value = acc_ref[...] + dot_nt(x, table_ref[...])
    gate = value[:, :units]
    hid_ref[...] = (gate / (1.0 + jnp.exp(-gate)) * value[:, units:]).astype(BF)
    peak = jnp.maximum(jnp.max(peak_in[...]), jnp.max(jnp.abs(x).astype(F32)))
    peak_ref[...] = jnp.full(peak_ref.shape, peak, F32)


def cut_kernel(order_ref, down_ref, *out_refs):
    width = out_refs[0].shape[1]
    for number, out_ref in enumerate(out_refs):
        start = pl.multiple_of(order_ref[number] * width, width)
        out_ref[...] = down_ref[:, pl.ds(start, width)]


def stack_kernel(order_ref, *refs):
    for number, piece in enumerate(refs[:-1]):
        refs[-1][order_ref[number]] = piece[...]


def pair_kernel(order_ref, own_ref, other_ref, out_ref):
    chips, unit, _ = own_ref.shape
    core = order_ref[4]
    for chip in range(chips):
        base = chip * CORES * unit
        out_ref[pl.ds(pl.multiple_of(base + core * unit, unit), unit), :] = own_ref[chip]
        out_ref[pl.ds(pl.multiple_of(base + (1 - core) * unit, unit), unit), :] = other_ref[chip]


def down_kernel(hid_ref, down_ref, peak_in, out_ref, peak_ref, h_ref):
    chips, _, units = hid_ref.shape
    for chip in range(chips):
        h_ref[:, chip * units : (chip + 1) * units] = hid_ref[chip]
    hidden = h_ref[...]
    value = dot_nn(hidden, down_ref[...]).astype(BF)
    _, rows, width = out_ref.shape
    for x in range(X):
        for core in range(CORES):
            out_ref[x * CORES + core] = value[
                x * rows : (x + 1) * rows, core * width : (core + 1) * width
            ]
    peak = jnp.max(jnp.abs(hidden).astype(F32))
    peak_ref[...] = jnp.where(iota(peak_ref.shape, 0) == 0, peak_in[...], peak)


def combine_kernel(high_ref, low_ref, row_ref, out_ref):
    rows = row_ref[...].reshape(high_ref.shape[1], row_ref.shape[2])
    value = dot_nn(high_ref[...], rows) + dot_nn(low_ref[...], rows)
    out_ref[...] = value.astype(BF).reshape(out_ref.shape)


def total_kernel(part_ref, out_ref):
    total = part_ref[0].astype(F32)
    for plane in range(1, part_ref.shape[0]):
        total = total + part_ref[plane].astype(F32)
    out_ref[...] = total.astype(BF)


def layer(tokens, expert_ids, route_weight, gate_weight, up_weight, down_weight):
    planes = lax.axis_size("z")
    chips = lax.axis_size("chip")
    core = lax.axis_index("core")
    place = lax.axis_index("chip")
    rows, width = tokens.shape
    unit, _ = gate_weight.shape[1:]
    chunk = CORES * width
    units = CORES * unit
    kept = X * planes * SLOTS // CORES
    shaped = jax.ShapeDtypeStruct

    def shift(array, step):
        return lax.ppermute(array, "chip", [(j, (j + step) % chips) for j in range(chips)])

    def partner(array):
        return lax.ppermute(array, "core", [(j, 1 - j) for j in range(CORES)])

    lane = jnp.arange(8, dtype=jnp.int32)
    turns = jnp.array([0, chips - 1, 1, 2, 0, 0, 0, 0], jnp.int32)
    order = jnp.where(
        lane < 4, (place + turns) % chips, jnp.where(lane == 4, core, lax.axis_index("z"))
    ).astype(jnp.int32)

    packed = pack_tokens(expert_ids.T, route_weight.T, tokens, planes)
    plane_rows = lax.all_to_all(packed, "z", split_axis=0, concat_axis=0, tiled=True)

    gate_other = partner(gate_weight[0])
    up_other = partner(up_weight[0])
    cuts = call(cut_kernel, order, (down_weight[0],), [shaped((unit, chunk), BF)] * chips)
    pieces = [cuts[0], shift(cuts[2], 1), shift(cuts[1], -1), shift(cuts[3], 2)]
    table = call(
        arrange_kernel,
        order,
        tuple(local(a) for a in (gate_weight[0], gate_other, up_weight[0], up_other)),
        shaped((chips, 2 * units, chunk), BF),
    )

    sent = call(
        pick_kernel,
        None,
        (local(plane_rows),),
        shaped((X * CORES, kept // X, width), BF),
        (
            pltpu.VMEM((planes * rows, width), BF),
            pltpu.VMEM((X * planes * SLOTS, planes * rows), BF),
        ),
    )
    received = lax.all_to_all(sent, ("x", "core"), split_axis=0, concat_axis=0, tiled=True)
    stacked = call(
        stack_kernel,
        order,
        tuple(remote(piece) for piece in pieces),
        shaped((chips, unit, chunk), BF),
    )
    stacked_other = partner(stacked)
    high, low = call(
        weigh_kernel,
        None,
        (local(plane_rows),),
        [shaped((planes * rows, X * planes * SLOTS), BF)] * 2,
    )

    top, bottom = call(join_kernel, None, (local(received),), [shaped((kept // 2, chunk), BF)] * 2)
    left_top, right_low = shift(top, 1), shift(bottom, -1)
    left_low, right_top = shift(bottom, 1), shift(top, -1)
    far_top, far_low = shift(left_top, 1), shift(right_low, -1)
    acc, peak, last = near_chunks(
        (top, bottom, left_top, left_low, right_top, right_low), table
    )
    hidden, peak = call(
        far_kernel,
        None,
        tuple(local(a) for a in (far_top, far_low, last, acc, peak)),
        [shaped((kept, units), BF), shaped((8, LANES), F32)],
        (pltpu.VMEM((kept, chunk), BF),),
    )
    down = call(
        pair_kernel,
        order,
        (local(stacked), local(stacked_other)),
        shaped((chips * units, chunk), BF),
    )
    gathered = lax.all_gather(hidden, "chip", axis=0)
    outputs, peak = call(
        down_kernel,
        None,
        tuple(local(a) for a in (gathered, down, peak)),
        [shaped((X * CORES, kept // X, width), BF), shaped((8, LANES), F32)],
        (pltpu.VMEM((kept, chips * units), BF),),
    )
    returned = lax.all_to_all(outputs, ("x", "core"), split_axis=0, concat_axis=0, tiled=True)
    column = jnp.maximum(peak, partner(peak))[:2, :1]
    sums = call(
        combine_kernel,
        None,
        tuple(local(a) for a in (high, low, returned)),
        shaped((planes, rows, width), BF),
    )
    parts = lax.all_to_all(sums, "z", split_axis=0, concat_axis=0, tiled=True)
    moe_out = call(total_kernel, None, (local(parts),), shaped((rows, width), BF))
    return moe_out, column


def solution(mesh):
    devices = np.asarray(mesh.devices)
    ep, tp = devices.shape
    fine = Mesh(
        devices.reshape(X, ep // X, tp // CORES, CORES), ("x", "z", "chip", "core")
    )
    ep, tp = ("x", "z"), ("chip", "core")
    return jax.shard_map(
        layer,
        mesh=fine,
        in_specs=(
            P(ep, tp),
            P(ep, None),
            P(ep, None),
            P(ep, tp, None),
            P(ep, tp, None),
            P(ep, tp, None),
        ),
        out_specs=(P(ep, tp), P(None, ep)),
        check_vma=False,
    )
```

profile of v0, /device:TPU:32, one launch (start us, length us, event | category | flops | bytes accessed | tf_op | source)
XLA Modules:
  0.0 157.0 jit_solution(5322975612650149858)
XLA Ops:
  0.6 0.0 copy-start.1
  0.6 1.8 %pack_tokens.1 = bf16[16,72,128]{2,1,0:T(8,128)(2,1)} custom-call(s32[8,16]{1,0:T(8,128)} %bitcast.12, f32[8,16]{1,0:T(8,128)} %bitcast.13, bf16[16,512]{1,0:T(8,128)(2,1)} %tok_hbm.1), custom_call_target="tpu_custom_call" | custom-call | tf_op jit(solution)/shard_map/pack_tokens/pallas_call | solution.py:93
  2.4 15.2 %all-to-all-start = ((bf16[16,72,128]{2,1,0:T(8,128)(2,1)}), bf16[16,72,128]{2,1,0:T(8,128)(2,1)S(1)}, u32[]{:S(2)}, u32[]{:S(2)}) async-start(bf16[16,72,128]{2,1,0:T(8,128)(2,1)} %pack_tokens.1), calls=%async_computation | async-start | bytes 589824 | tf_op jit(solution)/shard_map/all_to_all | solution.py:335
  17.7 0.7 compare_select_fusion.3.order_ref
  18.3 0.0 copy-start.3
  18.3 1.4 copy-done.3
  19.7 0.6 shard_map.91
  20.4 0.0 copy-start.4
  20.4 0.7 copy-done.4
  21.1 3.5 %collective-permute-start.8 = (bf16[192,1024]{1,0:T(8,128)(2,1)S(1)}, bf16[192,1024]{1,0:T(8,128)(2,1)S(1)}, u32[]{:S(2)}, u32[]{:S(2)}) collective-permute-start(bf16[192,1024]{1,0:T(8,128)(2,1)S(1)} %get-tuple-element.26), channel_id=1, source_target_pairs={{0,2},{2,4},{4,6},{6,0},{1,3},{3,5},{5,7},{7,1},{8,10},{10,12},{12... | collective-permute-start | bytes 1179656 | tf_op jit(solution)/shard_map/ppermute | solution.py:323
  24.6 3.6 %collective-permute-start.9 = (bf16[192,1024]{1,0:T(8,128)(2,1)S(1)}, bf16[192,1024]{1,0:T(8,128)(2,1)S(1)}, u32[]{:S(2)}, u32[]{:S(2)}) collective-permute-start(bf16[192,1024]{1,0:T(8,128)(2,1)S(1)} %get-tuple-element.27), channel_id=1, source_target_pairs={{0,6},{2,0},{4,2},{6,4},{1,7},{3,1},{5,3},{7,5},{8,14},{10,8},{12,... | collective-permute-start | bytes 1179656 | tf_op jit(solution)/shard_map/ppermute | solution.py:323
  28.2 3.9 %collective-permute-start.10 = (bf16[192,1024]{1,0:T(8,128)(2,1)S(1)}, bf16[192,1024]{1,0:T(8,128)(2,1)S(1)}, u32[]{:S(2)}, u32[]{:S(2)}) collective-permute-start(bf16[192,1024]{1,0:T(8,128)(2,1)S(1)} %get-tuple-element.28), channel_id=1, source_target_pairs={{0,4},{2,6},{4,0},{6,2},{1,5},{3,7},{5,1},{7,3},{8,12},{10,14},{12... | collective-permute-start | bytes 1179656 | tf_op jit(solution)/shard_map/ppermute | solution.py:323
  32.1 0.0 copy-done.1
  32.1 1.9 %collective-permute-start.6 = (bf16[192,4096]{1,0:T(8,128)(2,1)S(1)}, bf16[192,4096]{1,0:T(8,128)(2,1)}, u32[]{:S(2)}, u32[]{:S(2)}) collective-permute-start(bf16[192,4096]{1,0:T(8,128)(2,1)S(1)} %bitcast.7), channel_id=1, source_target_pairs={{0,1},{1,0},{2,3},{3,2},{4,5},{5,4},{6,7},{7,6},{8,9},{9,8},{10,11... | collective-permute-start | bytes 4718600 | tf_op jit(solution)/shard_map/ppermute | solution.py:326
  34.0 2.4 %collective-permute-start.7 = (bf16[192,4096]{1,0:T(8,128)(2,1)}, bf16[192,4096]{1,0:T(8,128)(2,1)}, u32[]{:S(2)}, u32[]{:S(2)}) collective-permute-start(bf16[192,4096]{1,0:T(8,128)(2,1)} %bitcast.9), channel_id=1, source_target_pairs={{0,1},{1,0},{2,3},{3,2},{4,5},{5,4},{6,7},{7,6},{8,9},{9,8},{10,11... | collective-permute-start | bytes 4718600 | tf_op jit(solution)/shard_map/ppermute | solution.py:326
  36.5 0.0 collective-permute-done.8.refs_1_
  36.5 0.0 copy-start.5
  36.5 2.0 %collective-permute-done.9.refs_2_ = bf16[192,1024]{1,0:T(8,128)(2,1)S(1)} collective-permute-done((bf16[192,1024]{1,0:T(8,128)(2,1)S(1)}, bf16[192,1024]{1,0:T(8,128)(2,1)S(1)}, u32[]{:S(2)}, u32[]{:S(2)}) %collective-permute-start.9) | collective-permute-done | bytes 393248 | tf_op jit(solution)/shard_map/ppermute | solution.py:323
  38.5 0.0 copy-start.6
  38.5 5.7 %collective-permute-done.10.refs_3_ = bf16[192,1024]{1,0:T(8,128)(2,1)S(1)} collective-permute-done((bf16[192,1024]{1,0:T(8,128)(2,1)S(1)}, bf16[192,1024]{1,0:T(8,128)(2,1)S(1)}, u32[]{:S(2)}, u32[]{:S(2)}) %collective-permute-start.10) | collective-permute-done | bytes 393248 | tf_op jit(solution)/shard_map/ppermute | solution.py:323
  44.2 0.0 copy-start.7
  44.2 0.0 copy-done.5
  44.2 0.0 copy-done.6
  44.2 0.8 copy-done.7
  45.0 1.5 shard_map.92.own_ref
  46.4 1.9 %collective-permute-start.11 = (bf16[4,192,1024]{2,1,0:T(8,128)(2,1)S(1)}, bf16[4,192,1024]{2,1,0:T(8,128)(2,1)}, u32[]{:S(2)}, u32[]{:S(2)}) collective-permute-start(bf16[4,192,1024]{2,1,0:T(8,128)(2,1)S(1)} %shard_map.92.own_ref), channel_id=1, source_target_pairs={{0,1},{1,0},{2,3},{3,2},{4,5},{5,4},{6,7},{7,6},{8,9},{9,8},{10,11... | collective-permute-start | bytes 4718600 | tf_op jit(solution)/shard_map/ppermute | solution.py:326
  48.4 0.0 all-to-all-done.got_ref
  48.4 0.0 copy-start.2
  48.4 0.5 shard_map.87
  48.9 14.6 %all_to_all.20.got_ref = bf16[8,64,512]{2,1,0:T(8,128)(2,1)S(1)} all-to-all(bf16[8,64,512]{2,1,0:T(8,128)(2,1)S(1)} %shard_map.87), channel_id=1, replica_groups=mesh['x'=4,'z'=16,'chip'=4,'core'=2] {'x','core'}, dimensions={0} | all-to-all | bytes 1048576 | tf_op jit(solution)/shard_map/all_to_all | solution.py:358
  63.5 5.0 %collective-permute-start = (bf16[128,1024]{1,0:T(8,128)(2,1)S(1)}, bf16[128,1024]{1,0:T(8,128)(2,1)S(1)}, u32[]{:S(2)}, u32[]{:S(2)}) collective-permute-start(bf16[128,1024]{1,0:T(8,128)(2,1)S(1)} %get-tuple-element.19.refs_0_), channel_id=1, source_target_pairs={{0,2},{2,4},{4,6},{6,0},{1,3},{3,5},{5,7},{7,1},{8,10},{10,12},{12... | collective-permute-start | bytes 786440 | tf_op jit(solution)/shard_map/ppermute | solution.py:323
  68.5 2.7 %collective-permute-start.2 = (bf16[128,1024]{1,0:T(8,128)(2,1)S(1)}, bf16[128,1024]{1,0:T(8,128)(2,1)S(1)}, u32[]{:S(2)}, u32[]{:S(2)}) collective-permute-start(bf16[128,1024]{1,0:T(8,128)(2,1)S(1)} %get-tuple-element.20.refs_1_), channel_id=1, source_target_pairs={{0,6},{2,0},{4,2},{6,4},{1,7},{3,1},{5,3},{7,5},{8,14},{10,8},{12,... | collective-permute-start | bytes 786440 | tf_op jit(solution)/shard_map/ppermute | solution.py:323
  71.1 0.0 collective-permute-done.6.gate_other
  71.2 3.2 %collective-permute-start.4 = (bf16[128,1024]{1,0:T(8,128)(2,1)S(1)}, bf16[128,1024]{1,0:T(8,128)(2,1)S(1)}, u32[]{:S(2)}, u32[]{:S(2)}) collective-permute-start(bf16[128,1024]{1,0:T(8,128)(2,1)S(1)} %get-tuple-element.20.refs_1_), channel_id=1, source_target_pairs={{0,2},{2,4},{4,6},{6,0},{1,3},{3,5},{5,7},{7,1},{8,10},{10,12},{12... | collective-permute-start | bytes 786440 | tf_op jit(solution)/shard_map/ppermute | solution.py:323
  74.3 0.0 collective-permute-done.7.up_other
  74.3 3.9 %collective-permute-start.5 = (bf16[128,1024]{1,0:T(8,128)(2,1)S(1)}, bf16[128,1024]{1,0:T(8,128)(2,1)S(1)}, u32[]{:S(2)}, u32[]{:S(2)}) collective-permute-start(bf16[128,1024]{1,0:T(8,128)(2,1)S(1)} %get-tuple-element.19.refs_0_), channel_id=1, source_target_pairs={{0,6},{2,0},{4,2},{6,4},{1,7},{3,1},{5,3},{7,5},{8,14},{10,8},{12,... | collective-permute-start | bytes 786440 | tf_op jit(solution)/shard_map/ppermute | solution.py:323
  78.2 0.0 collective-permute-done.refs_2_
  78.2 2.0 %collective-permute-start.1 = (bf16[128,1024]{1,0:T(8,128)(2,1)S(1)}, bf16[128,1024]{1,0:T(8,128)(2,1)S(1)}, u32[]{:S(2)}, u32[]{:S(2)}) collective-permute-start(bf16[128,1024]{1,0:T(8,128)(2,1)S(1)} %collective-permute-done.refs_2_), channel_id=1, source_target_pairs={{0,2},{2,4},{4,6},{6,0},{1,3},{3,5},{5,7},{7,1},{8,10},{10,12},{12... | collective-permute-start | bytes 786440 | tf_op jit(solution)/shard_map/ppermute | solution.py:323
  80.2 0.0 collective-permute-done.2.refs_5_
  80.2 5.1 %collective-permute-start.3 = (bf16[128,1024]{1,0:T(8,128)(2,1)S(1)}, bf16[128,1024]{1,0:T(8,128)(2,1)S(1)}, u32[]{:S(2)}, u32[]{:S(2)}) collective-permute-start(bf16[128,1024]{1,0:T(8,128)(2,1)S(1)} %collective-permute-done.2.refs_5_), channel_id=1, source_target_pairs={{0,6},{2,0},{4,2},{6,4},{1,7},{3,1},{5,3},{7,5},{8,14},{10,8},{12,... | collective-permute-start | bytes 786440 | tf_op jit(solution)/shard_map/ppermute | solution.py:323
  85.3 0.0 copy-done.2
  85.3 2.3 %shard_map.89.refs_6_ = bf16[4,768,1024]{2,1,0:T(8,128)(2,1)S(1)} custom-call(s32[8]{0:T(128)S(1)} %compare_select_fusion.3.order_ref, bf16[192,4096]{1,0:T(8,128)(2,1)S(1)} %bitcast.8, bf16[192,4096]{1,0:T(8,128)(2,1)} %collective-permute-done.6.gate_other, bf16[192,4096]{1,0:T(8,128)(2,1)S(1)} %bitcast.10, bf16[192,4096]{1,0:T(8,128)(2,1)} %collective-permute-done.7.up_other), custom_call_target="tpu_custom_call" | custom-call | tf_op jit(solution)/shard_map/pallas_call | solution.py:57
  87.6 0.0 copy-start
  87.7 2.6 %copy-done = bf16[4,768,1024]{2,1,0:T(8,128)(2,1)} copy-done((bf16[4,768,1024]{2,1,0:T(8,128)(2,1)}, bf16[4,768,1024]{2,1,0:T(8,128)(2,1)S(1)}, u32[]{:S(2)}) %copy-start) | copy-done | bytes 6291480
  90.3 0.0 collective-permute-done.4.refs_3_
  90.3 0.0 collective-permute-done.5.refs_4_
  90.3 3.9 %near_chunks.1 = (f32[256,768]{1,0:T(8,128)S(1)}, f32[1,1024]{1,0:T(1,128)S(1)}, bf16[768,1024]{1,0:T(8,128)(2,1)S(1)}) custom-call(bf16[128,1024]{1,0:T(8,128)(2,1)S(1)} %get-tuple-element.19.refs_0_, bf16[128,1024]{1,0:T(8,128)(2,1)S(1)} %get-tuple-element.20.refs_1_, bf16[128,1024]{1,0:T(8,128)(2,1)S(1)} %collective-permute-done.refs_2_, ...), custom_call_target="tpu_custom_call" | custom-call | flops 1207959552 | bytes 6291456 | tf_op jit(solution)/shard_map/near_chunks/pallas_call | solution.py:225
  94.2 0.0 collective-permute-done.11.other_ref
  94.2 1.6 %shard_map.93.down_ref = bf16[1536,1024]{1,0:T(8,128)(2,1)S(1)} custom-call(s32[8]{0:T(128)S(1)} %compare_select_fusion.3.order_ref, bf16[4,192,1024]{2,1,0:T(8,128)(2,1)S(1)} %shard_map.92.own_ref, bf16[4,192,1024]{2,1,0:T(8,128)(2,1)} %collective-permute-done.11.other_ref), custom_call_target="tpu_custom_call" | custom-call | tf_op jit(solution)/shard_map/pallas_call | solution.py:57
  95.8 0.0 collective-permute-done.1.top_ref
  95.8 0.0 collective-permute-done.3.low_ref
  95.8 0.7 shard_map.90
  96.5 13.3 %all-gather = bf16[1024,384]{1,0:T(8,128)(2,1)S(1)} all-gather(bf16[256,384]{1,0:T(8,128)(2,1)S(1)} %get-tuple-element.24), channel_id=2, replica_groups=mesh['x'=4,'z'=16,'chip'=4,'core'=2] {'chip'}, dimensions={0}, use_global_device_ids=true | all-gather | bytes 983040 | tf_op jit(solution)/shard_map/all_gather | solution.py:393
  109.8 1.8 %shard_map.94 = (bf16[8,64,512]{2,1,0:T(8,128)(2,1)}, f32[8,128]{1,0:T(8,128)S(1)}) custom-call(bf16[4,256,384]{2,1,0:T(8,128)(2,1)S(1)} %bitcast.6, bf16[1536,1024]{1,0:T(8,128)(2,1)S(1)} %shard_map.93.down_ref, f32[8,128]{1,0:T(8,128)S(1)} %get-tuple-element.29.peak_in), custom_call_target="tpu_custom_call" | custom-call | tf_op jit(solution)/shard_map/pallas_call | solution.py:57
  111.7 3.5 %all-to-all-start.2 = ((bf16[8,64,512]{2,1,0:T(8,128)(2,1)}), bf16[8,64,512]{2,1,0:T(8,128)(2,1)S(1)}, u32[]{:S(2)}, u32[]{:S(2)}) async-start(bf16[8,64,512]{2,1,0:T(8,128)(2,1)} %get-tuple-element.30), calls=%async_computation.2 | async-start | bytes 1048576 | tf_op jit(solution)/shard_map/all_to_all | solution.py:401
  115.2 0.5 shard_map.86
  115.6 9.8 %all-to-all-done.2.row_ref = bf16[8,64,512]{2,1,0:T(8,128)(2,1)S(1)} async-done(((bf16[8,64,512]{2,1,0:T(8,128)(2,1)}), bf16[8,64,512]{2,1,0:T(8,128)(2,1)S(1)}, u32[]{:S(2)}, u32[]{:S(2)}) %all-to-all-start.2) | async-done | bytes 524320 | tf_op jit(solution)/shard_map/all_to_all | solution.py:401
  125.4 1.1 shard_map.95
  126.5 12.0 %all-to-all-start.3 = ((bf16[16,16,512]{2,1,0:T(8,128)(2,1)}), bf16[16,16,512]{2,1,0:T(8,128)(2,1)S(1)}, u32[]{:S(2)}, u32[]{:S(2)}) async-start(bf16[16,16,512]{2,1,0:T(8,128)(2,1)} %shard_map.95), calls=%async_computation.3 | async-start | bytes 524288 | tf_op jit(solution)/shard_map/all_to_all | solution.py:409
  138.6 1.9 %collective-permute-start.12 = (f32[8,128]{1,0:T(8,128)S(1)}, f32[8,128]{1,0:T(8,128)S(1)}, u32[]{:S(2)}, u32[]{:S(2)}) collective-permute-start(f32[8,128]{1,0:T(8,128)S(1)} %get-tuple-element.31), channel_id=1, source_target_pairs={{0,1},{1,0},{2,3},{3,2},{4,5},{5,4},{6,7},{7,6},{8,9},{9,8},{10,11... | collective-permute-start | bytes 12296 | tf_op jit(solution)/shard_map/ppermute | solution.py:326
  140.5 1.1 collective-permute-done.12
  141.6 0.6 copy.9
  142.2 14.2 %all-to-all-done.3.part_ref = bf16[16,16,512]{2,1,0:T(8,128)(2,1)S(1)} async-done(((bf16[16,16,512]{2,1,0:T(8,128)(2,1)}), bf16[16,16,512]{2,1,0:T(8,128)(2,1)S(1)}, u32[]{:S(2)}, u32[]{:S(2)}) %all-to-all-start.3) | async-done | bytes 262176 | tf_op jit(solution)/shard_map/all_to_all | solution.py:409
  156.4 0.6 shard_map.96
  (3 shorter events, 0.0 us)
Async XLA Ops:
  0.6 31.5 %copy-start.1 = (bf16[1,192,4096]{2,1,0:T(8,128)(2,1)S(1)}, bf16[1,192,4096]{2,1,0:T(8,128)(2,1)}, u32[]{:S(2)}) copy-start(bf16[1,192,4096]{2,1,0:T(8,128)(2,1)} %param.10) | copy-start | bytes 4718596
  2.4 45.9 %all-to-all-start = ((bf16[16,72,128]{2,1,0:T(8,128)(2,1)}), bf16[16,72,128]{2,1,0:T(8,128)(2,1)S(1)}, u32[]{:S(2)}, u32[]{:S(2)}) async-start(bf16[16,72,128]{2,1,0:T(8,128)(2,1)} %pack_tokens.1), calls=%async_computation | async-start | bytes 589824 | tf_op jit(solution)/shard_map/all_to_all | solution.py:335
  18.3 1.4 copy-start.3
  20.4 0.7 copy-start.4
  21.1 15.3 %collective-permute-start.8 = (bf16[192,1024]{1,0:T(8,128)(2,1)S(1)}, bf16[192,1024]{1,0:T(8,128)(2,1)S(1)}, u32[]{:S(2)}, u32[]{:S(2)}) collective-permute-start(bf16[192,1024]{1,0:T(8,128)(2,1)S(1)} %get-tuple-element.26), channel_id=1, source_target_pairs={{0,2},{2,4},{4,6},{6,0},{1,3},{3,5},{5,7},{7,1},{8,10},{10,12},{12... | collective-permute-start | bytes 1179656 | tf_op jit(solution)/shard_map/ppermute | solution.py:323
  24.6 13.9 %collective-permute-start.9 = (bf16[192,1024]{1,0:T(8,128)(2,1)S(1)}, bf16[192,1024]{1,0:T(8,128)(2,1)S(1)}, u32[]{:S(2)}, u32[]{:S(2)}) collective-permute-start(bf16[192,1024]{1,0:T(8,128)(2,1)S(1)} %get-tuple-element.27), channel_id=1, source_target_pairs={{0,6},{2,0},{4,2},{6,4},{1,7},{3,1},{5,3},{7,5},{8,14},{10,8},{12,... | collective-permute-start | bytes 1179656 | tf_op jit(solution)/shard_map/ppermute | solution.py:323
  28.2 16.0 %collective-permute-start.10 = (bf16[192,1024]{1,0:T(8,128)(2,1)S(1)}, bf16[192,1024]{1,0:T(8,128)(2,1)S(1)}, u32[]{:S(2)}, u32[]{:S(2)}) collective-permute-start(bf16[192,1024]{1,0:T(8,128)(2,1)S(1)} %get-tuple-element.28), channel_id=1, source_target_pairs={{0,4},{2,6},{4,0},{6,2},{1,5},{3,7},{5,1},{7,3},{8,12},{10,14},{12... | collective-permute-start | bytes 1179656 | tf_op jit(solution)/shard_map/ppermute | solution.py:323
  32.1 39.0 %collective-permute-start.6 = (bf16[192,4096]{1,0:T(8,128)(2,1)S(1)}, bf16[192,4096]{1,0:T(8,128)(2,1)}, u32[]{:S(2)}, u32[]{:S(2)}) collective-permute-start(bf16[192,4096]{1,0:T(8,128)(2,1)S(1)} %bitcast.7), channel_id=1, source_target_pairs={{0,1},{1,0},{2,3},{3,2},{4,5},{5,4},{6,7},{7,6},{8,9},{9,8},{10,11... | collective-permute-start | bytes 4718600 | tf_op jit(solution)/shard_map/ppermute | solution.py:326
  34.0 40.3 %collective-permute-start.7 = (bf16[192,4096]{1,0:T(8,128)(2,1)}, bf16[192,4096]{1,0:T(8,128)(2,1)}, u32[]{:S(2)}, u32[]{:S(2)}) collective-permute-start(bf16[192,4096]{1,0:T(8,128)(2,1)} %bitcast.9), channel_id=1, source_target_pairs={{0,1},{1,0},{2,3},{3,2},{4,5},{5,4},{6,7},{7,6},{8,9},{9,8},{10,11... | collective-permute-start | bytes 4718600 | tf_op jit(solution)/shard_map/ppermute | solution.py:326
  36.5 7.7 %copy-start.5 = (bf16[192,1024]{1,0:T(8,128)(2,1)}, bf16[192,1024]{1,0:T(8,128)(2,1)S(1)}, u32[]{:S(2)}) copy-start(bf16[192,1024]{1,0:T(8,128)(2,1)S(1)} %collective-permute-done.8.refs_1_) | copy-start | bytes 1179652
  38.5 5.7 %copy-start.6 = (bf16[192,1024]{1,0:T(8,128)(2,1)}, bf16[192,1024]{1,0:T(8,128)(2,1)S(1)}, u32[]{:S(2)}) copy-start(bf16[192,1024]{1,0:T(8,128)(2,1)S(1)} %collective-permute-done.9.refs_2_) | copy-start | bytes 1179652
  44.2 0.8 copy-start.7
  46.4 47.7 %collective-permute-start.11 = (bf16[4,192,1024]{2,1,0:T(8,128)(2,1)S(1)}, bf16[4,192,1024]{2,1,0:T(8,128)(2,1)}, u32[]{:S(2)}, u32[]{:S(2)}) collective-permute-start(bf16[4,192,1024]{2,1,0:T(8,128)(2,1)S(1)} %shard_map.92.own_ref), channel_id=1, source_target_pairs={{0,1},{1,0},{2,3},{3,2},{4,5},{5,4},{6,7},{7,6},{8,9},{9,8},{10,11... | collective-permute-start | bytes 4718600 | tf_op jit(solution)/shard_map/ppermute | solution.py:326
  48.4 36.9 %copy-start.2 = (bf16[1,192,4096]{2,1,0:T(8,128)(2,1)S(1)}, bf16[1,192,4096]{2,1,0:T(8,128)(2,1)}, u32[]{:S(2)}) copy-start(bf16[1,192,4096]{2,1,0:T(8,128)(2,1)} %param.11) | copy-start | bytes 4718596
  63.5 14.8 %collective-permute-start = (bf16[128,1024]{1,0:T(8,128)(2,1)S(1)}, bf16[128,1024]{1,0:T(8,128)(2,1)S(1)}, u32[]{:S(2)}, u32[]{:S(2)}) collective-permute-start(bf16[128,1024]{1,0:T(8,128)(2,1)S(1)} %get-tuple-element.19.refs_0_), channel_id=1, source_target_pairs={{0,2},{2,4},{4,6},{6,0},{1,3},{3,5},{5,7},{7,1},{8,10},{10,12},{12... | collective-permute-start | bytes 786440 | tf_op jit(solution)/shard_map/ppermute | solution.py:323
  68.5 11.8 %collective-permute-start.2 = (bf16[128,1024]{1,0:T(8,128)(2,1)S(1)}, bf16[128,1024]{1,0:T(8,128)(2,1)S(1)}, u32[]{:S(2)}, u32[]{:S(2)}) collective-permute-start(bf16[128,1024]{1,0:T(8,128)(2,1)S(1)} %get-tuple-element.20.refs_1_), channel_id=1, source_target_pairs={{0,6},{2,0},{4,2},{6,4},{1,7},{3,1},{5,3},{7,5},{8,14},{10,8},{12,... | collective-permute-start | bytes 786440 | tf_op jit(solution)/shard_map/ppermute | solution.py:323
  71.2 19.1 %collective-permute-start.4 = (bf16[128,1024]{1,0:T(8,128)(2,1)S(1)}, bf16[128,1024]{1,0:T(8,128)(2,1)S(1)}, u32[]{:S(2)}, u32[]{:S(2)}) collective-permute-start(bf16[128,1024]{1,0:T(8,128)(2,1)S(1)} %get-tuple-element.20.refs_1_), channel_id=1, source_target_pairs={{0,2},{2,4},{4,6},{6,0},{1,3},{3,5},{5,7},{7,1},{8,10},{10,12},{12... | collective-permute-start | bytes 786440 | tf_op jit(solution)/shard_map/ppermute | solution.py:323
  74.3 15.9 %collective-permute-start.5 = (bf16[128,1024]{1,0:T(8,128)(2,1)S(1)}, bf16[128,1024]{1,0:T(8,128)(2,1)S(1)}, u32[]{:S(2)}, u32[]{:S(2)}) collective-permute-start(bf16[128,1024]{1,0:T(8,128)(2,1)S(1)} %get-tuple-element.19.refs_0_), channel_id=1, source_target_pairs={{0,6},{2,0},{4,2},{6,4},{1,7},{3,1},{5,3},{7,5},{8,14},{10,8},{12,... | collective-permute-start | bytes 786440 | tf_op jit(solution)/shard_map/ppermute | solution.py:323
  78.2 17.6 %collective-permute-start.1 = (bf16[128,1024]{1,0:T(8,128)(2,1)S(1)}, bf16[128,1024]{1,0:T(8,128)(2,1)S(1)}, u32[]{:S(2)}, u32[]{:S(2)}) collective-permute-start(bf16[128,1024]{1,0:T(8,128)(2,1)S(1)} %collective-permute-done.refs_2_), channel_id=1, source_target_pairs={{0,2},{2,4},{4,6},{6,0},{1,3},{3,5},{5,7},{7,1},{8,10},{10,12},{12... | collective-permute-start | bytes 786440 | tf_op jit(solution)/shard_map/ppermute | solution.py:323
  80.2 15.6 %collective-permute-start.3 = (bf16[128,1024]{1,0:T(8,128)(2,1)S(1)}, bf16[128,1024]{1,0:T(8,128)(2,1)S(1)}, u32[]{:S(2)}, u32[]{:S(2)}) collective-permute-start(bf16[128,1024]{1,0:T(8,128)(2,1)S(1)} %collective-permute-done.2.refs_5_), channel_id=1, source_target_pairs={{0,6},{2,0},{4,2},{6,4},{1,7},{3,1},{5,3},{7,5},{8,14},{10,8},{12,... | collective-permute-start | bytes 786440 | tf_op jit(solution)/shard_map/ppermute | solution.py:323
  87.6 2.6 %copy-start = (bf16[4,768,1024]{2,1,0:T(8,128)(2,1)}, bf16[4,768,1024]{2,1,0:T(8,128)(2,1)S(1)}, u32[]{:S(2)}) copy-start(bf16[4,768,1024]{2,1,0:T(8,128)(2,1)S(1)} %shard_map.89.refs_6_) | copy-start | bytes 18874372
  111.7 13.7 %all-to-all-start.2 = ((bf16[8,64,512]{2,1,0:T(8,128)(2,1)}), bf16[8,64,512]{2,1,0:T(8,128)(2,1)S(1)}, u32[]{:S(2)}, u32[]{:S(2)}) async-start(bf16[8,64,512]{2,1,0:T(8,128)(2,1)} %get-tuple-element.30), calls=%async_computation.2 | async-start | bytes 1048576 | tf_op jit(solution)/shard_map/all_to_all | solution.py:401
  126.5 29.8 %all-to-all-start.3 = ((bf16[16,16,512]{2,1,0:T(8,128)(2,1)}), bf16[16,16,512]{2,1,0:T(8,128)(2,1)S(1)}, u32[]{:S(2)}, u32[]{:S(2)}) async-start(bf16[16,16,512]{2,1,0:T(8,128)(2,1)} %shard_map.95), calls=%async_computation.3 | async-start | bytes 524288 | tf_op jit(solution)/shard_map/all_to_all | solution.py:409
  138.6 3.0 %collective-permute-start.12 = (f32[8,128]{1,0:T(8,128)S(1)}, f32[8,128]{1,0:T(8,128)S(1)}, u32[]{:S(2)}, u32[]{:S(2)}) collective-permute-start(f32[8,128]{1,0:T(8,128)S(1)} %get-tuple-element.31), channel_id=1, source_target_pairs={{0,1},{1,0},{2,3},{3,2},{4,5},{5,4},{6,7},{7,6},{8,9},{9,8},{10,11... | collective-permute-start | bytes 12296 | tf_op jit(solution)/shard_map/ppermute | solution.py:326
where the time goes:
time: 158 us; the launch traced here: 157 us
  starting transfers between devices  71.6 us (45%)
  waiting for transfers between devices  32.8 us (21%)
  blocking collectives  27.9 us (18%)
  Pallas kernels  17 us (11%)
  local copies, waits for them, and re-layouts  6.15 us (4%)
    ppermute x9, starting transfers between devices, shift(): lax.ppermute(array, 'chip', [(j, (j + step) % chips) for j in range(chips)])  32.7 us
    all_to_all x1, starting transfers between devices, layer(): lax.all_to_all(packed, 'z', split_axis=0, concat_axis=0, tiled=True)  15.2 us
    all_to_all x1, blocking collectives, layer(): lax.all_to_all(sent, ('x', 'core'), split_axis=0, concat_axis=0, tiled=True)  14.6 us
    all_to_all x1, waiting for transfers between devices, layer(): parts = lax.all_to_all(sums, 'z', split_axis=0, concat_axis=0, tiled=True)  14.2 us
    all_gather x1, blocking collectives, layer(): gathered = lax.all_gather(hidden, 'chip', axis=0)  13.3 us
    all_to_all x1, starting transfers between devices, layer(): parts = lax.all_to_all(sums, 'z', split_axis=0, concat_axis=0, tiled=True)  12 us
    pallas_call x11, Pallas kernels, call(): return run(*(() if order is None else (order,)), *inputs)  11.3 us
    all_to_all x1, waiting for transfers between devices, layer(): lax.all_to_all(outputs, ('x', 'core'), split_axis=0, concat_axis=0, tiled...  9.78 us
  transfers between devices with their start and end apart: 16, of which 5 were waited for; matrix products, arithmetic and copies ran while one was open for 1% of the time, Pallas kernels for 7%

commit v1 on v0

--- a/solution.py
+++ b/solution.py
@@ -40,6 +40,25 @@
 
 def iota(shape, axis):
     return lax.broadcasted_iota(jnp.int32, shape, axis)
+
+
+def run_copies(copies):
+    for copy in copies:
+        copy.start()
+    for copy in copies:
+        copy.wait()
+
+
+def move(kernel, order, inputs, out_shape, count):
+    single = isinstance(out_shape, jax.ShapeDtypeStruct)
+    return pl.pallas_call(
+        kernel,
+        in_specs=[IN_SMEM] + [IN_PLACE] * len(inputs),
+        out_specs=IN_PLACE if single else [IN_PLACE] * len(out_shape),
+        out_shape=out_shape,
+        scratch_shapes=[pltpu.SemaphoreType.DMA((count,))],
+        compiler_params=ROOM,
+    )(order, *(remote(array) for array in inputs))
 
 
 def call(kernel, order, inputs, out_shape, scratch=(), cost=None):
@@ -64,10 +83,7 @@
             ((ids_hbm, ids_ref), (route_hbm, route_ref), (tok_hbm, tok_ref))
         )
     ]
-    for copy in copies:
-        copy.start()
-    for copy in copies:
-        copy.wait()
+    run_copies(copies)
     planes, height, _ = out_ref.shape
     rows, width = tok_ref.shape
     for group in range(width // LANES):
@@ -178,30 +194,44 @@
             ]
 
 
-def arrange_kernel(order_ref, gate_own, gate_other, up_own, up_other, out_ref):
+def near_kernel(order_ref, *refs):
+    pieces, (gate_own, gate_other, up_own, up_other, down_own, down_other) = refs[:6], refs[6:12]
+    acc_ref, peak_ref, last_ref, down_ref, x_ref, w_ref, sems = refs[12:]
     core = order_ref[4]
-    chips, _, width = out_ref.shape
+    half, width = pieces[0].shape
     unit = gate_own.shape[0]
+    chips = down_own.shape[0]
     own = pl.multiple_of(core * unit, unit)
     other = pl.multiple_of((1 - core) * unit, unit)
+    fetched = []
     for number in range(chips):
         lanes = pl.ds(pl.multiple_of(order_ref[number] * width, width), width)
-        out_ref[number, pl.ds(own, unit), :] = gate_own[:, lanes]
-        out_ref[number, pl.ds(other, unit), :] = gate_other[:, lanes]
-        out_ref[number, pl.ds(own + CORES * unit, unit), :] = up_own[:, lanes]
-        out_ref[number, pl.ds(other + CORES * unit, unit), :] = up_other[:, lanes]
-
-
-def near_kernel(*refs):
-    pieces, (table_hbm, acc_ref, peak_ref, last_ref, x_ref, w_ref, sems) = refs[:6], refs[6:]
-    half = pieces[0].shape[0]
-    copies = [
-        pltpu.make_async_copy(
-            table_hbm.at[number], w_ref.at[number] if number < 3 else last_ref, sems.at[number]
-        )
-        for number in range(4)
-    ]
-    for copy in copies:
+        target = w_ref.at[number] if number < 3 else last_ref
+        group = []
+        for place, (source, first) in enumerate(
+            (
+                (gate_own, own),
+                (gate_other, other),
+                (up_own, own + CORES * unit),
+                (up_other, other + CORES * unit),
+            )
+        ):
+            group.append(
+                pltpu.make_async_copy(
+                    source.at[:, lanes], target.at[pl.ds(first, unit), :], sems.at[number, place]
+                )
+            )
+        fetched.append(group)
+    handed = []
+    for chip in range(chips):
+        for place, (source, first) in enumerate(((down_own, own), (down_other, other))):
+            rows = pl.ds(pl.multiple_of(chip * CORES * unit + first, unit), unit)
+            handed.append(
+                pltpu.make_async_copy(
+                    source.at[chip], down_ref.at[rows, :], sems.at[chips + place, chip]
+                )
+            )
+    for copy in [copy for group in fetched for copy in group] + handed:
         copy.start()
     peak = None
     total = None
@@ -209,39 +239,48 @@
         x_ref[number, pl.ds(0, half), :] = pieces[2 * number][...]
         x_ref[number, pl.ds(half, half), :] = pieces[2 * number + 1][...]
         x = x_ref[number]
-        copies[number].wait()
+        for copy in fetched[number]:
+            copy.wait()
         value = dot_nt(x, w_ref[number])
         total = value if total is None else total + value
         high = jnp.max(jnp.abs(x).astype(F32), axis=0, keepdims=True)
         peak = high if peak is None else jnp.maximum(peak, high)
     acc_ref[...] = total
     peak_ref[...] = peak
-    copies[3].wait()
-
-
-def near_chunks(pieces, table):
+    for copy in fetched[3] + handed:
+        copy.wait()
+
+
+def near_chunks(order, pieces, weights, downs):
     half, width = pieces[0].shape
-    wide = table.shape[1]
+    chips, unit, _ = downs[0].shape
+    wide = 2 * CORES * unit
     return pl.pallas_call(
         near_kernel,
-        in_specs=[IN_VMEM] * 6 + [IN_PLACE],
-        out_specs=[IN_VMEM] * 3,
+        in_specs=[IN_SMEM] + [IN_VMEM] * 6 + [IN_PLACE] * 6,
+        out_specs=[IN_VMEM] * 4,
         out_shape=[
             jax.ShapeDtypeStruct((2 * half, wide), F32),
             jax.ShapeDtypeStruct((1, width), F32),
             jax.ShapeDtypeStruct((wide, width), BF),
+            jax.ShapeDtypeStruct((chips * CORES * unit, width), BF),
         ],
         scratch_shapes=[
             pltpu.VMEM((3, 2 * half, width), BF),
             pltpu.VMEM((3, wide, width), BF),
-            pltpu.SemaphoreType.DMA((4,)),
+            pltpu.SemaphoreType.DMA((chips + 2, 4)),
         ],
         compiler_params=ROOM,
         cost_estimate=pl.CostEstimate(
-            flops=12 * half * width * wide, transcendentals=0, bytes_accessed=8 * width * wide
+            flops=12 * half * width * wide, transcendentals=0, bytes_accessed=12 * width * wide
         ),
         name="near_chunks",
-    )(*(local(piece) for piece in pieces), remote(table))
+    )(
+        order,
+        *(local(piece) for piece in pieces),
+        *(remote(array) for array in weights),
+        *(remote(array) for array in downs),
+    )
 
 
 def far_kernel(top_ref, low_ref, table_ref, acc_ref, peak_in, hid_ref, peak_ref, x_ref):
@@ -257,25 +296,29 @@
     peak_ref[...] = jnp.full(peak_ref.shape, peak, F32)
 
 
-def cut_kernel(order_ref, down_ref, *out_refs):
-    width = out_refs[0].shape[1]
-    for number, out_ref in enumerate(out_refs):
-        start = pl.multiple_of(order_ref[number] * width, width)
-        out_ref[...] = down_ref[:, pl.ds(start, width)]
+def cut_kernel(order_ref, down_ref, *refs):
+    outs, sems = refs[:-1], refs[-1]
+    width = outs[0].shape[1]
+    run_copies(
+        [
+            pltpu.make_async_copy(
+                down_ref.at[:, pl.ds(pl.multiple_of(order_ref[number] * width, width), width)],
+                out_ref,
+                sems.at[number],
+            )
+            for number, out_ref in enumerate(outs)
+        ]
+    )
 
 
 def stack_kernel(order_ref, *refs):
-    for number, piece in enumerate(refs[:-1]):
-        refs[-1][order_ref[number]] = piece[...]
-
-
-def pair_kernel(order_ref, own_ref, other_ref, out_ref):
-    chips, unit, _ = own_ref.shape
-    core = order_ref[4]
-    for chip in range(chips):
-        base = chip * CORES * unit
-        out_ref[pl.ds(pl.multiple_of(base + core * unit, unit), unit), :] = own_ref[chip]
-        out_ref[pl.ds(pl.multiple_of(base + (1 - core) * unit, unit), unit), :] = other_ref[chip]
+    pieces, (out_ref, sems) = refs[:-2], refs[-2:]
+    run_copies(
+        [
+            pltpu.make_async_copy(piece, out_ref.at[order_ref[number]], sems.at[number])
+            for number, piece in enumerate(pieces)
+        ]
+    )
 
 
 def down_kernel(hid_ref, down_ref, peak_in, out_ref, peak_ref, h_ref):
@@ -291,7 +334,7 @@
                 x * rows : (x + 1) * rows, core * width : (core + 1) * width
             ]
     peak = jnp.max(jnp.abs(hidden).astype(F32))
-    peak_ref[...] = jnp.where(iota(peak_ref.shape, 0) == 0, peak_in[...], peak)
+    peak_ref[...] = jnp.where(iota(peak_ref.shape, 1) == 0, peak_in[...], peak)
 
 
 def combine_kernel(high_ref, low_ref, row_ref, out_ref):
@@ -336,15 +379,8 @@
 
     gate_other = partner(gate_weight[0])
     up_other = partner(up_weight[0])
-    cuts = call(cut_kernel, order, (down_weight[0],), [shaped((unit, chunk), BF)] * chips)
+    cuts = move(cut_kernel, order, (down_weight[0],), [shaped((unit, chunk), BF)] * chips, chips)
     pieces = [cuts[0], shift(cuts[2], 1), shift(cuts[1], -1), shift(cuts[3], 2)]
-    table = call(
-        arrange_kernel,
-        order,
-        tuple(local(a) for a in (gate_weight[0], gate_other, up_weight[0], up_other)),
-        shaped((chips, 2 * units, chunk), BF),
-    )
-
     sent = call(
         pick_kernel,
         None,
@@ -356,12 +392,7 @@
         ),
     )
     received = lax.all_to_all(sent, ("x", "core"), split_axis=0, concat_axis=0, tiled=True)
-    stacked = call(
-        stack_kernel,
-        order,
-        tuple(remote(piece) for piece in pieces),
-        shaped((chips, unit, chunk), BF),
-    )
+    stacked = move(stack_kernel, order, pieces, shaped((chips, unit, chunk), BF), chips)
     stacked_other = partner(stacked)
     high, low = call(
         weigh_kernel,
@@ -374,8 +405,11 @@
     left_top, right_low = shift(top, 1), shift(bottom, -1)
     left_low, right_top = shift(bottom, 1), shift(top, -1)
     far_top, far_low = shift(left_top, 1), shift(right_low, -1)
-    acc, peak, last = near_chunks(
-        (top, bottom, left_top, left_low, right_top, right_low), table
+    acc, peak, last, down = near_chunks(
+        order,
+        (top, bottom, left_top, left_low, right_top, right_low),
+        (gate_weight[0], gate_other, up_weight[0], up_other),
+        (stacked, stacked_other),
     )
     hidden, peak = call(
         far_kernel,
@@ -383,12 +417,6 @@
         tuple(local(a) for a in (far_top, far_low, last, acc, peak)),
         [shaped((kept, units), BF), shaped((8, LANES), F32)],
         (pltpu.VMEM((kept, chunk), BF),),
-    )
-    down = call(
-        pair_kernel,
-        order,
-        (local(stacked), local(stacked_other)),
-        shaped((chips * units, chunk), BF),
     )
     gathered = lax.all_gather(hidden, "chip", axis=0)
     outputs, peak = call(
@@ -399,13 +427,14 @@
         (pltpu.VMEM((kept, chips * units), BF),),
     )
     returned = lax.all_to_all(outputs, ("x", "core"), split_axis=0, concat_axis=0, tiled=True)
-    column = jnp.maximum(peak, partner(peak))[:2, :1]
+    column = jnp.maximum(peak, partner(peak))[:1, :2].T
     sums = call(
         combine_kernel,
         None,
         tuple(local(a) for a in (high, low, returned)),
         shaped((planes, rows, width), BF),
     )
+    sums, column = lax.optimization_barrier((sums, column))
     parts = lax.all_to_all(sums, "z", split_axis=0, concat_axis=0, tiled=True)
     moe_out = call(total_kernel, None, (local(parts),), shaped((rows, width), BF))
     return moe_out, column

time: 158 us -> 151 us (0.956)
  blocking collectives: 27.9 us -> 58.4 us
  waiting for transfers between devices: 32.8 us -> 12.9 us
  starting transfers between devices: 71.6 us -> 60.6 us
  local copies, waits for them, and re-layouts: 6.15 us -> 2.03 us
  Pallas kernels: 17 us -> 14.8 us
    all_to_all x0 -> x1, blocking collectives: none -> 29.7 us  [layer(): parts = lax.all_to_all(sums, 'z', split_axis=0, concat_axis=0, tiled=True)]
    all_to_all x1 -> x0, waiting for transfers between devices: 14.2 us -> none  [layer(): parts = lax.all_to_all(sums, 'z', split_axis=0, concat_axis=0, tiled=True)]
    all_to_all x1 -> x0, starting transfers between devices: 12 us -> none  [layer(): parts = lax.all_to_all(sums, 'z', split_axis=0, concat_axis=0, tiled=True)]
    pallas_call x11 -> x7, Pallas kernels: 11.3 us -> 4.56 us  [call(): return run(*(() if order is None else (order,)), *inputs)]
    unnamed x17 -> x12, local copies, waits for them, and re-layouts: 6.14 us -> 1.51 us
    pallas_call x1 -> x3, Pallas kernels: 3.87 us -> 8.45 us  [the longest x1 4.59 us: near_chunks(): pl.pallas_call(near_kernel, in_specs=[IN_SMEM] + [IN_VMEM] * 6 + [IN_PLAC...]
    all_to_all x1, waiting for transfers between devices: 9.78 us -> 6.61 us  [layer(): lax.all_to_all(outputs, ('x', 'core'), split_axis=0, concat_axis=0, tiled...]
    ppermute x9, waiting for transfers between devices: 7.74 us -> 5.92 us  [shift(): lax.ppermute(array, 'chip', [(j, (j + step) % chips) for j in range(chips)])]
  transfers between devices with their start and end apart: 16 -> 15, of which waited for: 5 -> 4; matrix products, arithmetic and copies ran while one was open for 1% -> 1% of each run, Pallas kernels for 7% -> 6%
where the time goes in v1:
time: 151 us; the launch traced here: 150 us
  starting transfers between devices  60.6 us (40%)
  blocking collectives  58.4 us (39%)
  Pallas kernels  14.8 us (10%)
  waiting for transfers between devices  12.9 us (9%)
  local copies, waits for them, and re-layouts  2.03 us (1%)
    ppermute x9, starting transfers between devices, shift(): lax.ppermute(array, 'chip', [(j, (j + step) % chips) for j in range(chips)])  33.3 us
    all_to_all x1, blocking collectives, layer(): parts = lax.all_to_all(sums, 'z', split_axis=0, concat_axis=0, tiled=True)  29.7 us
    all_to_all x1, starting transfers between devices, layer(): lax.all_to_all(packed, 'z', split_axis=0, concat_axis=0, tiled=True)  15.2 us
    all_to_all x1, blocking collectives, layer(): lax.all_to_all(sent, ('x', 'core'), split_axis=0, concat_axis=0, tiled=True)  14.6 us
    all_gather x1, blocking collectives, layer(): gathered = lax.all_gather(hidden, 'chip', axis=0)  14.1 us
    ppermute x4, starting transfers between devices, partner(): return lax.ppermute(array, 'core', [(j, 1 - j) for j in range(CORES)])  8.55 us
    all_to_all x1, waiting for transfers between devices, layer(): lax.all_to_all(outputs, ('x', 'core'), split_axis=0, concat_axis=0, tiled...  6.61 us
    ppermute x9, waiting for transfers between devices, shift(): lax.ppermute(array, 'chip', [(j, (j + step) % chips) for j in range(chips)])  5.92 us
  transfers between devices with their start and end apart: 15, of which 4 were waited for; matrix products, arithmetic and copies ran while one was open for 1% of the time, Pallas kernels for 6%

profile of v1, /device:TPU:32, one launch (start us, length us, event | category | flops | bytes accessed | tf_op | source)
XLA Modules:
  0.0 150.3 jit_solution(14202033511965872456)
XLA Ops:
  0.6 0.0 copy-start.2
  0.6 1.8 %pack_tokens.1 = bf16[16,72,128]{2,1,0:T(8,128)(2,1)} custom-call(s32[8,16]{1,0:T(8,128)} %bitcast.14, f32[8,16]{1,0:T(8,128)} %bitcast.15, bf16[16,512]{1,0:T(8,128)(2,1)} %tok_hbm.1), custom_call_target="tpu_custom_call" | custom-call | tf_op jit(solution)/shard_map/pack_tokens/pallas_call | solution.py:109
  2.4 15.2 %all-to-all-start = ((bf16[16,72,128]{2,1,0:T(8,128)(2,1)}), bf16[16,72,128]{2,1,0:T(8,128)(2,1)S(1)}, u32[]{:S(2)}, u32[]{:S(2)}) async-start(bf16[16,72,128]{2,1,0:T(8,128)(2,1)} %pack_tokens.1), calls=%async_computation | async-start | bytes 589824 | tf_op jit(solution)/shard_map/all_to_all | solution.py:378
  17.7 0.7 compare_select_fusion.3.order_ref
  18.3 1.9 %shard_map.89 = (bf16[192,1024]{1,0:T(8,128)(2,1)S(1)}, bf16[192,1024]{1,0:T(8,128)(2,1)S(1)}, bf16[192,1024]{1,0:T(8,128)(2,1)S(1)}, bf16[192,1024]{1,0:T(8,128)(2,1)S(1)}) custom-call(s32[8]{0:T(128)S(1)} %compare_select_fusion.3.order_ref, bf16[192,4096]{1,0:T(8,128)(2,1)} %bitcast.9), custom_call_target="tpu_custom_call" | custom-call | tf_op jit(solution)/shard_map/pallas_call | solution.py:54
  20.3 0.0 copy-start.1
  20.3 0.7 copy-done.1
  21.0 5.1 %collective-permute-start.10 = (bf16[192,1024]{1,0:T(8,128)(2,1)S(1)}, bf16[192,1024]{1,0:T(8,128)(2,1)S(1)}, u32[]{:S(2)}, u32[]{:S(2)}) collective-permute-start(bf16[192,1024]{1,0:T(8,128)(2,1)S(1)} %get-tuple-element.27), channel_id=1, source_target_pairs={{0,4},{2,6},{4,0},{6,2},{1,5},{3,7},{5,1},{7,3},{8,12},{10,14},{12... | collective-permute-start | bytes 1179656 | tf_op jit(solution)/shard_map/ppermute | solution.py:366
  26.1 2.6 %collective-permute-start.8 = (bf16[192,1024]{1,0:T(8,128)(2,1)S(1)}, bf16[192,1024]{1,0:T(8,128)(2,1)S(1)}, u32[]{:S(2)}, u32[]{:S(2)}) collective-permute-start(bf16[192,1024]{1,0:T(8,128)(2,1)S(1)} %get-tuple-element.25), channel_id=1, source_target_pairs={{0,2},{2,4},{4,6},{6,0},{1,3},{3,5},{5,7},{7,1},{8,10},{10,12},{12... | collective-permute-start | bytes 1179656 | tf_op jit(solution)/shard_map/ppermute | solution.py:366
  28.7 4.5 %collective-permute-start.9 = (bf16[192,1024]{1,0:T(8,128)(2,1)S(1)}, bf16[192,1024]{1,0:T(8,128)(2,1)S(1)}, u32[]{:S(2)}, u32[]{:S(2)}) collective-permute-start(bf16[192,1024]{1,0:T(8,128)(2,1)S(1)} %get-tuple-element.26), channel_id=1, source_target_pairs={{0,6},{2,0},{4,2},{6,4},{1,7},{3,1},{5,3},{7,5},{8,14},{10,8},{12,... | collective-permute-start | bytes 1179656 | tf_op jit(solution)/shard_map/ppermute | solution.py:366
  33.2 0.0 copy-done.2
  33.2 1.9 %collective-permute-start.6 = (bf16[192,4096]{1,0:T(8,128)(2,1)S(1)}, bf16[192,4096]{1,0:T(8,128)(2,1)}, u32[]{:S(2)}, u32[]{:S(2)}) collective-permute-start(bf16[192,4096]{1,0:T(8,128)(2,1)S(1)} %bitcast.11), channel_id=1, source_target_pairs={{0,1},{1,0},{2,3},{3,2},{4,5},{5,4},{6,7},{7,6},{8,9},{9,8},{10,11... | collective-permute-start | bytes 4718600 | tf_op jit(solution)/shard_map/ppermute | solution.py:369
  35.1 2.4 %collective-permute-start.7 = (bf16[192,4096]{1,0:T(8,128)(2,1)}, bf16[192,4096]{1,0:T(8,128)(2,1)}, u32[]{:S(2)}, u32[]{:S(2)}) collective-permute-start(bf16[192,4096]{1,0:T(8,128)(2,1)} %bitcast.12), channel_id=1, source_target_pairs={{0,1},{1,0},{2,3},{3,2},{4,5},{5,4},{6,7},{7,6},{8,9},{9,8},{10,11... | collective-permute-start | bytes 4718600 | tf_op jit(solution)/shard_map/ppermute | solution.py:369
  37.5 0.0 collective-permute-done.10.refs_3_
  37.5 0.0 copy-start.3
  37.6 5.6 %collective-permute-done.8.refs_1_ = bf16[192,1024]{1,0:T(8,128)(2,1)S(1)} collective-permute-done((bf16[192,1024]{1,0:T(8,128)(2,1)S(1)}, bf16[192,1024]{1,0:T(8,128)(2,1)S(1)}, u32[]{:S(2)}, u32[]{:S(2)}) %collective-permute-start.8) | collective-permute-done | bytes 393248 | tf_op jit(solution)/shard_map/ppermute | solution.py:366
  43.1 0.0 copy-start.4
  43.1 0.3 collective-permute-done.9.refs_2_
  43.5 0.0 copy-start.5
  43.5 0.0 copy-done.3
  43.5 0.4 copy-done.4
  43.9 0.4 copy-done.5
  44.2 1.9 %shard_map.90.refs_10_ = bf16[4,192,1024]{2,1,0:T(8,128)(2,1)S(1)} custom-call(s32[8]{0:T(128)S(1)} %compare_select_fusion.3.order_ref, bf16[192,1024]{1,0:T(8,128)(2,1)} %copy-done.1, bf16[192,1024]{1,0:T(8,128)(2,1)} %copy-done.4, bf16[192,1024]{1,0:T(8,128)(2,1)} %copy-done.5, bf16[192,1024]{1,0:T(8,128)(2,1)} %copy-done.3), custom_call_target="tpu_custom_call" | custom-call | tf_op jit(solution)/shard_map/pallas_call | solution.py:54
  46.2 0.0 copy-start
  46.2 1.9 %collective-permute-start.11 = (bf16[4,192,1024]{2,1,0:T(8,128)(2,1)S(1)}, bf16[4,192,1024]{2,1,0:T(8,128)(2,1)}, u32[]{:S(2)}, u32[]{:S(2)}) collective-permute-start(bf16[4,192,1024]{2,1,0:T(8,128)(2,1)S(1)} %shard_map.90.refs_10_), channel_id=1, source_target_pairs={{0,1},{1,0},{2,3},{3,2},{4,5},{5,4},{6,7},{7,6},{8,9},{9,8},{10,11... | collective-permute-start | bytes 4718600 | tf_op jit(solution)/shard_map/ppermute | solution.py:369
  48.1 0.0 all-to-all-done.got_ref
  48.1 0.5 shard_map.87
  48.6 14.6 %all_to_all.20.got_ref = bf16[8,64,512]{2,1,0:T(8,128)(2,1)S(1)} all-to-all(bf16[8,64,512]{2,1,0:T(8,128)(2,1)S(1)} %shard_map.87), channel_id=1, replica_groups=mesh['x'=4,'z'=16,'chip'=4,'core'=2] {'x','core'}, dimensions={0} | all-to-all | bytes 1048576 | tf_op jit(solution)/shard_map/all_to_all | solution.py:394
  63.2 3.4 %collective-permute-start = (bf16[128,1024]{1,0:T(8,128)(2,1)S(1)}, bf16[128,1024]{1,0:T(8,128)(2,1)S(1)}, u32[]{:S(2)}, u32[]{:S(2)}) collective-permute-start(bf16[128,1024]{1,0:T(8,128)(2,1)S(1)} %get-tuple-element.22.refs_0_), channel_id=1, source_target_pairs={{0,2},{2,4},{4,6},{6,0},{1,3},{3,5},{5,7},{7,1},{8,10},{10,12},{12... | collective-permute-start | bytes 786440 | tf_op jit(solution)/shard_map/ppermute | solution.py:366
  66.6 3.6 %collective-permute-start.2 = (bf16[128,1024]{1,0:T(8,128)(2,1)S(1)}, bf16[128,1024]{1,0:T(8,128)(2,1)S(1)}, u32[]{:S(2)}, u32[]{:S(2)}) collective-permute-start(bf16[128,1024]{1,0:T(8,128)(2,1)S(1)} %get-tuple-element.23.refs_1_), channel_id=1, source_target_pairs={{0,6},{2,0},{4,2},{6,4},{1,7},{3,1},{5,3},{7,5},{8,14},{10,8},{12,... | collective-permute-start | bytes 786440 | tf_op jit(solution)/shard_map/ppermute | solution.py:366
  70.3 0.0 collective-permute-done.6.refs_7_
  70.3 2.2 %collective-permute-start.4 = (bf16[128,1024]{1,0:T(8,128)(2,1)S(1)}, bf16[128,1024]{1,0:T(8,128)(2,1)S(1)}, u32[]{:S(2)}, u32[]{:S(2)}) collective-permute-start(bf16[128,1024]{1,0:T(8,128)(2,1)S(1)} %get-tuple-element.23.refs_1_), channel_id=1, source_target_pairs={{0,2},{2,4},{4,6},{6,0},{1,3},{3,5},{5,7},{7,1},{8,10},{10,12},{12... | collective-permute-start | bytes 786440 | tf_op jit(solution)/shard_map/ppermute | solution.py:366
  72.5 0.0 collective-permute-done.7.refs_9_
  72.5 4.8 %collective-permute-start.5 = (bf16[128,1024]{1,0:T(8,128)(2,1)S(1)}, bf16[128,1024]{1,0:T(8,128)(2,1)S(1)}, u32[]{:S(2)}, u32[]{:S(2)}) collective-permute-start(bf16[128,1024]{1,0:T(8,128)(2,1)S(1)} %get-tuple-element.22.refs_0_), channel_id=1, source_target_pairs={{0,6},{2,0},{4,2},{6,4},{1,7},{3,1},{5,3},{7,5},{8,14},{10,8},{12,... | collective-permute-start | bytes 786440 | tf_op jit(solution)/shard_map/ppermute | solution.py:366
  77.4 0.0 collective-permute-done.refs_2_
  77.4 1.9 %collective-permute-start.1 = (bf16[128,1024]{1,0:T(8,128)(2,1)S(1)}, bf16[128,1024]{1,0:T(8,128)(2,1)S(1)}, u32[]{:S(2)}, u32[]{:S(2)}) collective-permute-start(bf16[128,1024]{1,0:T(8,128)(2,1)S(1)} %collective-permute-done.refs_2_), channel_id=1, source_target_pairs={{0,2},{2,4},{4,6},{6,0},{1,3},{3,5},{5,7},{7,1},{8,10},{10,12},{12... | collective-permute-start | bytes 786440 | tf_op jit(solution)/shard_map/ppermute | solution.py:366
  79.3 0.0 collective-permute-done.2.refs_5_
  79.3 5.1 %collective-permute-start.3 = (bf16[128,1024]{1,0:T(8,128)(2,1)S(1)}, bf16[128,1024]{1,0:T(8,128)(2,1)S(1)}, u32[]{:S(2)}, u32[]{:S(2)}) collective-permute-start(bf16[128,1024]{1,0:T(8,128)(2,1)S(1)} %collective-permute-done.2.refs_5_), channel_id=1, source_target_pairs={{0,6},{2,0},{4,2},{6,4},{1,7},{3,1},{5,3},{7,5},{8,14},{10,8},{12,... | collective-permute-start | bytes 786440 | tf_op jit(solution)/shard_map/ppermute | solution.py:366
  84.5 0.0 collective-permute-done.4.refs_3_
  84.5 0.0 collective-permute-done.5.refs_4_
  84.5 0.0 collective-permute-done.11.refs_11_
  84.5 0.0 copy-done
  84.5 4.6 %near_chunks.1 = (f32[256,768]{1,0:T(8,128)S(1)}, f32[1,1024]{1,0:T(1,128)S(1)}, bf16[768,1024]{1,0:T(8,128)(2,1)S(1)}, bf16[1536,1024]{1,0:T(8,128)(2,1)S(1)}) custom-call(s32[8]{0:T(128)S(1)} %compare_select_fusion.3.order_ref, bf16[128,1024]{1,0:T(8,128)(2,1)S(1)} %get-tuple-element.22.refs_0_, bf16[128,1024]{1,0:T(8,128)(2,1)S(1)} %get-tuple-element.23.refs_1_, ...), custom_call_target="tpu_custom_call" | custom-call | flops 1207959552 | bytes 9437184 | tf_op jit(solution)/shard_map/near_chunks/pallas_call | solution.py:258
  89.1 0.0 collective-permute-done.1.top_ref
  89.1 0.0 collective-permute-done.3.low_ref
  89.1 0.7 shard_map.91
  89.8 14.1 %all-gather = bf16[1024,384]{1,0:T(8,128)(2,1)S(1)} all-gather(bf16[256,384]{1,0:T(8,128)(2,1)S(1)} %get-tuple-element.31), channel_id=2, replica_groups=mesh['x'=4,'z'=16,'chip'=4,'core'=2] {'chip'}, dimensions={0}, use_global_device_ids=true | all-gather | bytes 983040 | tf_op jit(solution)/shard_map/all_gather | solution.py:421
  103.9 1.9 %shard_map.92 = (bf16[8,64,512]{2,1,0:T(8,128)(2,1)}, f32[8,128]{1,0:T(8,128)S(1)}) custom-call(bf16[4,256,384]{2,1,0:T(8,128)(2,1)S(1)} %bitcast.8, bf16[1536,1024]{1,0:T(8,128)(2,1)S(1)} %get-tuple-element.32.down_ref, f32[8,128]{1,0:T(8,128)S(1)} %get-tuple-element.33.peak_in), custom_call_target="tpu_custom_call" | custom-call | tf_op jit(solution)/shard_map/pallas_call | solution.py:76
  105.8 3.5 %all-to-all-start.2 = ((bf16[8,64,512]{2,1,0:T(8,128)(2,1)}), bf16[8,64,512]{2,1,0:T(8,128)(2,1)S(1)}, u32[]{:S(2)}, u32[]{:S(2)}) async-start(bf16[8,64,512]{2,1,0:T(8,128)(2,1)} %get-tuple-element.34), calls=%async_computation.2 | async-start | bytes 1048576 | tf_op jit(solution)/shard_map/all_to_all | solution.py:429
  109.3 2.3 %collective-permute-start.12 = (f32[8,128]{1,0:T(8,128)S(1)}, f32[8,128]{1,0:T(8,128)S(1)}, u32[]{:S(2)}, u32[]{:S(2)}) collective-permute-start(f32[8,128]{1,0:T(8,128)S(1)} %get-tuple-element.35), channel_id=1, source_target_pairs={{0,1},{1,0},{2,3},{3,2},{4,5},{5,4},{6,7},{7,6},{8,9},{9,8},{10,11... | collective-permute-start | bytes 12296 | tf_op jit(solution)/shard_map/ppermute | solution.py:369
  111.6 0.5 shard_map.86
  112.0 0.3 collective-permute-done.12
  112.4 0.5 slice_bitcast_fusion
  112.9 6.6 %all-to-all-done.2.row_ref = bf16[8,64,512]{2,1,0:T(8,128)(2,1)S(1)} async-done(((bf16[8,64,512]{2,1,0:T(8,128)(2,1)}), bf16[8,64,512]{2,1,0:T(8,128)(2,1)S(1)}, u32[]{:S(2)}, u32[]{:S(2)}) %all-to-all-start.2) | async-done | bytes 524320 | tf_op jit(solution)/shard_map/all_to_all | solution.py:429
  119.5 0.4 shard_map.93
  120.0 29.7 %all_to_all.21.part_ref = bf16[16,16,512]{2,1,0:T(8,128)(2,1)S(1)} all-to-all(bf16[16,16,512]{2,1,0:T(8,128)(2,1)S(1)} %shard_map.93), channel_id=1, replica_groups=mesh['x'=4,'z'=16,'chip'=4,'core'=2] {'z'}, dimensions={0} | all-to-all | bytes 524288 | tf_op jit(solution)/shard_map/all_to_all | solution.py:438
  149.6 0.6 shard_map.94
  (2 shorter events, 0.0 us)
Async XLA Ops:
  0.6 32.5 %copy-start.2 = (bf16[1,192,4096]{2,1,0:T(8,128)(2,1)S(1)}, bf16[1,192,4096]{2,1,0:T(8,128)(2,1)}, u32[]{:S(2)}) copy-start(bf16[1,192,4096]{2,1,0:T(8,128)(2,1)} %param.10) | copy-start | bytes 4718596
  2.4 45.7 %all-to-all-start = ((bf16[16,72,128]{2,1,0:T(8,128)(2,1)}), bf16[16,72,128]{2,1,0:T(8,128)(2,1)S(1)}, u32[]{:S(2)}, u32[]{:S(2)}) async-start(bf16[16,72,128]{2,1,0:T(8,128)(2,1)} %pack_tokens.1), calls=%async_computation | async-start | bytes 589824 | tf_op jit(solution)/shard_map/all_to_all | solution.py:378
  20.3 0.7 copy-start.1
  21.0 16.5 %collective-permute-start.10 = (bf16[192,1024]{1,0:T(8,128)(2,1)S(1)}, bf16[192,1024]{1,0:T(8,128)(2,1)S(1)}, u32[]{:S(2)}, u32[]{:S(2)}) collective-permute-start(bf16[192,1024]{1,0:T(8,128)(2,1)S(1)} %get-tuple-element.27), channel_id=1, source_target_pairs={{0,4},{2,6},{4,0},{6,2},{1,5},{3,7},{5,1},{7,3},{8,12},{10,14},{12... | collective-permute-start | bytes 1179656 | tf_op jit(solution)/shard_map/ppermute | solution.py:366
  26.1 17.0 %collective-permute-start.8 = (bf16[192,1024]{1,0:T(8,128)(2,1)S(1)}, bf16[192,1024]{1,0:T(8,128)(2,1)S(1)}, u32[]{:S(2)}, u32[]{:S(2)}) collective-permute-start(bf16[192,1024]{1,0:T(8,128)(2,1)S(1)} %get-tuple-element.25), channel_id=1, source_target_pairs={{0,2},{2,4},{4,6},{6,0},{1,3},{3,5},{5,7},{7,1},{8,10},{10,12},{12... | collective-permute-start | bytes 1179656 | tf_op jit(solution)/shard_map/ppermute | solution.py:366
  28.7 14.8 %collective-permute-start.9 = (bf16[192,1024]{1,0:T(8,128)(2,1)S(1)}, bf16[192,1024]{1,0:T(8,128)(2,1)S(1)}, u32[]{:S(2)}, u32[]{:S(2)}) collective-permute-start(bf16[192,1024]{1,0:T(8,128)(2,1)S(1)} %get-tuple-element.26), channel_id=1, source_target_pairs={{0,6},{2,0},{4,2},{6,4},{1,7},{3,1},{5,3},{7,5},{8,14},{10,8},{12,... | collective-permute-start | bytes 1179656 | tf_op jit(solution)/shard_map/ppermute | solution.py:366
  33.2 37.1 %collective-permute-start.6 = (bf16[192,4096]{1,0:T(8,128)(2,1)S(1)}, bf16[192,4096]{1,0:T(8,128)(2,1)}, u32[]{:S(2)}, u32[]{:S(2)}) collective-permute-start(bf16[192,4096]{1,0:T(8,128)(2,1)S(1)} %bitcast.11), channel_id=1, source_target_pairs={{0,1},{1,0},{2,3},{3,2},{4,5},{5,4},{6,7},{7,6},{8,9},{9,8},{10,11... | collective-permute-start | bytes 4718600 | tf_op jit(solution)/shard_map/ppermute | solution.py:369
  35.1 37.4 %collective-permute-start.7 = (bf16[192,4096]{1,0:T(8,128)(2,1)}, bf16[192,4096]{1,0:T(8,128)(2,1)}, u32[]{:S(2)}, u32[]{:S(2)}) collective-permute-start(bf16[192,4096]{1,0:T(8,128)(2,1)} %bitcast.12), channel_id=1, source_target_pairs={{0,1},{1,0},{2,3},{3,2},{4,5},{5,4},{6,7},{7,6},{8,9},{9,8},{10,11... | collective-permute-start | bytes 4718600 | tf_op jit(solution)/shard_map/ppermute | solution.py:369
  37.5 5.9 %copy-start.3 = (bf16[192,1024]{1,0:T(8,128)(2,1)}, bf16[192,1024]{1,0:T(8,128)(2,1)S(1)}, u32[]{:S(2)}) copy-start(bf16[192,1024]{1,0:T(8,128)(2,1)S(1)} %collective-permute-done.10.refs_3_) | copy-start | bytes 1179652
  43.1 0.7 copy-start.4
  43.5 0.8 copy-start.5
  46.2 38.3 %copy-start = (bf16[4,192,1024]{2,1,0:T(8,128)(2,1)}, bf16[4,192,1024]{2,1,0:T(8,128)(2,1)S(1)}, u32[]{:S(2)}) copy-start(bf16[4,192,1024]{2,1,0:T(8,128)(2,1)S(1)} %shard_map.90.refs_10_) | copy-start | bytes 4718596
  46.2 38.3 %collective-permute-start.11 = (bf16[4,192,1024]{2,1,0:T(8,128)(2,1)S(1)}, bf16[4,192,1024]{2,1,0:T(8,128)(2,1)}, u32[]{:S(2)}, u32[]{:S(2)}) collective-permute-start(bf16[4,192,1024]{2,1,0:T(8,128)(2,1)S(1)} %shard_map.90.refs_10_), channel_id=1, source_target_pairs={{0,1},{1,0},{2,3},{3,2},{4,5},{5,4},{6,7},{7,6},{8,9},{9,8},{10,11... | collective-permute-start | bytes 4718600 | tf_op jit(solution)/shard_map/ppermute | solution.py:369
  63.2 14.2 %collective-permute-start = (bf16[128,1024]{1,0:T(8,128)(2,1)S(1)}, bf16[128,1024]{1,0:T(8,128)(2,1)S(1)}, u32[]{:S(2)}, u32[]{:S(2)}) collective-permute-start(bf16[128,1024]{1,0:T(8,128)(2,1)S(1)} %get-tuple-element.22.refs_0_), channel_id=1, source_target_pairs={{0,2},{2,4},{4,6},{6,0},{1,3},{3,5},{5,7},{7,1},{8,10},{10,12},{12... | collective-permute-start | bytes 786440 | tf_op jit(solution)/shard_map/ppermute | solution.py:366
  66.6 12.7 %collective-permute-start.2 = (bf16[128,1024]{1,0:T(8,128)(2,1)S(1)}, bf16[128,1024]{1,0:T(8,128)(2,1)S(1)}, u32[]{:S(2)}, u32[]{:S(2)}) collective-permute-start(bf16[128,1024]{1,0:T(8,128)(2,1)S(1)} %get-tuple-element.23.refs_1_), channel_id=1, source_target_pairs={{0,6},{2,0},{4,2},{6,4},{1,7},{3,1},{5,3},{7,5},{8,14},{10,8},{12,... | collective-permute-start | bytes 786440 | tf_op jit(solution)/shard_map/ppermute | solution.py:366
  70.3 14.2 %collective-permute-start.4 = (bf16[128,1024]{1,0:T(8,128)(2,1)S(1)}, bf16[128,1024]{1,0:T(8,128)(2,1)S(1)}, u32[]{:S(2)}, u32[]{:S(2)}) collective-permute-start(bf16[128,1024]{1,0:T(8,128)(2,1)S(1)} %get-tuple-element.23.refs_1_), channel_id=1, source_target_pairs={{0,2},{2,4},{4,6},{6,0},{1,3},{3,5},{5,7},{7,1},{8,10},{10,12},{12... | collective-permute-start | bytes 786440 | tf_op jit(solution)/shard_map/ppermute | solution.py:366
  72.5 12.0 %collective-permute-start.5 = (bf16[128,1024]{1,0:T(8,128)(2,1)S(1)}, bf16[128,1024]{1,0:T(8,128)(2,1)S(1)}, u32[]{:S(2)}, u32[]{:S(2)}) collective-permute-start(bf16[128,1024]{1,0:T(8,128)(2,1)S(1)} %get-tuple-element.22.refs_0_), channel_id=1, source_target_pairs={{0,6},{2,0},{4,2},{6,4},{1,7},{3,1},{5,3},{7,5},{8,14},{10,8},{12,... | collective-permute-start | bytes 786440 | tf_op jit(solution)/shard_map/ppermute | solution.py:366
  77.4 11.7 %collective-permute-start.1 = (bf16[128,1024]{1,0:T(8,128)(2,1)S(1)}, bf16[128,1024]{1,0:T(8,128)(2,1)S(1)}, u32[]{:S(2)}, u32[]{:S(2)}) collective-permute-start(bf16[128,1024]{1,0:T(8,128)(2,1)S(1)} %collective-permute-done.refs_2_), channel_id=1, source_target_pairs={{0,2},{2,4},{4,6},{6,0},{1,3},{3,5},{5,7},{7,1},{8,10},{10,12},{12... | collective-permute-start | bytes 786440 | tf_op jit(solution)/shard_map/ppermute | solution.py:366
  79.3 9.8 %collective-permute-start.3 = (bf16[128,1024]{1,0:T(8,128)(2,1)S(1)}, bf16[128,1024]{1,0:T(8,128)(2,1)S(1)}, u32[]{:S(2)}, u32[]{:S(2)}) collective-permute-start(bf16[128,1024]{1,0:T(8,128)(2,1)S(1)} %collective-permute-done.2.refs_5_), channel_id=1, source_target_pairs={{0,6},{2,0},{4,2},{6,4},{1,7},{3,1},{5,3},{7,5},{8,14},{10,8},{12,... | collective-permute-start | bytes 786440 | tf_op jit(solution)/shard_map/ppermute | solution.py:366
  105.8 13.7 %all-to-all-start.2 = ((bf16[8,64,512]{2,1,0:T(8,128)(2,1)}), bf16[8,64,512]{2,1,0:T(8,128)(2,1)S(1)}, u32[]{:S(2)}, u32[]{:S(2)}) async-start(bf16[8,64,512]{2,1,0:T(8,128)(2,1)} %get-tuple-element.34), calls=%async_computation.2 | async-start | bytes 1048576 | tf_op jit(solution)/shard_map/all_to_all | solution.py:429
  109.3 3.1 %collective-permute-start.12 = (f32[8,128]{1,0:T(8,128)S(1)}, f32[8,128]{1,0:T(8,128)S(1)}, u32[]{:S(2)}, u32[]{:S(2)}) collective-permute-start(f32[8,128]{1,0:T(8,128)S(1)} %get-tuple-element.35), channel_id=1, source_target_pairs={{0,1},{1,0},{2,3},{3,2},{4,5},{5,4},{6,7},{7,6},{8,9},{9,8},{10,11... | collective-permute-start | bytes 12296 | tf_op jit(solution)/shard_map/ppermute | solution.py:369

commit v2 on v1

--- a/solution.py
+++ b/solution.py
@@ -11,6 +11,7 @@
 SLOTS = 8
 CORES = 2
 X = 4
+NEAR = 4
 LANES = 128
 BF = jnp.bfloat16
 F32 = jnp.float32
@@ -340,7 +341,12 @@
 def combine_kernel(high_ref, low_ref, row_ref, out_ref):
     rows = row_ref[...].reshape(high_ref.shape[1], row_ref.shape[2])
     value = dot_nn(high_ref[...], rows) + dot_nn(low_ref[...], rows)
-    out_ref[...] = value.astype(BF).reshape(out_ref.shape)
+    value = value.astype(BF)
+    near, blocks, rows, _ = out_ref.shape
+    for low in range(near):
+        for high in range(blocks):
+            start = (high * near + low) * rows
+            out_ref[low, high] = value[start : start + rows]
 
 
 def total_kernel(part_ref, out_ref):
@@ -351,7 +357,8 @@
 
 
 def layer(tokens, expert_ids, route_weight, gate_weight, up_weight, down_weight):
-    planes = lax.axis_size("z")
+    near = lax.axis_size("zlow")
+    planes = lax.axis_size("zhigh") * near
     chips = lax.axis_size("chip")
     core = lax.axis_index("core")
     place = lax.axis_index("chip")
@@ -371,11 +378,11 @@
     lane = jnp.arange(8, dtype=jnp.int32)
     turns = jnp.array([0, chips - 1, 1, 2, 0, 0, 0, 0], jnp.int32)
     order = jnp.where(
-        lane < 4, (place + turns) % chips, jnp.where(lane == 4, core, lax.axis_index("z"))
+        lane < 4, (place + turns) % chips, core
     ).astype(jnp.int32)
 
     packed = pack_tokens(expert_ids.T, route_weight.T, tokens, planes)
-    plane_rows = lax.all_to_all(packed, "z", split_axis=0, concat_axis=0, tiled=True)
+    plane_rows = lax.all_to_all(packed, ("zhigh", "zlow"), split_axis=0, concat_axis=0, tiled=True)
 
     gate_other = partner(gate_weight[0])
     up_other = partner(up_weight[0])
@@ -432,10 +439,12 @@
         combine_kernel,
         None,
         tuple(local(a) for a in (high, low, returned)),
-        shaped((planes, rows, width), BF),
+        shaped((near, planes // near, rows, width), BF),
     )
     sums, column = lax.optimization_barrier((sums, column))
-    parts = lax.all_to_all(sums, "z", split_axis=0, concat_axis=0, tiled=True)
+    parts = lax.all_to_all(sums, "zlow", split_axis=0, concat_axis=0, tiled=True)
+    sums = call(total_kernel, None, (local(parts),), shaped((planes // near, rows, width), BF))
+    parts = lax.all_to_all(sums, "zhigh", split_axis=0, concat_axis=0, tiled=True)
     moe_out = call(total_kernel, None, (local(parts),), shaped((rows, width), BF))
     return moe_out, column
 
@@ -444,9 +453,10 @@
     devices = np.asarray(mesh.devices)
     ep, tp = devices.shape
     fine = Mesh(
-        devices.reshape(X, ep // X, tp // CORES, CORES), ("x", "z", "chip", "core")
-    )
-    ep, tp = ("x", "z"), ("chip", "core")
+        devices.reshape(X, ep // (X * NEAR), NEAR, tp // CORES, CORES),
+        ("x", "zhigh", "zlow", "chip", "core"),
+    )
+    ep, tp = ("x", "zhigh", "zlow"), ("chip", "core")
     return jax.shard_map(
         layer,
         mesh=fine,

time: 151 us -> 157 us (1.040)
  the two profiles are of different devices: /device:TPU:32 before, /device:TPU:8 now
where the time goes in v2:
time: 157 us; the launch traced here: 156 us
  blocking collectives  65.8 us (42%)
  starting transfers between devices  55.7 us (35%)
  waiting for transfers between devices  15.8 us (10%)
  Pallas kernels  14.8 us (9%)
  local copies, waits for them, and re-layouts  2.14 us (1%)
    ppermute x9, starting transfers between devices, shift(): lax.ppermute(array, 'chip', [(j, (j + step) % chips) for j in range(chips)])  28.5 us
    all_to_all x1, blocking collectives, layer(): lax.all_to_all(sums, 'zhigh', split_axis=0, concat_axis=0, tiled=True)  22.6 us
    all_gather x1, blocking collectives, layer(): gathered = lax.all_gather(hidden, 'chip', axis=0)  15.5 us
    all_to_all x1, starting transfers between devices, layer(): lax.all_to_all(packed, ('zhigh', 'zlow'), split_axis=0, concat_axis=0, ti...  15.2 us
    all_to_all x1, blocking collectives, layer(): lax.all_to_all(sent, ('x', 'core'), split_axis=0, concat_axis=0, tiled=True)  14.6 us
    all_to_all x1, blocking collectives, layer(): lax.all_to_all(sums, 'zlow', split_axis=0, concat_axis=0, tiled=True)  13.1 us
    ppermute x9, waiting for transfers between devices, shift(): lax.ppermute(array, 'chip', [(j, (j + step) % chips) for j in range(chips)])  8.86 us
    ppermute x4, starting transfers between devices, partner(): return lax.ppermute(array, 'core', [(j, 1 - j) for j in range(CORES)])  8.55 us
  transfers between devices with their start and end apart: 15, of which 6 were waited for; matrix products, arithmetic and copies ran while one was open for 1% of the time, Pallas kernels for 6%

profile of v2, /device:TPU:8, one launch (start us, length us, event | category | flops | bytes accessed | tf_op | source)
XLA Modules:
  0.0 155.9 jit_solution(2637571965612840540)
XLA Ops:
  0.6 0.0 copy-start.2
  0.6 1.8 %pack_tokens.1 = bf16[16,72,128]{2,1,0:T(8,128)(2,1)} custom-call(s32[8,16]{1,0:T(8,128)} %bitcast.14, f32[8,16]{1,0:T(8,128)} %bitcast.15, bf16[16,512]{1,0:T(8,128)(2,1)} %tok_hbm.1), custom_call_target="tpu_custom_call" | custom-call | tf_op jit(solution)/shard_map/pack_tokens/pallas_call | solution.py:110
  2.4 15.2 %all-to-all-start = ((bf16[16,72,128]{2,1,0:T(8,128)(2,1)}), bf16[16,72,128]{2,1,0:T(8,128)(2,1)S(1)}, u32[]{:S(2)}, u32[]{:S(2)}) async-start(bf16[16,72,128]{2,1,0:T(8,128)(2,1)} %pack_tokens.1), calls=%async_computation | async-start | bytes 589824 | tf_op jit(solution)/shard_map/all_to_all | solution.py:385
  17.7 0.7 compare_select_fusion.2.order_ref
  18.3 1.9 %shard_map.89 = (bf16[192,1024]{1,0:T(8,128)(2,1)S(1)}, bf16[192,1024]{1,0:T(8,128)(2,1)S(1)}, bf16[192,1024]{1,0:T(8,128)(2,1)S(1)}, bf16[192,1024]{1,0:T(8,128)(2,1)S(1)}) custom-call(s32[8]{0:T(128)S(1)} %compare_select_fusion.2.order_ref, bf16[192,4096]{1,0:T(8,128)(2,1)} %bitcast.9), custom_call_target="tpu_custom_call" | custom-call | tf_op jit(solution)/shard_map/pallas_call | solution.py:55
  20.3 0.0 copy-start.1
  20.3 0.7 copy-done.1
  21.0 4.2 %collective-permute-start.10 = (bf16[192,1024]{1,0:T(8,128)(2,1)S(1)}, bf16[192,1024]{1,0:T(8,128)(2,1)S(1)}, u32[]{:S(2)}, u32[]{:S(2)}) collective-permute-start(bf16[192,1024]{1,0:T(8,128)(2,1)S(1)} %get-tuple-element.27), channel_id=1, source_target_pairs={{0,4},{2,6},{4,0},{6,2},{1,5},{3,7},{5,1},{7,3},{8,12},{10,14},{12... | collective-permute-start | bytes 1179656 | tf_op jit(solution)/shard_map/ppermute | solution.py:373
  25.2 1.9 %collective-permute-start.8 = (bf16[192,1024]{1,0:T(8,128)(2,1)S(1)}, bf16[192,1024]{1,0:T(8,128)(2,1)S(1)}, u32[]{:S(2)}, u32[]{:S(2)}) collective-permute-start(bf16[192,1024]{1,0:T(8,128)(2,1)S(1)} %get-tuple-element.25), channel_id=1, source_target_pairs={{0,2},{2,4},{4,6},{6,0},{1,3},{3,5},{5,7},{7,1},{8,10},{10,12},{12... | collective-permute-start | bytes 1179656 | tf_op jit(solution)/shard_map/ppermute | solution.py:373
  27.1 3.9 %collective-permute-start.9 = (bf16[192,1024]{1,0:T(8,128)(2,1)S(1)}, bf16[192,1024]{1,0:T(8,128)(2,1)S(1)}, u32[]{:S(2)}, u32[]{:S(2)}) collective-permute-start(bf16[192,1024]{1,0:T(8,128)(2,1)S(1)} %get-tuple-element.26), channel_id=1, source_target_pairs={{0,6},{2,0},{4,2},{6,4},{1,7},{3,1},{5,3},{7,5},{8,14},{10,8},{12,... | collective-permute-start | bytes 1179656 | tf_op jit(solution)/shard_map/ppermute | solution.py:373
  31.1 0.0 copy-done.2
  31.1 1.9 %collective-permute-start.6 = (bf16[192,4096]{1,0:T(8,128)(2,1)S(1)}, bf16[192,4096]{1,0:T(8,128)(2,1)}, u32[]{:S(2)}, u32[]{:S(2)}) collective-permute-start(bf16[192,4096]{1,0:T(8,128)(2,1)S(1)} %bitcast.11), channel_id=1, source_target_pairs={{0,1},{1,0},{2,3},{3,2},{4,5},{5,4},{6,7},{7,6},{8,9},{9,8},{10,11... | collective-permute-start | bytes 4718600 | tf_op jit(solution)/shard_map/ppermute | solution.py:376
  33.0 2.4 %collective-permute-start.7 = (bf16[192,4096]{1,0:T(8,128)(2,1)}, bf16[192,4096]{1,0:T(8,128)(2,1)}, u32[]{:S(2)}, u32[]{:S(2)}) collective-permute-start(bf16[192,4096]{1,0:T(8,128)(2,1)} %bitcast.12), channel_id=1, source_target_pairs={{0,1},{1,0},{2,3},{3,2},{4,5},{5,4},{6,7},{7,6},{8,9},{9,8},{10,11... | collective-permute-start | bytes 4718600 | tf_op jit(solution)/shard_map/ppermute | solution.py:376
  35.4 1.0 collective-permute-done.10.refs_3_
  36.4 0.0 copy-start.3
  36.4 7.1 %collective-permute-done.8.refs_1_ = bf16[192,1024]{1,0:T(8,128)(2,1)S(1)} collective-permute-done((bf16[192,1024]{1,0:T(8,128)(2,1)S(1)}, bf16[192,1024]{1,0:T(8,128)(2,1)S(1)}, u32[]{:S(2)}, u32[]{:S(2)}) %collective-permute-start.8) | collective-permute-done | bytes 393248 | tf_op jit(solution)/shard_map/ppermute | solution.py:373
  43.6 0.0 copy-start.4
  43.6 0.0 collective-permute-done.9.refs_2_
  43.6 0.0 copy-start.5
  43.6 0.0 copy-done.3
  43.6 0.7 copy-done.4
  44.3 0.2 copy-done.5
  44.4 1.9 %shard_map.90.refs_10_ = bf16[4,192,1024]{2,1,0:T(8,128)(2,1)S(1)} custom-call(s32[8]{0:T(128)S(1)} %compare_select_fusion.2.order_ref, bf16[192,1024]{1,0:T(8,128)(2,1)} %copy-done.1, bf16[192,1024]{1,0:T(8,128)(2,1)} %copy-done.4, bf16[192,1024]{1,0:T(8,128)(2,1)} %copy-done.5, bf16[192,1024]{1,0:T(8,128)(2,1)} %copy-done.3), custom_call_target="tpu_custom_call" | custom-call | tf_op jit(solution)/shard_map/pallas_call | solution.py:55
  46.4 0.0 copy-start
  46.4 1.9 %collective-permute-start.11 = (bf16[4,192,1024]{2,1,0:T(8,128)(2,1)S(1)}, bf16[4,192,1024]{2,1,0:T(8,128)(2,1)}, u32[]{:S(2)}, u32[]{:S(2)}) collective-permute-start(bf16[4,192,1024]{2,1,0:T(8,128)(2,1)S(1)} %shard_map.90.refs_10_), channel_id=1, source_target_pairs={{0,1},{1,0},{2,3},{3,2},{4,5},{5,4},{6,7},{7,6},{8,9},{9,8},{10,11... | collective-permute-start | bytes 4718600 | tf_op jit(solution)/shard_map/ppermute | solution.py:376
  48.3 0.0 all-to-all-done.got_ref
  48.3 0.5 shard_map.87
  48.8 14.6 %all_to_all.25.got_ref = bf16[8,64,512]{2,1,0:T(8,128)(2,1)S(1)} all-to-all(bf16[8,64,512]{2,1,0:T(8,128)(2,1)S(1)} %shard_map.87), channel_id=1, replica_groups=mesh['x'=4,'zhigh'=4,'zlow'=4,'chip'=4,'core'=2] {'x','core'}, dimensions={0} | all-to-all | bytes 1048576 | tf_op jit(solution)/shard_map/all_to_all | solution.py:401
  63.4 3.3 %collective-permute-start = (bf16[128,1024]{1,0:T(8,128)(2,1)S(1)}, bf16[128,1024]{1,0:T(8,128)(2,1)S(1)}, u32[]{:S(2)}, u32[]{:S(2)}) collective-permute-start(bf16[128,1024]{1,0:T(8,128)(2,1)S(1)} %get-tuple-element.22.refs_0_), channel_id=1, source_target_pairs={{0,2},{2,4},{4,6},{6,0},{1,3},{3,5},{5,7},{7,1},{8,10},{10,12},{12... | collective-permute-start | bytes 786440 | tf_op jit(solution)/shard_map/ppermute | solution.py:373
  66.8 2.5 %collective-permute-start.2 = (bf16[128,1024]{1,0:T(8,128)(2,1)S(1)}, bf16[128,1024]{1,0:T(8,128)(2,1)S(1)}, u32[]{:S(2)}, u32[]{:S(2)}) collective-permute-start(bf16[128,1024]{1,0:T(8,128)(2,1)S(1)} %get-tuple-element.23.refs_1_), channel_id=1, source_target_pairs={{0,6},{2,0},{4,2},{6,4},{1,7},{3,1},{5,3},{7,5},{8,14},{10,8},{12,... | collective-permute-start | bytes 786440 | tf_op jit(solution)/shard_map/ppermute | solution.py:373
  69.3 0.0 collective-permute-done.6.refs_7_
  69.3 3.3 %collective-permute-start.4 = (bf16[128,1024]{1,0:T(8,128)(2,1)S(1)}, bf16[128,1024]{1,0:T(8,128)(2,1)S(1)}, u32[]{:S(2)}, u32[]{:S(2)}) collective-permute-start(bf16[128,1024]{1,0:T(8,128)(2,1)S(1)} %get-tuple-element.23.refs_1_), channel_id=1, source_target_pairs={{0,2},{2,4},{4,6},{6,0},{1,3},{3,5},{5,7},{7,1},{8,10},{10,12},{12... | collective-permute-start | bytes 786440 | tf_op jit(solution)/shard_map/ppermute | solution.py:373
  72.6 0.0 collective-permute-done.7.refs_9_
  72.6 2.5 %collective-permute-start.5 = (bf16[128,1024]{1,0:T(8,128)(2,1)S(1)}, bf16[128,1024]{1,0:T(8,128)(2,1)S(1)}, u32[]{:S(2)}, u32[]{:S(2)}) collective-permute-start(bf16[128,1024]{1,0:T(8,128)(2,1)S(1)} %get-tuple-element.22.refs_0_), channel_id=1, source_target_pairs={{0,6},{2,0},{4,2},{6,4},{1,7},{3,1},{5,3},{7,5},{8,14},{10,8},{12,... | collective-permute-start | bytes 786440 | tf_op jit(solution)/shard_map/ppermute | solution.py:373
  75.2 0.0 collective-permute-done.refs_2_
  75.2 3.3 %collective-permute-start.1 = (bf16[128,1024]{1,0:T(8,128)(2,1)S(1)}, bf16[128,1024]{1,0:T(8,128)(2,1)S(1)}, u32[]{:S(2)}, u32[]{:S(2)}) collective-permute-start(bf16[128,1024]{1,0:T(8,128)(2,1)S(1)} %collective-permute-done.refs_2_), channel_id=1, source_target_pairs={{0,2},{2,4},{4,6},{6,0},{1,3},{3,5},{5,7},{7,1},{8,10},{10,12},{12... | collective-permute-start | bytes 786440 | tf_op jit(solution)/shard_map/ppermute | solution.py:373
  78.5 0.0 collective-permute-done.2.refs_5_
  78.5 3.4 %collective-permute-start.3 = (bf16[128,1024]{1,0:T(8,128)(2,1)S(1)}, bf16[128,1024]{1,0:T(8,128)(2,1)S(1)}, u32[]{:S(2)}, u32[]{:S(2)}) collective-permute-start(bf16[128,1024]{1,0:T(8,128)(2,1)S(1)} %collective-permute-done.2.refs_5_), channel_id=1, source_target_pairs={{0,6},{2,0},{4,2},{6,4},{1,7},{3,1},{5,3},{7,5},{8,14},{10,8},{12,... | collective-permute-start | bytes 786440 | tf_op jit(solution)/shard_map/ppermute | solution.py:373
  82.0 0.0 collective-permute-done.4.refs_3_
  82.0 0.3 collective-permute-done.5.refs_4_
  82.3 0.0 collective-permute-done.11.refs_11_
  82.3 0.0 copy-done
  82.3 4.6 %near_chunks.1 = (f32[256,768]{1,0:T(8,128)S(1)}, f32[1,1024]{1,0:T(1,128)S(1)}, bf16[768,1024]{1,0:T(8,128)(2,1)S(1)}, bf16[1536,1024]{1,0:T(8,128)(2,1)S(1)}) custom-call(s32[8]{0:T(128)S(1)} %compare_select_fusion.2.order_ref, bf16[128,1024]{1,0:T(8,128)(2,1)S(1)} %get-tuple-element.22.refs_0_, bf16[128,1024]{1,0:T(8,128)(2,1)S(1)} %get-tuple-element.23.refs_1_, ...), custom_call_target="tpu_custom_call" | custom-call | flops 1207959552 | bytes 9437184 | tf_op jit(solution)/shard_map/near_chunks/pallas_call | solution.py:259
  86.9 0.0 collective-permute-done.1.top_ref
  86.9 0.4 collective-permute-done.3.low_ref
  87.3 0.7 shard_map.91
  88.0 15.5 %all-gather = bf16[1024,384]{1,0:T(8,128)(2,1)S(1)} all-gather(bf16[256,384]{1,0:T(8,128)(2,1)S(1)} %get-tuple-element.31), channel_id=2, replica_groups=mesh['x'=4,'zhigh'=4,'zlow'=4,'chip'=4,'core'=2] {'chip'}, dimensions={0}, use_global_device_ids=true | all-gather | bytes 983040 | tf_op jit(solution)/shard_map/all_gather | solution.py:428
  103.5 1.8 %shard_map.92 = (bf16[8,64,512]{2,1,0:T(8,128)(2,1)}, f32[8,128]{1,0:T(8,128)S(1)}) custom-call(bf16[4,256,384]{2,1,0:T(8,128)(2,1)S(1)} %bitcast.8, bf16[1536,1024]{1,0:T(8,128)(2,1)S(1)} %get-tuple-element.32.down_ref, f32[8,128]{1,0:T(8,128)S(1)} %get-tuple-element.33.peak_in), custom_call_target="tpu_custom_call" | custom-call | tf_op jit(solution)/shard_map/pallas_call | solution.py:77
  105.3 3.5 %all-to-all-start.2 = ((bf16[8,64,512]{2,1,0:T(8,128)(2,1)}), bf16[8,64,512]{2,1,0:T(8,128)(2,1)S(1)}, u32[]{:S(2)}, u32[]{:S(2)}) async-start(bf16[8,64,512]{2,1,0:T(8,128)(2,1)} %get-tuple-element.34), calls=%async_computation.2 | async-start | bytes 1048576 | tf_op jit(solution)/shard_map/all_to_all | solution.py:436
  108.8 2.3 %collective-permute-start.12 = (f32[8,128]{1,0:T(8,128)S(1)}, f32[8,128]{1,0:T(8,128)S(1)}, u32[]{:S(2)}, u32[]{:S(2)}) collective-permute-start(f32[8,128]{1,0:T(8,128)S(1)} %get-tuple-element.35), channel_id=1, source_target_pairs={{0,1},{1,0},{2,3},{3,2},{4,5},{5,4},{6,7},{7,6},{8,9},{9,8},{10,11... | collective-permute-start | bytes 12296 | tf_op jit(solution)/shard_map/ppermute | solution.py:376
  111.1 0.5 shard_map.86
  111.6 0.3 collective-permute-done.12
  111.9 0.5 slice_bitcast_fusion
  112.5 6.6 %all-to-all-done.2.row_ref = bf16[8,64,512]{2,1,0:T(8,128)(2,1)S(1)} async-done(((bf16[8,64,512]{2,1,0:T(8,128)(2,1)}), bf16[8,64,512]{2,1,0:T(8,128)(2,1)S(1)}, u32[]{:S(2)}, u32[]{:S(2)}) %all-to-all-start.2) | async-done | bytes 524320 | tf_op jit(solution)/shard_map/all_to_all | solution.py:436
  119.1 0.4 shard_map.93
  119.5 13.1 %all_to_all.26.part_ref = bf16[4,4,16,512]{3,2,1,0:T(8,128)(2,1)S(1)} all-to-all(bf16[4,4,16,512]{3,2,1,0:T(8,128)(2,1)S(1)} %shard_map.93), channel_id=1, replica_groups=mesh['x'=4,'zhigh'=4,'zlow'=4,'chip'=4,'core'=2] {'zlow'}, dimensions={0} | all-to-all | bytes 524288 | tf_op jit(solution)/shard_map/all_to_all | solution.py:445
  132.6 22.6 %all_to_all.27.part_ref = bf16[4,16,512]{2,1,0:T(8,128)(2,1)S(1)} all-to-all(bf16[4,16,512]{2,1,0:T(8,128)(2,1)S(1)} %shard_map.94), channel_id=1, replica_groups=mesh['x'=4,'zhigh'=4,'zlow'=4,'chip'=4,'core'=2] {'zhigh'}, dimensions={0} | all-to-all | bytes 131072 | tf_op jit(solution)/shard_map/all_to_all | solution.py:447
  155.2 0.6 shard_map.95
  (3 shorter events, 0.1 us)
Async XLA Ops:
  0.6 30.4 %copy-start.2 = (bf16[1,192,4096]{2,1,0:T(8,128)(2,1)S(1)}, bf16[1,192,4096]{2,1,0:T(8,128)(2,1)}, u32[]{:S(2)}) copy-start(bf16[1,192,4096]{2,1,0:T(8,128)(2,1)} %param.10) | copy-start | bytes 4718596
  2.4 45.9 %all-to-all-start = ((bf16[16,72,128]{2,1,0:T(8,128)(2,1)}), bf16[16,72,128]{2,1,0:T(8,128)(2,1)S(1)}, u32[]{:S(2)}, u32[]{:S(2)}) async-start(bf16[16,72,128]{2,1,0:T(8,128)(2,1)} %pack_tokens.1), calls=%async_computation | async-start | bytes 589824 | tf_op jit(solution)/shard_map/all_to_all | solution.py:385
  20.3 0.7 copy-start.1
  21.0 15.4 %collective-permute-start.10 = (bf16[192,1024]{1,0:T(8,128)(2,1)S(1)}, bf16[192,1024]{1,0:T(8,128)(2,1)S(1)}, u32[]{:S(2)}, u32[]{:S(2)}) collective-permute-start(bf16[192,1024]{1,0:T(8,128)(2,1)S(1)} %get-tuple-element.27), channel_id=1, source_target_pairs={{0,4},{2,6},{4,0},{6,2},{1,5},{3,7},{5,1},{7,3},{8,12},{10,14},{12... | collective-permute-start | bytes 1179656 | tf_op jit(solution)/shard_map/ppermute | solution.py:373
  25.2 18.3 %collective-permute-start.8 = (bf16[192,1024]{1,0:T(8,128)(2,1)S(1)}, bf16[192,1024]{1,0:T(8,128)(2,1)S(1)}, u32[]{:S(2)}, u32[]{:S(2)}) collective-permute-start(bf16[192,1024]{1,0:T(8,128)(2,1)S(1)} %get-tuple-element.25), channel_id=1, source_target_pairs={{0,2},{2,4},{4,6},{6,0},{1,3},{3,5},{5,7},{7,1},{8,10},{10,12},{12... | collective-permute-start | bytes 1179656 | tf_op jit(solution)/shard_map/ppermute | solution.py:373
  27.1 16.4 %collective-permute-start.9 = (bf16[192,1024]{1,0:T(8,128)(2,1)S(1)}, bf16[192,1024]{1,0:T(8,128)(2,1)S(1)}, u32[]{:S(2)}, u32[]{:S(2)}) collective-permute-start(bf16[192,1024]{1,0:T(8,128)(2,1)S(1)} %get-tuple-element.26), channel_id=1, source_target_pairs={{0,6},{2,0},{4,2},{6,4},{1,7},{3,1},{5,3},{7,5},{8,14},{10,8},{12,... | collective-permute-start | bytes 1179656 | tf_op jit(solution)/shard_map/ppermute | solution.py:373
  31.1 38.2 %collective-permute-start.6 = (bf16[192,4096]{1,0:T(8,128)(2,1)S(1)}, bf16[192,4096]{1,0:T(8,128)(2,1)}, u32[]{:S(2)}, u32[]{:S(2)}) collective-permute-start(bf16[192,4096]{1,0:T(8,128)(2,1)S(1)} %bitcast.11), channel_id=1, source_target_pairs={{0,1},{1,0},{2,3},{3,2},{4,5},{5,4},{6,7},{7,6},{8,9},{9,8},{10,11... | collective-permute-start | bytes 4718600 | tf_op jit(solution)/shard_map/ppermute | solution.py:376
  33.0 39.6 %collective-permute-start.7 = (bf16[192,4096]{1,0:T(8,128)(2,1)}, bf16[192,4096]{1,0:T(8,128)(2,1)}, u32[]{:S(2)}, u32[]{:S(2)}) collective-permute-start(bf16[192,4096]{1,0:T(8,128)(2,1)} %bitcast.12), channel_id=1, source_target_pairs={{0,1},{1,0},{2,3},{3,2},{4,5},{5,4},{6,7},{7,6},{8,9},{9,8},{10,11... | collective-permute-start | bytes 4718600 | tf_op jit(solution)/shard_map/ppermute | solution.py:376
  36.4 7.1 %copy-start.3 = (bf16[192,1024]{1,0:T(8,128)(2,1)}, bf16[192,1024]{1,0:T(8,128)(2,1)S(1)}, u32[]{:S(2)}) copy-start(bf16[192,1024]{1,0:T(8,128)(2,1)S(1)} %collective-permute-done.10.refs_3_) | copy-start | bytes 1179652
  43.6 0.7 copy-start.4
  43.6 0.9 copy-start.5
  46.4 35.9 %copy-start = (bf16[4,192,1024]{2,1,0:T(8,128)(2,1)}, bf16[4,192,1024]{2,1,0:T(8,128)(2,1)S(1)}, u32[]{:S(2)}) copy-start(bf16[4,192,1024]{2,1,0:T(8,128)(2,1)S(1)} %shard_map.90.refs_10_) | copy-start | bytes 4718596
  46.4 35.9 %collective-permute-start.11 = (bf16[4,192,1024]{2,1,0:T(8,128)(2,1)S(1)}, bf16[4,192,1024]{2,1,0:T(8,128)(2,1)}, u32[]{:S(2)}, u32[]{:S(2)}) collective-permute-start(bf16[4,192,1024]{2,1,0:T(8,128)(2,1)S(1)} %shard_map.90.refs_10_), channel_id=1, source_target_pairs={{0,1},{1,0},{2,3},{3,2},{4,5},{5,4},{6,7},{7,6},{8,9},{9,8},{10,11... | collective-permute-start | bytes 4718600 | tf_op jit(solution)/shard_map/ppermute | solution.py:376
  63.4 11.7 %collective-permute-start = (bf16[128,1024]{1,0:T(8,128)(2,1)S(1)}, bf16[128,1024]{1,0:T(8,128)(2,1)S(1)}, u32[]{:S(2)}, u32[]{:S(2)}) collective-permute-start(bf16[128,1024]{1,0:T(8,128)(2,1)S(1)} %get-tuple-element.22.refs_0_), channel_id=1, source_target_pairs={{0,2},{2,4},{4,6},{6,0},{1,3},{3,5},{5,7},{7,1},{8,10},{10,12},{12... | collective-permute-start | bytes 786440 | tf_op jit(solution)/shard_map/ppermute | solution.py:373
  66.8 11.8 %collective-permute-start.2 = (bf16[128,1024]{1,0:T(8,128)(2,1)S(1)}, bf16[128,1024]{1,0:T(8,128)(2,1)S(1)}, u32[]{:S(2)}, u32[]{:S(2)}) collective-permute-start(bf16[128,1024]{1,0:T(8,128)(2,1)S(1)} %get-tuple-element.23.refs_1_), channel_id=1, source_target_pairs={{0,6},{2,0},{4,2},{6,4},{1,7},{3,1},{5,3},{7,5},{8,14},{10,8},{12,... | collective-permute-start | bytes 786440 | tf_op jit(solution)/shard_map/ppermute | solution.py:373
  69.3 12.7 %collective-permute-start.4 = (bf16[128,1024]{1,0:T(8,128)(2,1)S(1)}, bf16[128,1024]{1,0:T(8,128)(2,1)S(1)}, u32[]{:S(2)}, u32[]{:S(2)}) collective-permute-start(bf16[128,1024]{1,0:T(8,128)(2,1)S(1)} %get-tuple-element.23.refs_1_), channel_id=1, source_target_pairs={{0,2},{2,4},{4,6},{6,0},{1,3},{3,5},{5,7},{7,1},{8,10},{10,12},{12... | collective-permute-start | bytes 786440 | tf_op jit(solution)/shard_map/ppermute | solution.py:373
  72.6 9.6 %collective-permute-start.5 = (bf16[128,1024]{1,0:T(8,128)(2,1)S(1)}, bf16[128,1024]{1,0:T(8,128)(2,1)S(1)}, u32[]{:S(2)}, u32[]{:S(2)}) collective-permute-start(bf16[128,1024]{1,0:T(8,128)(2,1)S(1)} %get-tuple-element.22.refs_0_), channel_id=1, source_target_pairs={{0,6},{2,0},{4,2},{6,4},{1,7},{3,1},{5,3},{7,5},{8,14},{10,8},{12,... | collective-permute-start | bytes 786440 | tf_op jit(solution)/shard_map/ppermute | solution.py:373
  75.2 11.7 %collective-permute-start.1 = (bf16[128,1024]{1,0:T(8,128)(2,1)S(1)}, bf16[128,1024]{1,0:T(8,128)(2,1)S(1)}, u32[]{:S(2)}, u32[]{:S(2)}) collective-permute-start(bf16[128,1024]{1,0:T(8,128)(2,1)S(1)} %collective-permute-done.refs_2_), channel_id=1, source_target_pairs={{0,2},{2,4},{4,6},{6,0},{1,3},{3,5},{5,7},{7,1},{8,10},{10,12},{12... | collective-permute-start | bytes 786440 | tf_op jit(solution)/shard_map/ppermute | solution.py:373
  78.5 8.8 %collective-permute-start.3 = (bf16[128,1024]{1,0:T(8,128)(2,1)S(1)}, bf16[128,1024]{1,0:T(8,128)(2,1)S(1)}, u32[]{:S(2)}, u32[]{:S(2)}) collective-permute-start(bf16[128,1024]{1,0:T(8,128)(2,1)S(1)} %collective-permute-done.2.refs_5_), channel_id=1, source_target_pairs={{0,6},{2,0},{4,2},{6,4},{1,7},{3,1},{5,3},{7,5},{8,14},{10,8},{12,... | collective-permute-start | bytes 786440 | tf_op jit(solution)/shard_map/ppermute | solution.py:373
  105.3 13.7 %all-to-all-start.2 = ((bf16[8,64,512]{2,1,0:T(8,128)(2,1)}), bf16[8,64,512]{2,1,0:T(8,128)(2,1)S(1)}, u32[]{:S(2)}, u32[]{:S(2)}) async-start(bf16[8,64,512]{2,1,0:T(8,128)(2,1)} %get-tuple-element.34), calls=%async_computation.2 | async-start | bytes 1048576 | tf_op jit(solution)/shard_map/all_to_all | solution.py:436
  108.8 3.1 %collective-permute-start.12 = (f32[8,128]{1,0:T(8,128)S(1)}, f32[8,128]{1,0:T(8,128)S(1)}, u32[]{:S(2)}, u32[]{:S(2)}) collective-permute-start(f32[8,128]{1,0:T(8,128)S(1)} %get-tuple-element.35), channel_id=1, source_target_pairs={{0,1},{1,0},{2,3},{3,2},{4,5},{5,4},{6,7},{7,6},{8,9},{9,8},{10,11... | collective-permute-start | bytes 12296 | tf_op jit(solution)/shard_map/ppermute | solution.py:376

commit v3 on v1

--- a/solution.py
+++ b/solution.py
@@ -231,7 +231,8 @@
                     source.at[chip], down_ref.at[rows, :], sems.at[chips + place, chip]
                 )
             )
-    for copy in [copy for group in fetched for copy in group] + handed:
+    stages = fetched + [handed]
+    for copy in stages[0] + stages[1]:
         copy.start()
     peak = None
     total = None
@@ -239,15 +240,17 @@
         x_ref[number, pl.ds(0, half), :] = pieces[2 * number][...]
         x_ref[number, pl.ds(half, half), :] = pieces[2 * number + 1][...]
         x = x_ref[number]
-        for copy in fetched[number]:
+        for copy in stages[number]:
             copy.wait()
+        for copy in stages[number + 2]:
+            copy.start()
         value = dot_nt(x, w_ref[number])
         total = value if total is None else total + value
         high = jnp.max(jnp.abs(x).astype(F32), axis=0, keepdims=True)
         peak = high if peak is None else jnp.maximum(peak, high)
     acc_ref[...] = total
     peak_ref[...] = peak
-    for copy in fetched[3] + handed:
+    for copy in stages[3] + stages[4]:
         copy.wait()
 
 
@@ -362,16 +365,15 @@
     kept = X * planes * SLOTS // CORES
     shaped = jax.ShapeDtypeStruct
 
-    def shift(array, step):
-        return lax.ppermute(array, "chip", [(j, (j + step) % chips) for j in range(chips)])
+    def swap(array, mask):
+        return lax.ppermute(array, "chip", [(j, j ^ mask) for j in range(chips)])
 
     def partner(array):
         return lax.ppermute(array, "core", [(j, 1 - j) for j in range(CORES)])
 
     lane = jnp.arange(8, dtype=jnp.int32)
-    turns = jnp.array([0, chips - 1, 1, 2, 0, 0, 0, 0], jnp.int32)
     order = jnp.where(
-        lane < 4, (place + turns) % chips, jnp.where(lane == 4, core, lax.axis_index("z"))
+        lane < 2, place ^ lane, jnp.where(lane < 4, place ^ (5 - lane), core)
     ).astype(jnp.int32)
 
     packed = pack_tokens(expert_ids.T, route_weight.T, tokens, planes)
@@ -380,7 +382,7 @@
     gate_other = partner(gate_weight[0])
     up_other = partner(up_weight[0])
     cuts = move(cut_kernel, order, (down_weight[0],), [shaped((unit, chunk), BF)] * chips, chips)
-    pieces = [cuts[0], shift(cuts[2], 1), shift(cuts[1], -1), shift(cuts[3], 2)]
+    pieces = [cuts[0], swap(cuts[1], 1), swap(cuts[2], 3), swap(cuts[3], 2)]
     sent = call(
         pick_kernel,
         None,
@@ -402,12 +404,14 @@
     )
 
     top, bottom = call(join_kernel, None, (local(received),), [shaped((kept // 2, chunk), BF)] * 2)
-    left_top, right_low = shift(top, 1), shift(bottom, -1)
-    left_low, right_top = shift(bottom, 1), shift(top, -1)
-    far_top, far_low = shift(left_top, 1), shift(right_low, -1)
+    cross_top = swap(top, 3)
+    beside_low = swap(bottom, 1)
+    cross_low = swap(bottom, 3)
+    beside_top = swap(top, 1)
+    far_top, far_low = swap(cross_top, 1), swap(beside_low, 3)
     acc, peak, last, down = near_chunks(
         order,
-        (top, bottom, left_top, left_low, right_top, right_low),
+        (top, bottom, beside_top, beside_low, cross_top, cross_low),
         (gate_weight[0], gate_other, up_weight[0], up_other),
         (stacked, stacked_other),
     )

time: 151 us -> 151 us (level)
  waiting for transfers between devices: 12.9 us -> 17.8 us
  starting transfers between devices: 60.6 us -> 56 us
    ppermute x9, waiting for transfers between devices: 5.92 us -> 10.8 us  [swap(): return lax.ppermute(array, 'chip', [(j, j ^ mask) for j in range(chips)])]
    ppermute x9, starting transfers between devices: 33.3 us -> 28.7 us  [swap(): return lax.ppermute(array, 'chip', [(j, j ^ mask) for j in range(chips)])]
  transfers between devices with their start and end apart: 15 -> 15, of which waited for: 4 -> 7; matrix products, arithmetic and copies ran while one was open for 1% -> 0% of each run, Pallas kernels for 6% -> 7%
where the time goes in v3:
time: 151 us; the launch traced here: 150 us
  blocking collectives  57.7 us (38%)
  starting transfers between devices  56 us (37%)
  waiting for transfers between devices  17.8 us (12%)
  Pallas kernels  15.9 us (11%)
  local copies, waits for them, and re-layouts  2.14 us (1%)
    all_to_all x1, blocking collectives, layer(): parts = lax.all_to_all(sums, 'z', split_axis=0, concat_axis=0, tiled=True)  29.7 us
    ppermute x9, starting transfers between devices, swap(): return lax.ppermute(array, 'chip', [(j, j ^ mask) for j in range(chips)])  28.7 us
    all_to_all x1, starting transfers between devices, layer(): lax.all_to_all(packed, 'z', split_axis=0, concat_axis=0, tiled=True)  15.2 us
    all_to_all x1, blocking collectives, layer(): lax.all_to_all(sent, ('x', 'core'), split_axis=0, concat_axis=0, tiled=True)  14.6 us
    all_gather x1, blocking collectives, layer(): gathered = lax.all_gather(hidden, 'chip', axis=0)  13.5 us
    ppermute x9, waiting for transfers between devices, swap(): return lax.ppermute(array, 'chip', [(j, j ^ mask) for j in range(chips)])  10.8 us
    ppermute x4, starting transfers between devices, partner(): return lax.ppermute(array, 'core', [(j, 1 - j) for j in range(CORES)])  8.55 us
    all_to_all x1, waiting for transfers between devices, layer(): lax.all_to_all(outputs, ('x', 'core'), split_axis=0, concat_axis=0, tiled...  6.61 us
  transfers between devices with their start and end apart: 15, of which 7 were waited for; matrix products, arithmetic and copies ran while one was open for 0% of the time, Pallas kernels for 7%

profile of v3, /device:TPU:32, one launch (start us, length us, event | category | flops | bytes accessed | tf_op | source)
XLA Modules:
  0.0 150.5 jit_solution(1396081753201584072)
XLA Ops:
  0.6 0.0 copy-start.2
  0.6 1.8 %pack_tokens.1 = bf16[16,72,128]{2,1,0:T(8,128)(2,1)} custom-call(s32[8,16]{1,0:T(8,128)} %bitcast.14, f32[8,16]{1,0:T(8,128)} %bitcast.15, bf16[16,512]{1,0:T(8,128)(2,1)} %tok_hbm.1), custom_call_target="tpu_custom_call" | custom-call | tf_op jit(solution)/shard_map/pack_tokens/pallas_call | solution.py:109
  2.4 15.2 %all-to-all-start = ((bf16[16,72,128]{2,1,0:T(8,128)(2,1)}), bf16[16,72,128]{2,1,0:T(8,128)(2,1)S(1)}, u32[]{:S(2)}, u32[]{:S(2)}) async-start(bf16[16,72,128]{2,1,0:T(8,128)(2,1)} %pack_tokens.1), calls=%async_computation | async-start | bytes 589824 | tf_op jit(solution)/shard_map/all_to_all | solution.py:380
  17.7 1.9 %shard_map.80 = (bf16[192,1024]{1,0:T(8,128)(2,1)S(1)}, bf16[192,1024]{1,0:T(8,128)(2,1)S(1)}, bf16[192,1024]{1,0:T(8,128)(2,1)S(1)}, bf16[192,1024]{1,0:T(8,128)(2,1)S(1)}) custom-call(s32[8]{0:T(128)S(1)} %compare_select_fusion.1.order_ref, bf16[192,4096]{1,0:T(8,128)(2,1)} %bitcast.9), custom_call_target="tpu_custom_call" | custom-call | tf_op jit(solution)/shard_map/pallas_call | solution.py:54
  19.6 0.0 copy-start.1
  19.6 0.7 copy-done.1
  20.4 5.1 %collective-permute-start.10 = (bf16[192,1024]{1,0:T(8,128)(2,1)S(1)}, bf16[192,1024]{1,0:T(8,128)(2,1)S(1)}, u32[]{:S(2)}, u32[]{:S(2)}) collective-permute-start(bf16[192,1024]{1,0:T(8,128)(2,1)S(1)} %get-tuple-element.27), channel_id=1, source_target_pairs={{0,4},{2,6},{4,0},{6,2},{1,5},{3,7},{5,1},{7,3},{8,12},{10,14},{12... | collective-permute-start | bytes 1179656 | tf_op jit(solution)/shard_map/ppermute | solution.py:369
  25.4 2.6 %collective-permute-start.8 = (bf16[192,1024]{1,0:T(8,128)(2,1)S(1)}, bf16[192,1024]{1,0:T(8,128)(2,1)S(1)}, u32[]{:S(2)}, u32[]{:S(2)}) collective-permute-start(bf16[192,1024]{1,0:T(8,128)(2,1)S(1)} %get-tuple-element.25), channel_id=1, source_target_pairs={{0,2},{2,0},{4,6},{6,4},{1,3},{3,1},{5,7},{7,5},{8,10},{10,8},{12,... | collective-permute-start | bytes 1179656 | tf_op jit(solution)/shard_map/ppermute | solution.py:369
  28.0 2.3 %collective-permute-start.9 = (bf16[192,1024]{1,0:T(8,128)(2,1)S(1)}, bf16[192,1024]{1,0:T(8,128)(2,1)S(1)}, u32[]{:S(2)}, u32[]{:S(2)}) collective-permute-start(bf16[192,1024]{1,0:T(8,128)(2,1)S(1)} %get-tuple-element.26), channel_id=1, source_target_pairs={{0,6},{2,4},{4,2},{6,0},{1,7},{3,5},{5,3},{7,1},{8,14},{10,12},{12... | collective-permute-start | bytes 1179656 | tf_op jit(solution)/shard_map/ppermute | solution.py:369
  30.3 0.0 copy-done.2
  30.4 1.9 %collective-permute-start.6 = (bf16[192,4096]{1,0:T(8,128)(2,1)S(1)}, bf16[192,4096]{1,0:T(8,128)(2,1)}, u32[]{:S(2)}, u32[]{:S(2)}) collective-permute-start(bf16[192,4096]{1,0:T(8,128)(2,1)S(1)} %bitcast.11), channel_id=1, source_target_pairs={{0,1},{1,0},{2,3},{3,2},{4,5},{5,4},{6,7},{7,6},{8,9},{9,8},{10,11... | collective-permute-start | bytes 4718600 | tf_op jit(solution)/shard_map/ppermute | solution.py:372
  32.3 2.4 %collective-permute-start.7 = (bf16[192,4096]{1,0:T(8,128)(2,1)}, bf16[192,4096]{1,0:T(8,128)(2,1)}, u32[]{:S(2)}, u32[]{:S(2)}) collective-permute-start(bf16[192,4096]{1,0:T(8,128)(2,1)} %bitcast.12), channel_id=1, source_target_pairs={{0,1},{1,0},{2,3},{3,2},{4,5},{5,4},{6,7},{7,6},{8,9},{9,8},{10,11... | collective-permute-start | bytes 4718600 | tf_op jit(solution)/shard_map/ppermute | solution.py:372
  34.7 1.0 collective-permute-done.10.refs_3_
  35.7 0.0 copy-start.3
  35.7 7.1 %collective-permute-done.8.refs_1_ = bf16[192,1024]{1,0:T(8,128)(2,1)S(1)} collective-permute-done((bf16[192,1024]{1,0:T(8,128)(2,1)S(1)}, bf16[192,1024]{1,0:T(8,128)(2,1)S(1)}, u32[]{:S(2)}, u32[]{:S(2)}) %collective-permute-start.8) | collective-permute-done | bytes 393248 | tf_op jit(solution)/shard_map/ppermute | solution.py:369
  42.8 0.0 copy-start.4
  42.8 0.0 collective-permute-done.9.refs_2_
  42.8 0.0 copy-start.5
  42.9 0.0 copy-done.3
  42.9 0.7 copy-done.4
  43.6 0.2 copy-done.5
  43.7 1.9 %shard_map.81.refs_10_ = bf16[4,192,1024]{2,1,0:T(8,128)(2,1)S(1)} custom-call(s32[8]{0:T(128)S(1)} %compare_select_fusion.1.order_ref, bf16[192,1024]{1,0:T(8,128)(2,1)} %copy-done.1, bf16[192,1024]{1,0:T(8,128)(2,1)} %copy-done.4, bf16[192,1024]{1,0:T(8,128)(2,1)} %copy-done.5, bf16[192,1024]{1,0:T(8,128)(2,1)} %copy-done.3), custom_call_target="tpu_custom_call" | custom-call | tf_op jit(solution)/shard_map/pallas_call | solution.py:54
  45.7 0.0 copy-start
  45.7 1.9 %collective-permute-start.11 = (bf16[4,192,1024]{2,1,0:T(8,128)(2,1)S(1)}, bf16[4,192,1024]{2,1,0:T(8,128)(2,1)}, u32[]{:S(2)}, u32[]{:S(2)}) collective-permute-start(bf16[4,192,1024]{2,1,0:T(8,128)(2,1)S(1)} %shard_map.81.refs_10_), channel_id=1, source_target_pairs={{0,1},{1,0},{2,3},{3,2},{4,5},{5,4},{6,7},{7,6},{8,9},{9,8},{10,11... | collective-permute-start | bytes 4718600 | tf_op jit(solution)/shard_map/ppermute | solution.py:372
  47.6 0.0 all-to-all-done.got_ref
  47.6 0.5 shard_map.78
  48.1 14.6 %all_to_all.20.got_ref = bf16[8,64,512]{2,1,0:T(8,128)(2,1)S(1)} all-to-all(bf16[8,64,512]{2,1,0:T(8,128)(2,1)S(1)} %shard_map.78), channel_id=1, replica_groups=mesh['x'=4,'z'=16,'chip'=4,'core'=2] {'x','core'}, dimensions={0} | all-to-all | bytes 1048576 | tf_op jit(solution)/shard_map/all_to_all | solution.py:396
  62.7 4.4 %collective-permute-start = (bf16[128,1024]{1,0:T(8,128)(2,1)S(1)}, bf16[128,1024]{1,0:T(8,128)(2,1)S(1)}, u32[]{:S(2)}, u32[]{:S(2)}) collective-permute-start(bf16[128,1024]{1,0:T(8,128)(2,1)S(1)} %get-tuple-element.22.refs_0_), channel_id=1, source_target_pairs={{0,6},{2,4},{4,2},{6,0},{1,7},{3,5},{5,3},{7,1},{8,14},{10,12},{12... | collective-permute-start | bytes 786440 | tf_op jit(solution)/shard_map/ppermute | solution.py:369
  67.1 2.0 %collective-permute-start.2 = (bf16[128,1024]{1,0:T(8,128)(2,1)S(1)}, bf16[128,1024]{1,0:T(8,128)(2,1)S(1)}, u32[]{:S(2)}, u32[]{:S(2)}) collective-permute-start(bf16[128,1024]{1,0:T(8,128)(2,1)S(1)} %get-tuple-element.23.refs_1_), channel_id=1, source_target_pairs={{0,2},{2,0},{4,6},{6,4},{1,3},{3,1},{5,7},{7,5},{8,10},{10,8},{12,... | collective-permute-start | bytes 786440 | tf_op jit(solution)/shard_map/ppermute | solution.py:369
  69.2 0.0 collective-permute-done.6.refs_7_
  69.2 3.8 %collective-permute-start.4 = (bf16[128,1024]{1,0:T(8,128)(2,1)S(1)}, bf16[128,1024]{1,0:T(8,128)(2,1)S(1)}, u32[]{:S(2)}, u32[]{:S(2)}) collective-permute-start(bf16[128,1024]{1,0:T(8,128)(2,1)S(1)} %get-tuple-element.22.refs_0_), channel_id=1, source_target_pairs={{0,2},{2,0},{4,6},{6,4},{1,3},{3,1},{5,7},{7,5},{8,10},{10,8},{12,... | collective-permute-start | bytes 786440 | tf_op jit(solution)/shard_map/ppermute | solution.py:369
  73.0 0.0 collective-permute-done.7.refs_9_
  73.0 2.6 %collective-permute-start.5 = (bf16[128,1024]{1,0:T(8,128)(2,1)S(1)}, bf16[128,1024]{1,0:T(8,128)(2,1)S(1)}, u32[]{:S(2)}, u32[]{:S(2)}) collective-permute-start(bf16[128,1024]{1,0:T(8,128)(2,1)S(1)} %get-tuple-element.23.refs_1_), channel_id=1, source_target_pairs={{0,6},{2,4},{4,2},{6,0},{1,7},{3,5},{5,3},{7,1},{8,14},{10,12},{12... | collective-permute-start | bytes 786440 | tf_op jit(solution)/shard_map/ppermute | solution.py:369
  75.7 0.0 collective-permute-done.refs_4_
  75.7 2.0 %collective-permute-start.1 = (bf16[128,1024]{1,0:T(8,128)(2,1)S(1)}, bf16[128,1024]{1,0:T(8,128)(2,1)S(1)}, u32[]{:S(2)}, u32[]{:S(2)}) collective-permute-start(bf16[128,1024]{1,0:T(8,128)(2,1)S(1)} %collective-permute-done.refs_4_), channel_id=1, source_target_pairs={{0,2},{2,0},{4,6},{6,4},{1,3},{3,1},{5,7},{7,5},{8,10},{10,8},{12,... | collective-permute-start | bytes 786440 | tf_op jit(solution)/shard_map/ppermute | solution.py:369
  77.7 0.5 collective-permute-done.2.refs_3_
  78.2 3.8 %collective-permute-start.3 = (bf16[128,1024]{1,0:T(8,128)(2,1)S(1)}, bf16[128,1024]{1,0:T(8,128)(2,1)S(1)}, u32[]{:S(2)}, u32[]{:S(2)}) collective-permute-start(bf16[128,1024]{1,0:T(8,128)(2,1)S(1)} %collective-permute-done.2.refs_3_), channel_id=1, source_target_pairs={{0,6},{2,4},{4,2},{6,0},{1,7},{3,5},{5,3},{7,1},{8,14},{10,12},{12... | collective-permute-start | bytes 786440 | tf_op jit(solution)/shard_map/ppermute | solution.py:369
  82.0 1.8 %collective-permute-done.4.refs_2_ = bf16[128,1024]{1,0:T(8,128)(2,1)S(1)} collective-permute-done((bf16[128,1024]{1,0:T(8,128)(2,1)S(1)}, bf16[128,1024]{1,0:T(8,128)(2,1)S(1)}, u32[]{:S(2)}, u32[]{:S(2)}) %collective-permute-start.4) | collective-permute-done | bytes 262176 | tf_op jit(solution)/shard_map/ppermute | solution.py:369
  83.8 0.4 collective-permute-done.5.refs_5_
  84.3 0.0 collective-permute-done.11.refs_11_
  84.3 0.0 copy-done
  84.3 5.7 %near_chunks.1 = (f32[256,768]{1,0:T(8,128)S(1)}, f32[1,1024]{1,0:T(1,128)S(1)}, bf16[768,1024]{1,0:T(8,128)(2,1)S(1)}, bf16[1536,1024]{1,0:T(8,128)(2,1)S(1)}) custom-call(s32[8]{0:T(128)S(1)} %compare_select_fusion.1.order_ref, bf16[128,1024]{1,0:T(8,128)(2,1)S(1)} %get-tuple-element.22.refs_0_, bf16[128,1024]{1,0:T(8,128)(2,1)S(1)} %get-tuple-element.23.refs_1_, ...), custom_call_target="tpu_custom_call" | custom-call | flops 1207959552 | bytes 9437184 | tf_op jit(solution)/shard_map/near_chunks/pallas_call | solution.py:261
  90.0 0.0 collective-permute-done.1.top_ref
  90.0 0.0 collective-permute-done.3.low_ref
  90.0 0.7 shard_map.82
  90.7 13.5 %all-gather = bf16[1024,384]{1,0:T(8,128)(2,1)S(1)} all-gather(bf16[256,384]{1,0:T(8,128)(2,1)S(1)} %get-tuple-element.31), channel_id=2, replica_groups=mesh['x'=4,'z'=16,'chip'=4,'core'=2] {'chip'}, dimensions={0}, use_global_device_ids=true | all-gather | bytes 983040 | tf_op jit(solution)/shard_map/all_gather | solution.py:425
  104.1 1.8 %shard_map.83 = (bf16[8,64,512]{2,1,0:T(8,128)(2,1)}, f32[8,128]{1,0:T(8,128)S(1)}) custom-call(bf16[4,256,384]{2,1,0:T(8,128)(2,1)S(1)} %bitcast.8, bf16[1536,1024]{1,0:T(8,128)(2,1)S(1)} %get-tuple-element.32.down_ref, f32[8,128]{1,0:T(8,128)S(1)} %get-tuple-element.33.peak_in), custom_call_target="tpu_custom_call" | custom-call | tf_op jit(solution)/shard_map/pallas_call | solution.py:76
  106.0 3.5 %all-to-all-start.2 = ((bf16[8,64,512]{2,1,0:T(8,128)(2,1)}), bf16[8,64,512]{2,1,0:T(8,128)(2,1)S(1)}, u32[]{:S(2)}, u32[]{:S(2)}) async-start(bf16[8,64,512]{2,1,0:T(8,128)(2,1)} %get-tuple-element.34), calls=%async_computation.2 | async-start | bytes 1048576 | tf_op jit(solution)/shard_map/all_to_all | solution.py:433
  109.5 2.3 %collective-permute-start.12 = (f32[8,128]{1,0:T(8,128)S(1)}, f32[8,128]{1,0:T(8,128)S(1)}, u32[]{:S(2)}, u32[]{:S(2)}) collective-permute-start(f32[8,128]{1,0:T(8,128)S(1)} %get-tuple-element.35), channel_id=1, source_target_pairs={{0,1},{1,0},{2,3},{3,2},{4,5},{5,4},{6,7},{7,6},{8,9},{9,8},{10,11... | collective-permute-start | bytes 12296 | tf_op jit(solution)/shard_map/ppermute | solution.py:372
  111.8 0.5 shard_map.77
  112.2 0.3 collective-permute-done.12
  112.6 0.5 slice_bitcast_fusion
  113.1 6.6 %all-to-all-done.2.row_ref = bf16[8,64,512]{2,1,0:T(8,128)(2,1)S(1)} async-done(((bf16[8,64,512]{2,1,0:T(8,128)(2,1)}), bf16[8,64,512]{2,1,0:T(8,128)(2,1)S(1)}, u32[]{:S(2)}, u32[]{:S(2)}) %all-to-all-start.2) | async-done | bytes 524320 | tf_op jit(solution)/shard_map/all_to_all | solution.py:433
  119.7 0.4 shard_map.84
  120.2 29.7 %all_to_all.21.part_ref = bf16[16,16,512]{2,1,0:T(8,128)(2,1)S(1)} all-to-all(bf16[16,16,512]{2,1,0:T(8,128)(2,1)S(1)} %shard_map.84), channel_id=1, replica_groups=mesh['x'=4,'z'=16,'chip'=4,'core'=2] {'z'}, dimensions={0} | all-to-all | bytes 524288 | tf_op jit(solution)/shard_map/all_to_all | solution.py:442
  149.8 0.6 shard_map.85
  (3 shorter events, 0.0 us)
Async XLA Ops:
  0.6 29.7 %copy-start.2 = (bf16[1,192,4096]{2,1,0:T(8,128)(2,1)S(1)}, bf16[1,192,4096]{2,1,0:T(8,128)(2,1)}, u32[]{:S(2)}) copy-start(bf16[1,192,4096]{2,1,0:T(8,128)(2,1)} %param.9) | copy-start | bytes 4718596
  2.4 45.2 %all-to-all-start = ((bf16[16,72,128]{2,1,0:T(8,128)(2,1)}), bf16[16,72,128]{2,1,0:T(8,128)(2,1)S(1)}, u32[]{:S(2)}, u32[]{:S(2)}) async-start(bf16[16,72,128]{2,1,0:T(8,128)(2,1)} %pack_tokens.1), calls=%async_computation | async-start | bytes 589824 | tf_op jit(solution)/shard_map/all_to_all | solution.py:380
  19.6 0.7 copy-start.1
  20.4 15.4 %collective-permute-start.10 = (bf16[192,1024]{1,0:T(8,128)(2,1)S(1)}, bf16[192,1024]{1,0:T(8,128)(2,1)S(1)}, u32[]{:S(2)}, u32[]{:S(2)}) collective-permute-start(bf16[192,1024]{1,0:T(8,128)(2,1)S(1)} %get-tuple-element.27), channel_id=1, source_target_pairs={{0,4},{2,6},{4,0},{6,2},{1,5},{3,7},{5,1},{7,3},{8,12},{10,14},{12... | collective-permute-start | bytes 1179656 | tf_op jit(solution)/shard_map/ppermute | solution.py:369
  25.4 17.4 %collective-permute-start.8 = (bf16[192,1024]{1,0:T(8,128)(2,1)S(1)}, bf16[192,1024]{1,0:T(8,128)(2,1)S(1)}, u32[]{:S(2)}, u32[]{:S(2)}) collective-permute-start(bf16[192,1024]{1,0:T(8,128)(2,1)S(1)} %get-tuple-element.25), channel_id=1, source_target_pairs={{0,2},{2,0},{4,6},{6,4},{1,3},{3,1},{5,7},{7,5},{8,10},{10,8},{12,... | collective-permute-start | bytes 1179656 | tf_op jit(solution)/shard_map/ppermute | solution.py:369
  28.0 14.8 %collective-permute-start.9 = (bf16[192,1024]{1,0:T(8,128)(2,1)S(1)}, bf16[192,1024]{1,0:T(8,128)(2,1)S(1)}, u32[]{:S(2)}, u32[]{:S(2)}) collective-permute-start(bf16[192,1024]{1,0:T(8,128)(2,1)S(1)} %get-tuple-element.26), channel_id=1, source_target_pairs={{0,6},{2,4},{4,2},{6,0},{1,7},{3,5},{5,3},{7,1},{8,14},{10,12},{12... | collective-permute-start | bytes 1179656 | tf_op jit(solution)/shard_map/ppermute | solution.py:369
  30.4 38.8 %collective-permute-start.6 = (bf16[192,4096]{1,0:T(8,128)(2,1)S(1)}, bf16[192,4096]{1,0:T(8,128)(2,1)}, u32[]{:S(2)}, u32[]{:S(2)}) collective-permute-start(bf16[192,4096]{1,0:T(8,128)(2,1)S(1)} %bitcast.11), channel_id=1, source_target_pairs={{0,1},{1,0},{2,3},{3,2},{4,5},{5,4},{6,7},{7,6},{8,9},{9,8},{10,11... | collective-permute-start | bytes 4718600 | tf_op jit(solution)/shard_map/ppermute | solution.py:372
  32.3 40.7 %collective-permute-start.7 = (bf16[192,4096]{1,0:T(8,128)(2,1)}, bf16[192,4096]{1,0:T(8,128)(2,1)}, u32[]{:S(2)}, u32[]{:S(2)}) collective-permute-start(bf16[192,4096]{1,0:T(8,128)(2,1)} %bitcast.12), channel_id=1, source_target_pairs={{0,1},{1,0},{2,3},{3,2},{4,5},{5,4},{6,7},{7,6},{8,9},{9,8},{10,11... | collective-permute-start | bytes 4718600 | tf_op jit(solution)/shard_map/ppermute | solution.py:372
  35.7 7.1 %copy-start.3 = (bf16[192,1024]{1,0:T(8,128)(2,1)}, bf16[192,1024]{1,0:T(8,128)(2,1)S(1)}, u32[]{:S(2)}) copy-start(bf16[192,1024]{1,0:T(8,128)(2,1)S(1)} %collective-permute-done.10.refs_3_) | copy-start | bytes 1179652
  42.8 0.7 copy-start.4
  42.8 0.9 copy-start.5
  45.7 38.6 %copy-start = (bf16[4,192,1024]{2,1,0:T(8,128)(2,1)}, bf16[4,192,1024]{2,1,0:T(8,128)(2,1)S(1)}, u32[]{:S(2)}) copy-start(bf16[4,192,1024]{2,1,0:T(8,128)(2,1)S(1)} %shard_map.81.refs_10_) | copy-start | bytes 4718596
  45.7 38.6 %collective-permute-start.11 = (bf16[4,192,1024]{2,1,0:T(8,128)(2,1)S(1)}, bf16[4,192,1024]{2,1,0:T(8,128)(2,1)}, u32[]{:S(2)}, u32[]{:S(2)}) collective-permute-start(bf16[4,192,1024]{2,1,0:T(8,128)(2,1)S(1)} %shard_map.81.refs_10_), channel_id=1, source_target_pairs={{0,1},{1,0},{2,3},{3,2},{4,5},{5,4},{6,7},{7,6},{8,9},{9,8},{10,11... | collective-permute-start | bytes 4718600 | tf_op jit(solution)/shard_map/ppermute | solution.py:372
  62.7 13.0 %collective-permute-start = (bf16[128,1024]{1,0:T(8,128)(2,1)S(1)}, bf16[128,1024]{1,0:T(8,128)(2,1)S(1)}, u32[]{:S(2)}, u32[]{:S(2)}) collective-permute-start(bf16[128,1024]{1,0:T(8,128)(2,1)S(1)} %get-tuple-element.22.refs_0_), channel_id=1, source_target_pairs={{0,6},{2,4},{4,2},{6,0},{1,7},{3,5},{5,3},{7,1},{8,14},{10,12},{12... | collective-permute-start | bytes 786440 | tf_op jit(solution)/shard_map/ppermute | solution.py:369
  67.1 11.1 %collective-permute-start.2 = (bf16[128,1024]{1,0:T(8,128)(2,1)S(1)}, bf16[128,1024]{1,0:T(8,128)(2,1)S(1)}, u32[]{:S(2)}, u32[]{:S(2)}) collective-permute-start(bf16[128,1024]{1,0:T(8,128)(2,1)S(1)} %get-tuple-element.23.refs_1_), channel_id=1, source_target_pairs={{0,2},{2,0},{4,6},{6,4},{1,3},{3,1},{5,7},{7,5},{8,10},{10,8},{12,... | collective-permute-start | bytes 786440 | tf_op jit(solution)/shard_map/ppermute | solution.py:369
  69.2 14.6 %collective-permute-start.4 = (bf16[128,1024]{1,0:T(8,128)(2,1)S(1)}, bf16[128,1024]{1,0:T(8,128)(2,1)S(1)}, u32[]{:S(2)}, u32[]{:S(2)}) collective-permute-start(bf16[128,1024]{1,0:T(8,128)(2,1)S(1)} %get-tuple-element.22.refs_0_), channel_id=1, source_target_pairs={{0,2},{2,0},{4,6},{6,4},{1,3},{3,1},{5,7},{7,5},{8,10},{10,8},{12,... | collective-permute-start | bytes 786440 | tf_op jit(solution)/shard_map/ppermute | solution.py:369
  73.0 11.2 %collective-permute-start.5 = (bf16[128,1024]{1,0:T(8,128)(2,1)S(1)}, bf16[128,1024]{1,0:T(8,128)(2,1)S(1)}, u32[]{:S(2)}, u32[]{:S(2)}) collective-permute-start(bf16[128,1024]{1,0:T(8,128)(2,1)S(1)} %get-tuple-element.23.refs_1_), channel_id=1, source_target_pairs={{0,6},{2,4},{4,2},{6,0},{1,7},{3,5},{5,3},{7,1},{8,14},{10,12},{12... | collective-permute-start | bytes 786440 | tf_op jit(solution)/shard_map/ppermute | solution.py:369
  75.7 14.3 %collective-permute-start.1 = (bf16[128,1024]{1,0:T(8,128)(2,1)S(1)}, bf16[128,1024]{1,0:T(8,128)(2,1)S(1)}, u32[]{:S(2)}, u32[]{:S(2)}) collective-permute-start(bf16[128,1024]{1,0:T(8,128)(2,1)S(1)} %collective-permute-done.refs_4_), channel_id=1, source_target_pairs={{0,2},{2,0},{4,6},{6,4},{1,3},{3,1},{5,7},{7,5},{8,10},{10,8},{12,... | collective-permute-start | bytes 786440 | tf_op jit(solution)/shard_map/ppermute | solution.py:369
  78.2 11.8 %collective-permute-start.3 = (bf16[128,1024]{1,0:T(8,128)(2,1)S(1)}, bf16[128,1024]{1,0:T(8,128)(2,1)S(1)}, u32[]{:S(2)}, u32[]{:S(2)}) collective-permute-start(bf16[128,1024]{1,0:T(8,128)(2,1)S(1)} %collective-permute-done.2.refs_3_), channel_id=1, source_target_pairs={{0,6},{2,4},{4,2},{6,0},{1,7},{3,5},{5,3},{7,1},{8,14},{10,12},{12... | collective-permute-start | bytes 786440 | tf_op jit(solution)/shard_map/ppermute | solution.py:369
  106.0 13.7 %all-to-all-start.2 = ((bf16[8,64,512]{2,1,0:T(8,128)(2,1)}), bf16[8,64,512]{2,1,0:T(8,128)(2,1)S(1)}, u32[]{:S(2)}, u32[]{:S(2)}) async-start(bf16[8,64,512]{2,1,0:T(8,128)(2,1)} %get-tuple-element.34), calls=%async_computation.2 | async-start | bytes 1048576 | tf_op jit(solution)/shard_map/all_to_all | solution.py:433
  109.5 3.1 %collective-permute-start.12 = (f32[8,128]{1,0:T(8,128)S(1)}, f32[8,128]{1,0:T(8,128)S(1)}, u32[]{:S(2)}, u32[]{:S(2)}) collective-permute-start(f32[8,128]{1,0:T(8,128)S(1)} %get-tuple-element.35), channel_id=1, source_target_pairs={{0,1},{1,0},{2,3},{3,2},{4,5},{5,4},{6,7},{7,6},{8,9},{9,8},{10,11... | collective-permute-start | bytes 12296 | tf_op jit(solution)/shard_map/ppermute | solution.py:372

commit v4 on v3

--- a/solution.py
+++ b/solution.py
@@ -231,8 +231,7 @@
                     source.at[chip], down_ref.at[rows, :], sems.at[chips + place, chip]
                 )
             )
-    stages = fetched + [handed]
-    for copy in stages[0] + stages[1]:
+    for copy in [copy for group in fetched for copy in group] + handed:
         copy.start()
     peak = None
     total = None
@@ -240,17 +239,15 @@
         x_ref[number, pl.ds(0, half), :] = pieces[2 * number][...]
         x_ref[number, pl.ds(half, half), :] = pieces[2 * number + 1][...]
         x = x_ref[number]
-        for copy in stages[number]:
+        for copy in fetched[number]:
             copy.wait()
-        for copy in stages[number + 2]:
-            copy.start()
         value = dot_nt(x, w_ref[number])
         total = value if total is None else total + value
         high = jnp.max(jnp.abs(x).astype(F32), axis=0, keepdims=True)
         peak = high if peak is None else jnp.maximum(peak, high)
     acc_ref[...] = total
     peak_ref[...] = peak
-    for copy in stages[3] + stages[4]:
+    for copy in fetched[3] + handed:
         copy.wait()
 
 
@@ -406,9 +403,10 @@
     top, bottom = call(join_kernel, None, (local(received),), [shaped((kept // 2, chunk), BF)] * 2)
     cross_top = swap(top, 3)
     beside_low = swap(bottom, 1)
+    beside_top = swap(top, 1)
     cross_low = swap(bottom, 3)
-    beside_top = swap(top, 1)
-    far_top, far_low = swap(cross_top, 1), swap(beside_low, 3)
+    far_low = swap(beside_low, 3)
+    far_top = swap(cross_top, 1)
     acc, peak, last, down = near_chunks(
         order,
         (top, bottom, beside_top, beside_low, cross_top, cross_low),

time: 151 us -> 150 us (level)
  transfers between devices with their start and end apart: 15 -> 15, of which waited for: 7 -> 7; matrix products, arithmetic and copies ran while one was open for 0% -> 0% of each run, Pallas kernels for 7% -> 6%
where the time goes in v4:
time: 150 us; the launch traced here: 149 us
  blocking collectives  57.5 us (38%)
  starting transfers between devices  56 us (37%)
  waiting for transfers between devices  17.8 us (12%)
  Pallas kernels  14.8 us (10%)
  local copies, waits for them, and re-layouts  2.14 us (1%)
    all_to_all x1, blocking collectives, layer(): parts = lax.all_to_all(sums, 'z', split_axis=0, concat_axis=0, tiled=True)  29.7 us
    ppermute x9, starting transfers between devices, swap(): return lax.ppermute(array, 'chip', [(j, j ^ mask) for j in range(chips)])  28.7 us
    all_to_all x1, starting transfers between devices, layer(): lax.all_to_all(packed, 'z', split_axis=0, concat_axis=0, tiled=True)  15.2 us
    all_to_all x1, blocking collectives, layer(): lax.all_to_all(sent, ('x', 'core'), split_axis=0, concat_axis=0, tiled=True)  14.6 us
    all_gather x1, blocking collectives, layer(): gathered = lax.all_gather(hidden, 'chip', axis=0)  13.3 us
    ppermute x9, waiting for transfers between devices, swap(): return lax.ppermute(array, 'chip', [(j, j ^ mask) for j in range(chips)])  10.8 us
    ppermute x4, starting transfers between devices, partner(): return lax.ppermute(array, 'core', [(j, 1 - j) for j in range(CORES)])  8.55 us
    all_to_all x1, waiting for transfers between devices, layer(): lax.all_to_all(outputs, ('x', 'core'), split_axis=0, concat_axis=0, tiled...  6.61 us
  transfers between devices with their start and end apart: 15, of which 7 were waited for; matrix products, arithmetic and copies ran while one was open for 0% of the time, Pallas kernels for 6%

profile of v4, /device:TPU:32, one launch (start us, length us, event | category | flops | bytes accessed | tf_op | source)
XLA Modules:
  0.0 149.2 jit_solution(17985183709014561511)
XLA Ops:
  0.6 0.0 copy-start.2
  0.6 1.8 %pack_tokens.1 = bf16[16,72,128]{2,1,0:T(8,128)(2,1)} custom-call(s32[8,16]{1,0:T(8,128)} %bitcast.14, f32[8,16]{1,0:T(8,128)} %bitcast.15, bf16[16,512]{1,0:T(8,128)(2,1)} %tok_hbm.1), custom_call_target="tpu_custom_call" | custom-call | tf_op jit(solution)/shard_map/pack_tokens/pallas_call | solution.py:109
  2.4 15.2 %all-to-all-start = ((bf16[16,72,128]{2,1,0:T(8,128)(2,1)}), bf16[16,72,128]{2,1,0:T(8,128)(2,1)S(1)}, u32[]{:S(2)}, u32[]{:S(2)}) async-start(bf16[16,72,128]{2,1,0:T(8,128)(2,1)} %pack_tokens.1), calls=%async_computation | async-start | bytes 589824 | tf_op jit(solution)/shard_map/all_to_all | solution.py:377
  17.7 1.9 %shard_map.80 = (bf16[192,1024]{1,0:T(8,128)(2,1)S(1)}, bf16[192,1024]{1,0:T(8,128)(2,1)S(1)}, bf16[192,1024]{1,0:T(8,128)(2,1)S(1)}, bf16[192,1024]{1,0:T(8,128)(2,1)S(1)}) custom-call(s32[8]{0:T(128)S(1)} %compare_select_fusion.1.order_ref, bf16[192,4096]{1,0:T(8,128)(2,1)} %bitcast.9), custom_call_target="tpu_custom_call" | custom-call | tf_op jit(solution)/shard_map/pallas_call | solution.py:54
  19.6 0.0 copy-start.1
  19.6 0.7 copy-done.1
  20.4 5.1 %collective-permute-start.10 = (bf16[192,1024]{1,0:T(8,128)(2,1)S(1)}, bf16[192,1024]{1,0:T(8,128)(2,1)S(1)}, u32[]{:S(2)}, u32[]{:S(2)}) collective-permute-start(bf16[192,1024]{1,0:T(8,128)(2,1)S(1)} %get-tuple-element.27), channel_id=1, source_target_pairs={{0,4},{2,6},{4,0},{6,2},{1,5},{3,7},{5,1},{7,3},{8,12},{10,14},{12... | collective-permute-start | bytes 1179656 | tf_op jit(solution)/shard_map/ppermute | solution.py:366
  25.4 2.6 %collective-permute-start.8 = (bf16[192,1024]{1,0:T(8,128)(2,1)S(1)}, bf16[192,1024]{1,0:T(8,128)(2,1)S(1)}, u32[]{:S(2)}, u32[]{:S(2)}) collective-permute-start(bf16[192,1024]{1,0:T(8,128)(2,1)S(1)} %get-tuple-element.25), channel_id=1, source_target_pairs={{0,2},{2,0},{4,6},{6,4},{1,3},{3,1},{5,7},{7,5},{8,10},{10,8},{12,... | collective-permute-start | bytes 1179656 | tf_op jit(solution)/shard_map/ppermute | solution.py:366
  28.0 2.3 %collective-permute-start.9 = (bf16[192,1024]{1,0:T(8,128)(2,1)S(1)}, bf16[192,1024]{1,0:T(8,128)(2,1)S(1)}, u32[]{:S(2)}, u32[]{:S(2)}) collective-permute-start(bf16[192,1024]{1,0:T(8,128)(2,1)S(1)} %get-tuple-element.26), channel_id=1, source_target_pairs={{0,6},{2,4},{4,2},{6,0},{1,7},{3,5},{5,3},{7,1},{8,14},{10,12},{12... | collective-permute-start | bytes 1179656 | tf_op jit(solution)/shard_map/ppermute | solution.py:366
  30.3 0.0 copy-done.2
  30.4 1.9 %collective-permute-start.6 = (bf16[192,4096]{1,0:T(8,128)(2,1)S(1)}, bf16[192,4096]{1,0:T(8,128)(2,1)}, u32[]{:S(2)}, u32[]{:S(2)}) collective-permute-start(bf16[192,4096]{1,0:T(8,128)(2,1)S(1)} %bitcast.11), channel_id=1, source_target_pairs={{0,1},{1,0},{2,3},{3,2},{4,5},{5,4},{6,7},{7,6},{8,9},{9,8},{10,11... | collective-permute-start | bytes 4718600 | tf_op jit(solution)/shard_map/ppermute | solution.py:369
  32.3 2.4 %collective-permute-start.7 = (bf16[192,4096]{1,0:T(8,128)(2,1)}, bf16[192,4096]{1,0:T(8,128)(2,1)}, u32[]{:S(2)}, u32[]{:S(2)}) collective-permute-start(bf16[192,4096]{1,0:T(8,128)(2,1)} %bitcast.12), channel_id=1, source_target_pairs={{0,1},{1,0},{2,3},{3,2},{4,5},{5,4},{6,7},{7,6},{8,9},{9,8},{10,11... | collective-permute-start | bytes 4718600 | tf_op jit(solution)/shard_map/ppermute | solution.py:369
  34.7 1.0 collective-permute-done.10.refs_3_
  35.7 0.0 copy-start.3
  35.7 7.1 %collective-permute-done.8.refs_1_ = bf16[192,1024]{1,0:T(8,128)(2,1)S(1)} collective-permute-done((bf16[192,1024]{1,0:T(8,128)(2,1)S(1)}, bf16[192,1024]{1,0:T(8,128)(2,1)S(1)}, u32[]{:S(2)}, u32[]{:S(2)}) %collective-permute-start.8) | collective-permute-done | bytes 393248 | tf_op jit(solution)/shard_map/ppermute | solution.py:366
  42.8 0.0 copy-start.4
  42.8 0.0 collective-permute-done.9.refs_2_
  42.8 0.0 copy-start.5
  42.9 0.0 copy-done.3
  42.9 0.7 copy-done.4
  43.6 0.2 copy-done.5
  43.7 1.9 %shard_map.81.refs_10_ = bf16[4,192,1024]{2,1,0:T(8,128)(2,1)S(1)} custom-call(s32[8]{0:T(128)S(1)} %compare_select_fusion.1.order_ref, bf16[192,1024]{1,0:T(8,128)(2,1)} %copy-done.1, bf16[192,1024]{1,0:T(8,128)(2,1)} %copy-done.4, bf16[192,1024]{1,0:T(8,128)(2,1)} %copy-done.5, bf16[192,1024]{1,0:T(8,128)(2,1)} %copy-done.3), custom_call_target="tpu_custom_call" | custom-call | tf_op jit(solution)/shard_map/pallas_call | solution.py:54
  45.7 0.0 copy-start
  45.7 1.9 %collective-permute-start.11 = (bf16[4,192,1024]{2,1,0:T(8,128)(2,1)S(1)}, bf16[4,192,1024]{2,1,0:T(8,128)(2,1)}, u32[]{:S(2)}, u32[]{:S(2)}) collective-permute-start(bf16[4,192,1024]{2,1,0:T(8,128)(2,1)S(1)} %shard_map.81.refs_10_), channel_id=1, source_target_pairs={{0,1},{1,0},{2,3},{3,2},{4,5},{5,4},{6,7},{7,6},{8,9},{9,8},{10,11... | collective-permute-start | bytes 4718600 | tf_op jit(solution)/shard_map/ppermute | solution.py:369
  47.6 0.0 all-to-all-done.got_ref
  47.6 0.5 shard_map.78
  48.1 14.6 %all_to_all.20.got_ref = bf16[8,64,512]{2,1,0:T(8,128)(2,1)S(1)} all-to-all(bf16[8,64,512]{2,1,0:T(8,128)(2,1)S(1)} %shard_map.78), channel_id=1, replica_groups=mesh['x'=4,'z'=16,'chip'=4,'core'=2] {'x','core'}, dimensions={0} | all-to-all | bytes 1048576 | tf_op jit(solution)/shard_map/all_to_all | solution.py:393
  62.7 4.4 %collective-permute-start = (bf16[128,1024]{1,0:T(8,128)(2,1)S(1)}, bf16[128,1024]{1,0:T(8,128)(2,1)S(1)}, u32[]{:S(2)}, u32[]{:S(2)}) collective-permute-start(bf16[128,1024]{1,0:T(8,128)(2,1)S(1)} %get-tuple-element.22.refs_0_), channel_id=1, source_target_pairs={{0,6},{2,4},{4,2},{6,0},{1,7},{3,5},{5,3},{7,1},{8,14},{10,12},{12... | collective-permute-start | bytes 786440 | tf_op jit(solution)/shard_map/ppermute | solution.py:366
  67.1 2.0 %collective-permute-start.2 = (bf16[128,1024]{1,0:T(8,128)(2,1)S(1)}, bf16[128,1024]{1,0:T(8,128)(2,1)S(1)}, u32[]{:S(2)}, u32[]{:S(2)}) collective-permute-start(bf16[128,1024]{1,0:T(8,128)(2,1)S(1)} %get-tuple-element.23.refs_1_), channel_id=1, source_target_pairs={{0,2},{2,0},{4,6},{6,4},{1,3},{3,1},{5,7},{7,5},{8,10},{10,8},{12,... | collective-permute-start | bytes 786440 | tf_op jit(solution)/shard_map/ppermute | solution.py:366
  69.2 0.0 collective-permute-done.6.refs_7_
  69.2 3.8 %collective-permute-start.4 = (bf16[128,1024]{1,0:T(8,128)(2,1)S(1)}, bf16[128,1024]{1,0:T(8,128)(2,1)S(1)}, u32[]{:S(2)}, u32[]{:S(2)}) collective-permute-start(bf16[128,1024]{1,0:T(8,128)(2,1)S(1)} %get-tuple-element.22.refs_0_), channel_id=1, source_target_pairs={{0,2},{2,0},{4,6},{6,4},{1,3},{3,1},{5,7},{7,5},{8,10},{10,8},{12,... | collective-permute-start | bytes 786440 | tf_op jit(solution)/shard_map/ppermute | solution.py:366
  73.0 0.0 collective-permute-done.7.refs_9_
  73.0 2.6 %collective-permute-start.5 = (bf16[128,1024]{1,0:T(8,128)(2,1)S(1)}, bf16[128,1024]{1,0:T(8,128)(2,1)S(1)}, u32[]{:S(2)}, u32[]{:S(2)}) collective-permute-start(bf16[128,1024]{1,0:T(8,128)(2,1)S(1)} %get-tuple-element.23.refs_1_), channel_id=1, source_target_pairs={{0,6},{2,4},{4,2},{6,0},{1,7},{3,5},{5,3},{7,1},{8,14},{10,12},{12... | collective-permute-start | bytes 786440 | tf_op jit(solution)/shard_map/ppermute | solution.py:366
  75.7 0.0 collective-permute-done.refs_4_
  75.7 2.0 %collective-permute-start.1 = (bf16[128,1024]{1,0:T(8,128)(2,1)S(1)}, bf16[128,1024]{1,0:T(8,128)(2,1)S(1)}, u32[]{:S(2)}, u32[]{:S(2)}) collective-permute-start(bf16[128,1024]{1,0:T(8,128)(2,1)S(1)} %collective-permute-done.refs_4_), channel_id=1, source_target_pairs={{0,2},{2,0},{4,6},{6,4},{1,3},{3,1},{5,7},{7,5},{8,10},{10,8},{12,... | collective-permute-start | bytes 786440 | tf_op jit(solution)/shard_map/ppermute | solution.py:366
  77.7 0.5 collective-permute-done.2.refs_3_
  78.2 3.8 %collective-permute-start.3 = (bf16[128,1024]{1,0:T(8,128)(2,1)S(1)}, bf16[128,1024]{1,0:T(8,128)(2,1)S(1)}, u32[]{:S(2)}, u32[]{:S(2)}) collective-permute-start(bf16[128,1024]{1,0:T(8,128)(2,1)S(1)} %collective-permute-done.2.refs_3_), channel_id=1, source_target_pairs={{0,6},{2,4},{4,2},{6,0},{1,7},{3,5},{5,3},{7,1},{8,14},{10,12},{12... | collective-permute-start | bytes 786440 | tf_op jit(solution)/shard_map/ppermute | solution.py:366
  82.0 1.8 %collective-permute-done.4.refs_2_ = bf16[128,1024]{1,0:T(8,128)(2,1)S(1)} collective-permute-done((bf16[128,1024]{1,0:T(8,128)(2,1)S(1)}, bf16[128,1024]{1,0:T(8,128)(2,1)S(1)}, u32[]{:S(2)}, u32[]{:S(2)}) %collective-permute-start.4) | collective-permute-done | bytes 262176 | tf_op jit(solution)/shard_map/ppermute | solution.py:366
  83.8 0.4 collective-permute-done.5.refs_5_
  84.3 0.0 collective-permute-done.11.refs_11_
  84.3 0.0 copy-done
  84.3 4.6 %near_chunks.1 = (f32[256,768]{1,0:T(8,128)S(1)}, f32[1,1024]{1,0:T(1,128)S(1)}, bf16[768,1024]{1,0:T(8,128)(2,1)S(1)}, bf16[1536,1024]{1,0:T(8,128)(2,1)S(1)}) custom-call(s32[8]{0:T(128)S(1)} %compare_select_fusion.1.order_ref, bf16[128,1024]{1,0:T(8,128)(2,1)S(1)} %get-tuple-element.22.refs_0_, bf16[128,1024]{1,0:T(8,128)(2,1)S(1)} %get-tuple-element.23.refs_1_, ...), custom_call_target="tpu_custom_call" | custom-call | flops 1207959552 | bytes 9437184 | tf_op jit(solution)/shard_map/near_chunks/pallas_call | solution.py:258
  88.9 0.0 collective-permute-done.1.top_ref
  88.9 0.0 collective-permute-done.3.low_ref
  88.9 0.7 shard_map.82
  89.5 13.3 %all-gather = bf16[1024,384]{1,0:T(8,128)(2,1)S(1)} all-gather(bf16[256,384]{1,0:T(8,128)(2,1)S(1)} %get-tuple-element.31), channel_id=2, replica_groups=mesh['x'=4,'z'=16,'chip'=4,'core'=2] {'chip'}, dimensions={0}, use_global_device_ids=true | all-gather | bytes 983040 | tf_op jit(solution)/shard_map/all_gather | solution.py:423
  102.9 1.9 %shard_map.83 = (bf16[8,64,512]{2,1,0:T(8,128)(2,1)}, f32[8,128]{1,0:T(8,128)S(1)}) custom-call(bf16[4,256,384]{2,1,0:T(8,128)(2,1)S(1)} %bitcast.8, bf16[1536,1024]{1,0:T(8,128)(2,1)S(1)} %get-tuple-element.32.down_ref, f32[8,128]{1,0:T(8,128)S(1)} %get-tuple-element.33.peak_in), custom_call_target="tpu_custom_call" | custom-call | tf_op jit(solution)/shard_map/pallas_call | solution.py:76
  104.7 3.5 %all-to-all-start.2 = ((bf16[8,64,512]{2,1,0:T(8,128)(2,1)}), bf16[8,64,512]{2,1,0:T(8,128)(2,1)S(1)}, u32[]{:S(2)}, u32[]{:S(2)}) async-start(bf16[8,64,512]{2,1,0:T(8,128)(2,1)} %get-tuple-element.34), calls=%async_computation.2 | async-start | bytes 1048576 | tf_op jit(solution)/shard_map/all_to_all | solution.py:431
  108.2 2.3 %collective-permute-start.12 = (f32[8,128]{1,0:T(8,128)S(1)}, f32[8,128]{1,0:T(8,128)S(1)}, u32[]{:S(2)}, u32[]{:S(2)}) collective-permute-start(f32[8,128]{1,0:T(8,128)S(1)} %get-tuple-element.35), channel_id=1, source_target_pairs={{0,1},{1,0},{2,3},{3,2},{4,5},{5,4},{6,7},{7,6},{8,9},{9,8},{10,11... | collective-permute-start | bytes 12296 | tf_op jit(solution)/shard_map/ppermute | solution.py:369
  110.5 0.5 shard_map.77
  111.0 0.3 collective-permute-done.12
  111.3 0.5 slice_bitcast_fusion
  111.8 6.6 %all-to-all-done.2.row_ref = bf16[8,64,512]{2,1,0:T(8,128)(2,1)S(1)} async-done(((bf16[8,64,512]{2,1,0:T(8,128)(2,1)}), bf16[8,64,512]{2,1,0:T(8,128)(2,1)S(1)}, u32[]{:S(2)}, u32[]{:S(2)}) %all-to-all-start.2) | async-done | bytes 524320 | tf_op jit(solution)/shard_map/all_to_all | solution.py:431
  118.4 0.4 shard_map.84
  118.9 29.7 %all_to_all.21.part_ref = bf16[16,16,512]{2,1,0:T(8,128)(2,1)S(1)} all-to-all(bf16[16,16,512]{2,1,0:T(8,128)(2,1)S(1)} %shard_map.84), channel_id=1, replica_groups=mesh['x'=4,'z'=16,'chip'=4,'core'=2] {'z'}, dimensions={0} | all-to-all | bytes 524288 | tf_op jit(solution)/shard_map/all_to_all | solution.py:440
  148.5 0.6 shard_map.85
  (3 shorter events, 0.0 us)
Async XLA Ops:
  0.6 29.7 %copy-start.2 = (bf16[1,192,4096]{2,1,0:T(8,128)(2,1)S(1)}, bf16[1,192,4096]{2,1,0:T(8,128)(2,1)}, u32[]{:S(2)}) copy-start(bf16[1,192,4096]{2,1,0:T(8,128)(2,1)} %param.9) | copy-start | bytes 4718596
  2.4 45.2 %all-to-all-start = ((bf16[16,72,128]{2,1,0:T(8,128)(2,1)}), bf16[16,72,128]{2,1,0:T(8,128)(2,1)S(1)}, u32[]{:S(2)}, u32[]{:S(2)}) async-start(bf16[16,72,128]{2,1,0:T(8,128)(2,1)} %pack_tokens.1), calls=%async_computation | async-start | bytes 589824 | tf_op jit(solution)/shard_map/all_to_all | solution.py:377
  19.6 0.7 copy-start.1
  20.4 15.4 %collective-permute-start.10 = (bf16[192,1024]{1,0:T(8,128)(2,1)S(1)}, bf16[192,1024]{1,0:T(8,128)(2,1)S(1)}, u32[]{:S(2)}, u32[]{:S(2)}) collective-permute-start(bf16[192,1024]{1,0:T(8,128)(2,1)S(1)} %get-tuple-element.27), channel_id=1, source_target_pairs={{0,4},{2,6},{4,0},{6,2},{1,5},{3,7},{5,1},{7,3},{8,12},{10,14},{12... | collective-permute-start | bytes 1179656 | tf_op jit(solution)/shard_map/ppermute | solution.py:366
  25.4 17.4 %collective-permute-start.8 = (bf16[192,1024]{1,0:T(8,128)(2,1)S(1)}, bf16[192,1024]{1,0:T(8,128)(2,1)S(1)}, u32[]{:S(2)}, u32[]{:S(2)}) collective-permute-start(bf16[192,1024]{1,0:T(8,128)(2,1)S(1)} %get-tuple-element.25), channel_id=1, source_target_pairs={{0,2},{2,0},{4,6},{6,4},{1,3},{3,1},{5,7},{7,5},{8,10},{10,8},{12,... | collective-permute-start | bytes 1179656 | tf_op jit(solution)/shard_map/ppermute | solution.py:366
  28.0 14.8 %collective-permute-start.9 = (bf16[192,1024]{1,0:T(8,128)(2,1)S(1)}, bf16[192,1024]{1,0:T(8,128)(2,1)S(1)}, u32[]{:S(2)}, u32[]{:S(2)}) collective-permute-start(bf16[192,1024]{1,0:T(8,128)(2,1)S(1)} %get-tuple-element.26), channel_id=1, source_target_pairs={{0,6},{2,4},{4,2},{6,0},{1,7},{3,5},{5,3},{7,1},{8,14},{10,12},{12... | collective-permute-start | bytes 1179656 | tf_op jit(solution)/shard_map/ppermute | solution.py:366
  30.4 38.8 %collective-permute-start.6 = (bf16[192,4096]{1,0:T(8,128)(2,1)S(1)}, bf16[192,4096]{1,0:T(8,128)(2,1)}, u32[]{:S(2)}, u32[]{:S(2)}) collective-permute-start(bf16[192,4096]{1,0:T(8,128)(2,1)S(1)} %bitcast.11), channel_id=1, source_target_pairs={{0,1},{1,0},{2,3},{3,2},{4,5},{5,4},{6,7},{7,6},{8,9},{9,8},{10,11... | collective-permute-start | bytes 4718600 | tf_op jit(solution)/shard_map/ppermute | solution.py:369
  32.3 40.7 %collective-permute-start.7 = (bf16[192,4096]{1,0:T(8,128)(2,1)}, bf16[192,4096]{1,0:T(8,128)(2,1)}, u32[]{:S(2)}, u32[]{:S(2)}) collective-permute-start(bf16[192,4096]{1,0:T(8,128)(2,1)} %bitcast.12), channel_id=1, source_target_pairs={{0,1},{1,0},{2,3},{3,2},{4,5},{5,4},{6,7},{7,6},{8,9},{9,8},{10,11... | collective-permute-start | bytes 4718600 | tf_op jit(solution)/shard_map/ppermute | solution.py:369
  35.7 7.1 %copy-start.3 = (bf16[192,1024]{1,0:T(8,128)(2,1)}, bf16[192,1024]{1,0:T(8,128)(2,1)S(1)}, u32[]{:S(2)}) copy-start(bf16[192,1024]{1,0:T(8,128)(2,1)S(1)} %collective-permute-done.10.refs_3_) | copy-start | bytes 1179652
  42.8 0.7 copy-start.4
  42.8 0.9 copy-start.5
  45.7 38.6 %copy-start = (bf16[4,192,1024]{2,1,0:T(8,128)(2,1)}, bf16[4,192,1024]{2,1,0:T(8,128)(2,1)S(1)}, u32[]{:S(2)}) copy-start(bf16[4,192,1024]{2,1,0:T(8,128)(2,1)S(1)} %shard_map.81.refs_10_) | copy-start | bytes 4718596
  45.7 38.6 %collective-permute-start.11 = (bf16[4,192,1024]{2,1,0:T(8,128)(2,1)S(1)}, bf16[4,192,1024]{2,1,0:T(8,128)(2,1)}, u32[]{:S(2)}, u32[]{:S(2)}) collective-permute-start(bf16[4,192,1024]{2,1,0:T(8,128)(2,1)S(1)} %shard_map.81.refs_10_), channel_id=1, source_target_pairs={{0,1},{1,0},{2,3},{3,2},{4,5},{5,4},{6,7},{7,6},{8,9},{9,8},{10,11... | collective-permute-start | bytes 4718600 | tf_op jit(solution)/shard_map/ppermute | solution.py:369
  62.7 13.0 %collective-permute-start = (bf16[128,1024]{1,0:T(8,128)(2,1)S(1)}, bf16[128,1024]{1,0:T(8,128)(2,1)S(1)}, u32[]{:S(2)}, u32[]{:S(2)}) collective-permute-start(bf16[128,1024]{1,0:T(8,128)(2,1)S(1)} %get-tuple-element.22.refs_0_), channel_id=1, source_target_pairs={{0,6},{2,4},{4,2},{6,0},{1,7},{3,5},{5,3},{7,1},{8,14},{10,12},{12... | collective-permute-start | bytes 786440 | tf_op jit(solution)/shard_map/ppermute | solution.py:366
  67.1 11.1 %collective-permute-start.2 = (bf16[128,1024]{1,0:T(8,128)(2,1)S(1)}, bf16[128,1024]{1,0:T(8,128)(2,1)S(1)}, u32[]{:S(2)}, u32[]{:S(2)}) collective-permute-start(bf16[128,1024]{1,0:T(8,128)(2,1)S(1)} %get-tuple-element.23.refs_1_), channel_id=1, source_target_pairs={{0,2},{2,0},{4,6},{6,4},{1,3},{3,1},{5,7},{7,5},{8,10},{10,8},{12,... | collective-permute-start | bytes 786440 | tf_op jit(solution)/shard_map/ppermute | solution.py:366
  69.2 14.6 %collective-permute-start.4 = (bf16[128,1024]{1,0:T(8,128)(2,1)S(1)}, bf16[128,1024]{1,0:T(8,128)(2,1)S(1)}, u32[]{:S(2)}, u32[]{:S(2)}) collective-permute-start(bf16[128,1024]{1,0:T(8,128)(2,1)S(1)} %get-tuple-element.22.refs_0_), channel_id=1, source_target_pairs={{0,2},{2,0},{4,6},{6,4},{1,3},{3,1},{5,7},{7,5},{8,10},{10,8},{12,... | collective-permute-start | bytes 786440 | tf_op jit(solution)/shard_map/ppermute | solution.py:366
  73.0 11.2 %collective-permute-start.5 = (bf16[128,1024]{1,0:T(8,128)(2,1)S(1)}, bf16[128,1024]{1,0:T(8,128)(2,1)S(1)}, u32[]{:S(2)}, u32[]{:S(2)}) collective-permute-start(bf16[128,1024]{1,0:T(8,128)(2,1)S(1)} %get-tuple-element.23.refs_1_), channel_id=1, source_target_pairs={{0,6},{2,4},{4,2},{6,0},{1,7},{3,5},{5,3},{7,1},{8,14},{10,12},{12... | collective-permute-start | bytes 786440 | tf_op jit(solution)/shard_map/ppermute | solution.py:366
  75.7 13.2 %collective-permute-start.1 = (bf16[128,1024]{1,0:T(8,128)(2,1)S(1)}, bf16[128,1024]{1,0:T(8,128)(2,1)S(1)}, u32[]{:S(2)}, u32[]{:S(2)}) collective-permute-start(bf16[128,1024]{1,0:T(8,128)(2,1)S(1)} %collective-permute-done.refs_4_), channel_id=1, source_target_pairs={{0,2},{2,0},{4,6},{6,4},{1,3},{3,1},{5,7},{7,5},{8,10},{10,8},{12,... | collective-permute-start | bytes 786440 | tf_op jit(solution)/shard_map/ppermute | solution.py:366
  78.2 10.7 %collective-permute-start.3 = (bf16[128,1024]{1,0:T(8,128)(2,1)S(1)}, bf16[128,1024]{1,0:T(8,128)(2,1)S(1)}, u32[]{:S(2)}, u32[]{:S(2)}) collective-permute-start(bf16[128,1024]{1,0:T(8,128)(2,1)S(1)} %collective-permute-done.2.refs_3_), channel_id=1, source_target_pairs={{0,6},{2,4},{4,2},{6,0},{1,7},{3,5},{5,3},{7,1},{8,14},{10,12},{12... | collective-permute-start | bytes 786440 | tf_op jit(solution)/shard_map/ppermute | solution.py:366
  104.7 13.7 %all-to-all-start.2 = ((bf16[8,64,512]{2,1,0:T(8,128)(2,1)}), bf16[8,64,512]{2,1,0:T(8,128)(2,1)S(1)}, u32[]{:S(2)}, u32[]{:S(2)}) async-start(bf16[8,64,512]{2,1,0:T(8,128)(2,1)} %get-tuple-element.34), calls=%async_computation.2 | async-start | bytes 1048576 | tf_op jit(solution)/shard_map/all_to_all | solution.py:431
  108.2 3.1 %collective-permute-start.12 = (f32[8,128]{1,0:T(8,128)S(1)}, f32[8,128]{1,0:T(8,128)S(1)}, u32[]{:S(2)}, u32[]{:S(2)}) collective-permute-start(f32[8,128]{1,0:T(8,128)S(1)} %get-tuple-element.35), channel_id=1, source_target_pairs={{0,1},{1,0},{2,3},{3,2},{4,5},{5,4},{6,7},{7,6},{8,9},{9,8},{10,11... | collective-permute-start | bytes 12296 | tf_op jit(solution)/shard_map/ppermute | solution.py:369

commit v5 on v4

--- a/solution.py
+++ b/solution.py
@@ -195,12 +195,12 @@
 
 
 def near_kernel(order_ref, *refs):
-    pieces, (gate_own, gate_other, up_own, up_other, down_own, down_other) = refs[:6], refs[6:12]
-    acc_ref, peak_ref, last_ref, down_ref, x_ref, w_ref, sems = refs[12:]
+    pieces, (gate_own, gate_other, up_own, up_other) = refs[:6], refs[6:10]
+    acc_ref, peak_ref, last_ref, x_ref, w_ref, sems = refs[10:]
     core = order_ref[4]
     half, width = pieces[0].shape
     unit = gate_own.shape[0]
-    chips = down_own.shape[0]
+    chips = gate_own.shape[1] // width
     own = pl.multiple_of(core * unit, unit)
     other = pl.multiple_of((1 - core) * unit, unit)
     fetched = []
@@ -222,16 +222,7 @@
                 )
             )
         fetched.append(group)
-    handed = []
-    for chip in range(chips):
-        for place, (source, first) in enumerate(((down_own, own), (down_other, other))):
-            rows = pl.ds(pl.multiple_of(chip * CORES * unit + first, unit), unit)
-            handed.append(
-                pltpu.make_async_copy(
-                    source.at[chip], down_ref.at[rows, :], sems.at[chips + place, chip]
-                )
-            )
-    for copy in [copy for group in fetched for copy in group] + handed:
+    for copy in [copy for group in fetched for copy in group]:
         copy.start()
     peak = None
     total = None
@@ -247,28 +238,28 @@
         peak = high if peak is None else jnp.maximum(peak, high)
     acc_ref[...] = total
     peak_ref[...] = peak
-    for copy in fetched[3] + handed:
+    for copy in fetched[3]:
         copy.wait()
 
 
-def near_chunks(order, pieces, weights, downs):
+def near_chunks(order, pieces, weights):
     half, width = pieces[0].shape
-    chips, unit, _ = downs[0].shape
+    unit, every = weights[0].shape
+    chips = every // width
     wide = 2 * CORES * unit
     return pl.pallas_call(
         near_kernel,
-        in_specs=[IN_SMEM] + [IN_VMEM] * 6 + [IN_PLACE] * 6,
-        out_specs=[IN_VMEM] * 4,
+        in_specs=[IN_SMEM] + [IN_VMEM] * 6 + [IN_PLACE] * 4,
+        out_specs=[IN_VMEM] * 3,
         out_shape=[
             jax.ShapeDtypeStruct((2 * half, wide), F32),
             jax.ShapeDtypeStruct((1, width), F32),
             jax.ShapeDtypeStruct((wide, width), BF),
-            jax.ShapeDtypeStruct((chips * CORES * unit, width), BF),
         ],
         scratch_shapes=[
             pltpu.VMEM((3, 2 * half, width), BF),
             pltpu.VMEM((3, wide, width), BF),
-            pltpu.SemaphoreType.DMA((chips + 2, 4)),
+            pltpu.SemaphoreType.DMA((chips, 4)),
         ],
         compiler_params=ROOM,
         cost_estimate=pl.CostEstimate(
@@ -279,7 +270,6 @@
         order,
         *(local(piece) for piece in pieces),
         *(remote(array) for array in weights),
-        *(remote(array) for array in downs),
     )
 
 
@@ -319,6 +309,34 @@
             for number, piece in enumerate(pieces)
         ]
     )
+
+
+def pair_kernel(order_ref, own_ref, other_ref, out_ref, sems):
+    chips, unit, _ = own_ref.shape
+    core = order_ref[4]
+    copies = []
+    for chip in range(chips):
+        for number, (source, place) in enumerate(((own_ref, core), (other_ref, 1 - core))):
+            first = pl.multiple_of((chip * CORES + place) * unit, unit)
+            copies.append(
+                pltpu.make_async_copy(
+                    source.at[chip], out_ref.at[pl.ds(first, unit), :], sems.at[chip, number]
+                )
+            )
+    run_copies(copies)
+
+
+def pair_rows(order, own, other):
+    chips, unit, width = own.shape
+    return pl.pallas_call(
+        pair_kernel,
+        in_specs=[IN_SMEM] + [IN_PLACE] * 2,
+        out_specs=IN_VMEM,
+        out_shape=jax.ShapeDtypeStruct((chips * CORES * unit, width), BF),
+        scratch_shapes=[pltpu.SemaphoreType.DMA((chips, CORES))],
+        compiler_params=ROOM,
+        name="pair_rows",
+    )(order, remote(own), remote(other))
 
 
 def down_kernel(hid_ref, down_ref, peak_in, out_ref, peak_ref, h_ref):
@@ -393,6 +411,7 @@
     received = lax.all_to_all(sent, ("x", "core"), split_axis=0, concat_axis=0, tiled=True)
     stacked = move(stack_kernel, order, pieces, shaped((chips, unit, chunk), BF), chips)
     stacked_other = partner(stacked)
+    down = pair_rows(order, stacked, stacked_other)
     high, low = call(
         weigh_kernel,
         None,
@@ -403,15 +422,13 @@
     top, bottom = call(join_kernel, None, (local(received),), [shaped((kept // 2, chunk), BF)] * 2)
     cross_top = swap(top, 3)
     beside_low = swap(bottom, 1)
+    cross_low = swap(bottom, 3)
     beside_top = swap(top, 1)
-    cross_low = swap(bottom, 3)
-    far_low = swap(beside_low, 3)
-    far_top = swap(cross_top, 1)
-    acc, peak, last, down = near_chunks(
+    far_top, far_low = swap(cross_top, 1), swap(beside_low, 3)
+    acc, peak, last = near_chunks(
         order,
         (top, bottom, beside_top, beside_low, cross_top, cross_low),
         (gate_weight[0], gate_other, up_weight[0], up_other),
-        (stacked, stacked_other),
     )
     hidden, peak = call(
         far_kernel,

time: 150 us -> 154 us (1.027)
  Pallas kernels: 14.8 us -> 17 us
    pallas_call x0 -> x1, Pallas kernels: none -> 2.44 us  [pair_rows(): pl.pallas_call(pair_kernel, in_specs=[IN_SMEM] + [IN_PLACE] * 2, out_spec...]
  transfers between devices with their start and end apart: 15 -> 15, of which waited for: 7 -> 7; matrix products, arithmetic and copies ran while one was open for 0% -> 0% of each run, Pallas kernels for 6% -> 8%
where the time goes in v5:
time: 154 us; the launch traced here: 153 us
  blocking collectives  58 us (38%)
  starting transfers between devices  56 us (36%)
  waiting for transfers between devices  17.8 us (12%)
  Pallas kernels  17 us (11%)
  local copies, waits for them, and re-layouts  3.3 us (2%)
    all_to_all x1, blocking collectives, layer(): parts = lax.all_to_all(sums, 'z', split_axis=0, concat_axis=0, tiled=True)  29.7 us
    ppermute x9, starting transfers between devices, swap(): return lax.ppermute(array, 'chip', [(j, j ^ mask) for j in range(chips)])  28.7 us
    all_to_all x1, starting transfers between devices, layer(): lax.all_to_all(packed, 'z', split_axis=0, concat_axis=0, tiled=True)  15.2 us
    all_to_all x1, blocking collectives, layer(): lax.all_to_all(sent, ('x', 'core'), split_axis=0, concat_axis=0, tiled=True)  14.6 us
    all_gather x1, blocking collectives, layer(): gathered = lax.all_gather(hidden, 'chip', axis=0)  13.8 us
    ppermute x9, waiting for transfers between devices, swap(): return lax.ppermute(array, 'chip', [(j, j ^ mask) for j in range(chips)])  10.9 us
    ppermute x4, starting transfers between devices, partner(): return lax.ppermute(array, 'core', [(j, 1 - j) for j in range(CORES)])  8.55 us
    all_to_all x1, waiting for transfers between devices, layer(): lax.all_to_all(outputs, ('x', 'core'), split_axis=0, concat_axis=0, tiled...  6.61 us
  transfers between devices with their start and end apart: 15, of which 7 were waited for; matrix products, arithmetic and copies ran while one was open for 0% of the time, Pallas kernels for 8%

profile of v5, /device:TPU:32, one launch (start us, length us, event | category | flops | bytes accessed | tf_op | source)
XLA Modules:
  0.0 153.1 jit_solution(9333910272635128963)
XLA Ops:
  0.6 1.7 %pack_tokens.1 = bf16[16,72,128]{2,1,0:T(8,128)(2,1)} custom-call(s32[8,16]{1,0:T(8,128)} %bitcast.10, f32[8,16]{1,0:T(8,128)} %bitcast.11, bf16[16,512]{1,0:T(8,128)(2,1)} %tok_hbm.1), custom_call_target="tpu_custom_call" | custom-call | tf_op jit(solution)/shard_map/pack_tokens/pallas_call | solution.py:109
  2.3 15.2 %all-to-all-start = ((bf16[16,72,128]{2,1,0:T(8,128)(2,1)}), bf16[16,72,128]{2,1,0:T(8,128)(2,1)S(1)}, u32[]{:S(2)}, u32[]{:S(2)}) async-start(bf16[16,72,128]{2,1,0:T(8,128)(2,1)} %pack_tokens.1), calls=%async_computation | async-start | bytes 589824 | tf_op jit(solution)/shard_map/all_to_all | solution.py:395
  17.5 1.9 %shard_map.81 = (bf16[192,1024]{1,0:T(8,128)(2,1)S(1)}, bf16[192,1024]{1,0:T(8,128)(2,1)S(1)}, bf16[192,1024]{1,0:T(8,128)(2,1)S(1)}, bf16[192,1024]{1,0:T(8,128)(2,1)S(1)}) custom-call(s32[8]{0:T(128)S(1)} %compare_select_fusion.1.order_ref, bf16[192,4096]{1,0:T(8,128)(2,1)} %bitcast.9), custom_call_target="tpu_custom_call" | custom-call | tf_op jit(solution)/shard_map/pallas_call | solution.py:54
  19.5 0.0 copy-start.1
  19.5 0.7 copy-done.1
  20.2 5.1 %collective-permute-start.10 = (bf16[192,1024]{1,0:T(8,128)(2,1)S(1)}, bf16[192,1024]{1,0:T(8,128)(2,1)S(1)}, u32[]{:S(2)}, u32[]{:S(2)}) collective-permute-start(bf16[192,1024]{1,0:T(8,128)(2,1)S(1)} %get-tuple-element.30), channel_id=1, source_target_pairs={{0,4},{2,6},{4,0},{6,2},{1,5},{3,7},{5,1},{7,3},{8,12},{10,14},{12... | collective-permute-start | bytes 1179656 | tf_op jit(solution)/shard_map/ppermute | solution.py:384
  25.3 2.6 %collective-permute-start.8 = (bf16[192,1024]{1,0:T(8,128)(2,1)S(1)}, bf16[192,1024]{1,0:T(8,128)(2,1)S(1)}, u32[]{:S(2)}, u32[]{:S(2)}) collective-permute-start(bf16[192,1024]{1,0:T(8,128)(2,1)S(1)} %get-tuple-element.28), channel_id=1, source_target_pairs={{0,2},{2,0},{4,6},{6,4},{1,3},{3,1},{5,7},{7,5},{8,10},{10,8},{12,... | collective-permute-start | bytes 1179656 | tf_op jit(solution)/shard_map/ppermute | solution.py:384
  27.9 2.3 %collective-permute-start.9 = (bf16[192,1024]{1,0:T(8,128)(2,1)S(1)}, bf16[192,1024]{1,0:T(8,128)(2,1)S(1)}, u32[]{:S(2)}, u32[]{:S(2)}) collective-permute-start(bf16[192,1024]{1,0:T(8,128)(2,1)S(1)} %get-tuple-element.29), channel_id=1, source_target_pairs={{0,6},{2,4},{4,2},{6,0},{1,7},{3,5},{5,3},{7,1},{8,14},{10,12},{12... | collective-permute-start | bytes 1179656 | tf_op jit(solution)/shard_map/ppermute | solution.py:384
  30.2 1.9 %collective-permute-start.6 = (bf16[192,4096]{1,0:T(8,128)(2,1)}, bf16[192,4096]{1,0:T(8,128)(2,1)}, u32[]{:S(2)}, u32[]{:S(2)}) collective-permute-start(bf16[192,4096]{1,0:T(8,128)(2,1)} %bitcast.2.refs_6_), channel_id=1, source_target_pairs={{0,1},{1,0},{2,3},{3,2},{4,5},{5,4},{6,7},{7,6},{8,9},{9,8},{10,11... | collective-permute-start | bytes 4718600 | tf_op jit(solution)/shard_map/ppermute | solution.py:387
  32.2 2.4 %collective-permute-start.7 = (bf16[192,4096]{1,0:T(8,128)(2,1)}, bf16[192,4096]{1,0:T(8,128)(2,1)}, u32[]{:S(2)}, u32[]{:S(2)}) collective-permute-start(bf16[192,4096]{1,0:T(8,128)(2,1)} %bitcast.3.refs_8_), channel_id=1, source_target_pairs={{0,1},{1,0},{2,3},{3,2},{4,5},{5,4},{6,7},{7,6},{8,9},{9,8},{10,11... | collective-permute-start | bytes 4718600 | tf_op jit(solution)/shard_map/ppermute | solution.py:387
  34.6 1.0 collective-permute-done.10.refs_3_
  35.6 0.0 copy-start.3
  35.6 7.1 %collective-permute-done.8.refs_1_ = bf16[192,1024]{1,0:T(8,128)(2,1)S(1)} collective-permute-done((bf16[192,1024]{1,0:T(8,128)(2,1)S(1)}, bf16[192,1024]{1,0:T(8,128)(2,1)S(1)}, u32[]{:S(2)}, u32[]{:S(2)}) %collective-permute-start.8) | collective-permute-done | bytes 393248 | tf_op jit(solution)/shard_map/ppermute | solution.py:384
  42.7 0.0 copy-start.4
  42.7 0.0 collective-permute-done.9.refs_2_
  42.7 0.0 copy-start.5
  42.7 0.0 copy-done.3
  42.7 0.7 copy-done.4
  43.5 0.2 copy-done.5
  43.6 1.9 %shard_map.82.own_ref = bf16[4,192,1024]{2,1,0:T(8,128)(2,1)S(1)} custom-call(s32[8]{0:T(128)S(1)} %compare_select_fusion.1.order_ref, bf16[192,1024]{1,0:T(8,128)(2,1)} %copy-done.1, bf16[192,1024]{1,0:T(8,128)(2,1)} %copy-done.4, bf16[192,1024]{1,0:T(8,128)(2,1)} %copy-done.5, bf16[192,1024]{1,0:T(8,128)(2,1)} %copy-done.3), custom_call_target="tpu_custom_call" | custom-call | tf_op jit(solution)/shard_map/pallas_call | solution.py:54
  45.6 0.0 copy-start
  45.6 1.9 %collective-permute-start.11 = (bf16[4,192,1024]{2,1,0:T(8,128)(2,1)S(1)}, bf16[4,192,1024]{2,1,0:T(8,128)(2,1)S(1)}, u32[]{:S(2)}, u32[]{:S(2)}) collective-permute-start(bf16[4,192,1024]{2,1,0:T(8,128)(2,1)S(1)} %shard_map.82.own_ref), channel_id=1, source_target_pairs={{0,1},{1,0},{2,3},{3,2},{4,5},{5,4},{6,7},{7,6},{8,9},{9,8},{10,11... | collective-permute-start | bytes 4718600 | tf_op jit(solution)/shard_map/ppermute | solution.py:387
  47.5 0.0 all-to-all-done.got_ref
  47.5 0.5 shard_map.78
  48.0 14.6 %all_to_all.20.got_ref = bf16[8,64,512]{2,1,0:T(8,128)(2,1)S(1)} all-to-all(bf16[8,64,512]{2,1,0:T(8,128)(2,1)S(1)} %shard_map.78), channel_id=1, replica_groups=mesh['x'=4,'z'=16,'chip'=4,'core'=2] {'x','core'}, dimensions={0} | all-to-all | bytes 1048576 | tf_op jit(solution)/shard_map/all_to_all | solution.py:411
  62.6 4.4 %collective-permute-start = (bf16[128,1024]{1,0:T(8,128)(2,1)S(1)}, bf16[128,1024]{1,0:T(8,128)(2,1)S(1)}, u32[]{:S(2)}, u32[]{:S(2)}) collective-permute-start(bf16[128,1024]{1,0:T(8,128)(2,1)S(1)} %get-tuple-element.21.refs_0_), channel_id=1, source_target_pairs={{0,6},{2,4},{4,2},{6,0},{1,7},{3,5},{5,3},{7,1},{8,14},{10,12},{12... | collective-permute-start | bytes 786440 | tf_op jit(solution)/shard_map/ppermute | solution.py:384
  67.0 2.0 %collective-permute-start.2 = (bf16[128,1024]{1,0:T(8,128)(2,1)S(1)}, bf16[128,1024]{1,0:T(8,128)(2,1)S(1)}, u32[]{:S(2)}, u32[]{:S(2)}) collective-permute-start(bf16[128,1024]{1,0:T(8,128)(2,1)S(1)} %get-tuple-element.22.refs_1_), channel_id=1, source_target_pairs={{0,2},{2,0},{4,6},{6,4},{1,3},{3,1},{5,7},{7,5},{8,10},{10,8},{12,... | collective-permute-start | bytes 786440 | tf_op jit(solution)/shard_map/ppermute | solution.py:384
  69.1 0.0 collective-permute-done.6.refs_7_
  69.1 3.8 %collective-permute-start.4 = (bf16[128,1024]{1,0:T(8,128)(2,1)S(1)}, bf16[128,1024]{1,0:T(8,128)(2,1)S(1)}, u32[]{:S(2)}, u32[]{:S(2)}) collective-permute-start(bf16[128,1024]{1,0:T(8,128)(2,1)S(1)} %get-tuple-element.21.refs_0_), channel_id=1, source_target_pairs={{0,2},{2,0},{4,6},{6,4},{1,3},{3,1},{5,7},{7,5},{8,10},{10,8},{12,... | collective-permute-start | bytes 786440 | tf_op jit(solution)/shard_map/ppermute | solution.py:384
  72.9 0.0 collective-permute-done.7.refs_9_
  72.9 2.6 %collective-permute-start.5 = (bf16[128,1024]{1,0:T(8,128)(2,1)S(1)}, bf16[128,1024]{1,0:T(8,128)(2,1)S(1)}, u32[]{:S(2)}, u32[]{:S(2)}) collective-permute-start(bf16[128,1024]{1,0:T(8,128)(2,1)S(1)} %get-tuple-element.22.refs_1_), channel_id=1, source_target_pairs={{0,6},{2,4},{4,2},{6,0},{1,7},{3,5},{5,3},{7,1},{8,14},{10,12},{12... | collective-permute-start | bytes 786440 | tf_op jit(solution)/shard_map/ppermute | solution.py:384
  75.5 0.0 collective-permute-done.refs_4_
  75.6 2.0 %collective-permute-start.1 = (bf16[128,1024]{1,0:T(8,128)(2,1)S(1)}, bf16[128,1024]{1,0:T(8,128)(2,1)S(1)}, u32[]{:S(2)}, u32[]{:S(2)}) collective-permute-start(bf16[128,1024]{1,0:T(8,128)(2,1)S(1)} %collective-permute-done.refs_4_), channel_id=1, source_target_pairs={{0,2},{2,0},{4,6},{6,4},{1,3},{3,1},{5,7},{7,5},{8,10},{10,8},{12,... | collective-permute-start | bytes 786440 | tf_op jit(solution)/shard_map/ppermute | solution.py:384
  77.6 0.5 collective-permute-done.2.refs_3_
  78.1 3.8 %collective-permute-start.3 = (bf16[128,1024]{1,0:T(8,128)(2,1)S(1)}, bf16[128,1024]{1,0:T(8,128)(2,1)S(1)}, u32[]{:S(2)}, u32[]{:S(2)}) collective-permute-start(bf16[128,1024]{1,0:T(8,128)(2,1)S(1)} %collective-permute-done.2.refs_3_), channel_id=1, source_target_pairs={{0,6},{2,4},{4,2},{6,0},{1,7},{3,5},{5,3},{7,1},{8,14},{10,12},{12... | collective-permute-start | bytes 786440 | tf_op jit(solution)/shard_map/ppermute | solution.py:384
  81.9 1.8 %collective-permute-done.4.refs_2_ = bf16[128,1024]{1,0:T(8,128)(2,1)S(1)} collective-permute-done((bf16[128,1024]{1,0:T(8,128)(2,1)S(1)}, bf16[128,1024]{1,0:T(8,128)(2,1)S(1)}, u32[]{:S(2)}, u32[]{:S(2)}) %collective-permute-start.4) | collective-permute-done | bytes 262176 | tf_op jit(solution)/shard_map/ppermute | solution.py:384
  83.7 0.4 collective-permute-done.5.refs_5_
  84.1 4.5 %near_chunks.1 = (f32[256,768]{1,0:T(8,128)S(1)}, f32[1,1024]{1,0:T(1,128)S(1)}, bf16[768,1024]{1,0:T(8,128)(2,1)S(1)}) custom-call(s32[8]{0:T(128)S(1)} %compare_select_fusion.1.order_ref, bf16[128,1024]{1,0:T(8,128)(2,1)S(1)} %get-tuple-element.21.refs_0_, bf16[128,1024]{1,0:T(8,128)(2,1)S(1)} %get-tuple-element.22.refs_1_, ...), custom_call_target="tpu_custom_call" | custom-call | flops 1207959552 | bytes 9437184 | tf_op jit(solution)/shard_map/near_chunks/pallas_call | solution.py:250
  88.6 0.0 copy-done
  88.6 0.0 collective-permute-done.11.other_ref
  88.7 0.0 copy-start.2
  88.7 1.2 copy-done.2
  89.8 2.4 %pair_rows.1.down_ref = bf16[1536,1024]{1,0:T(8,128)(2,1)S(1)} custom-call(s32[8]{0:T(128)S(1)} %compare_select_fusion.1.order_ref, bf16[4,192,1024]{2,1,0:T(8,128)(2,1)} %copy-done, bf16[4,192,1024]{2,1,0:T(8,128)(2,1)} %copy-done.2), custom_call_target="tpu_custom_call" | custom-call | tf_op jit(solution)/shard_map/pair_rows/pallas_call | solution.py:331
  92.3 0.0 collective-permute-done.1.top_ref
  92.3 0.0 collective-permute-done.3.low_ref
  92.3 0.7 shard_map.80
  93.0 13.8 %all-gather = bf16[1024,384]{1,0:T(8,128)(2,1)S(1)} all-gather(bf16[256,384]{1,0:T(8,128)(2,1)S(1)} %get-tuple-element.26), channel_id=2, replica_groups=mesh['x'=4,'z'=16,'chip'=4,'core'=2] {'chip'}, dimensions={0}, use_global_device_ids=true | all-gather | bytes 983040 | tf_op jit(solution)/shard_map/all_gather | solution.py:440
  106.7 1.8 %shard_map.83 = (bf16[8,64,512]{2,1,0:T(8,128)(2,1)}, f32[8,128]{1,0:T(8,128)S(1)}) custom-call(bf16[4,256,384]{2,1,0:T(8,128)(2,1)S(1)} %bitcast.8, bf16[1536,1024]{1,0:T(8,128)(2,1)S(1)} %pair_rows.1.down_ref, f32[8,128]{1,0:T(8,128)S(1)} %get-tuple-element.31.peak_in), custom_call_target="tpu_custom_call" | custom-call | tf_op jit(solution)/shard_map/pallas_call | solution.py:76
  108.6 3.5 %all-to-all-start.2 = ((bf16[8,64,512]{2,1,0:T(8,128)(2,1)}), bf16[8,64,512]{2,1,0:T(8,128)(2,1)S(1)}, u32[]{:S(2)}, u32[]{:S(2)}) async-start(bf16[8,64,512]{2,1,0:T(8,128)(2,1)} %get-tuple-element.32), calls=%async_computation.2 | async-start | bytes 1048576 | tf_op jit(solution)/shard_map/all_to_all | solution.py:448
  112.1 2.3 %collective-permute-start.12 = (f32[8,128]{1,0:T(8,128)S(1)}, f32[8,128]{1,0:T(8,128)S(1)}, u32[]{:S(2)}, u32[]{:S(2)}) collective-permute-start(f32[8,128]{1,0:T(8,128)S(1)} %get-tuple-element.33), channel_id=1, source_target_pairs={{0,1},{1,0},{2,3},{3,2},{4,5},{5,4},{6,7},{7,6},{8,9},{9,8},{10,11... | collective-permute-start | bytes 12296 | tf_op jit(solution)/shard_map/ppermute | solution.py:387
  114.4 0.5 shard_map.77
  114.8 0.3 collective-permute-done.12
  115.2 0.5 slice_bitcast_fusion
  115.7 6.6 %all-to-all-done.2.row_ref = bf16[8,64,512]{2,1,0:T(8,128)(2,1)S(1)} async-done(((bf16[8,64,512]{2,1,0:T(8,128)(2,1)}), bf16[8,64,512]{2,1,0:T(8,128)(2,1)S(1)}, u32[]{:S(2)}, u32[]{:S(2)}) %all-to-all-start.2) | async-done | bytes 524320 | tf_op jit(solution)/shard_map/all_to_all | solution.py:448
  122.3 0.4 shard_map.84
  122.8 29.7 %all_to_all.21.part_ref = bf16[16,16,512]{2,1,0:T(8,128)(2,1)S(1)} all-to-all(bf16[16,16,512]{2,1,0:T(8,128)(2,1)S(1)} %shard_map.84), channel_id=1, replica_groups=mesh['x'=4,'z'=16,'chip'=4,'core'=2] {'z'}, dimensions={0} | all-to-all | bytes 524288 | tf_op jit(solution)/shard_map/all_to_all | solution.py:457
  152.4 0.6 shard_map.85
  (3 shorter events, 0.0 us)
Async XLA Ops:
  2.3 45.2 %all-to-all-start = ((bf16[16,72,128]{2,1,0:T(8,128)(2,1)}), bf16[16,72,128]{2,1,0:T(8,128)(2,1)S(1)}, u32[]{:S(2)}, u32[]{:S(2)}) async-start(bf16[16,72,128]{2,1,0:T(8,128)(2,1)} %pack_tokens.1), calls=%async_computation | async-start | bytes 589824 | tf_op jit(solution)/shard_map/all_to_all | solution.py:395
  19.5 0.7 copy-start.1
  20.2 15.4 %collective-permute-start.10 = (bf16[192,1024]{1,0:T(8,128)(2,1)S(1)}, bf16[192,1024]{1,0:T(8,128)(2,1)S(1)}, u32[]{:S(2)}, u32[]{:S(2)}) collective-permute-start(bf16[192,1024]{1,0:T(8,128)(2,1)S(1)} %get-tuple-element.30), channel_id=1, source_target_pairs={{0,4},{2,6},{4,0},{6,2},{1,5},{3,7},{5,1},{7,3},{8,12},{10,14},{12... | collective-permute-start | bytes 1179656 | tf_op jit(solution)/shard_map/ppermute | solution.py:384
  25.3 17.4 %collective-permute-start.8 = (bf16[192,1024]{1,0:T(8,128)(2,1)S(1)}, bf16[192,1024]{1,0:T(8,128)(2,1)S(1)}, u32[]{:S(2)}, u32[]{:S(2)}) collective-permute-start(bf16[192,1024]{1,0:T(8,128)(2,1)S(1)} %get-tuple-element.28), channel_id=1, source_target_pairs={{0,2},{2,0},{4,6},{6,4},{1,3},{3,1},{5,7},{7,5},{8,10},{10,8},{12,... | collective-permute-start | bytes 1179656 | tf_op jit(solution)/shard_map/ppermute | solution.py:384
  27.9 14.8 %collective-permute-start.9 = (bf16[192,1024]{1,0:T(8,128)(2,1)S(1)}, bf16[192,1024]{1,0:T(8,128)(2,1)S(1)}, u32[]{:S(2)}, u32[]{:S(2)}) collective-permute-start(bf16[192,1024]{1,0:T(8,128)(2,1)S(1)} %get-tuple-element.29), channel_id=1, source_target_pairs={{0,6},{2,4},{4,2},{6,0},{1,7},{3,5},{5,3},{7,1},{8,14},{10,12},{12... | collective-permute-start | bytes 1179656 | tf_op jit(solution)/shard_map/ppermute | solution.py:384
  30.2 38.8 %collective-permute-start.6 = (bf16[192,4096]{1,0:T(8,128)(2,1)}, bf16[192,4096]{1,0:T(8,128)(2,1)}, u32[]{:S(2)}, u32[]{:S(2)}) collective-permute-start(bf16[192,4096]{1,0:T(8,128)(2,1)} %bitcast.2.refs_6_), channel_id=1, source_target_pairs={{0,1},{1,0},{2,3},{3,2},{4,5},{5,4},{6,7},{7,6},{8,9},{9,8},{10,11... | collective-permute-start | bytes 4718600 | tf_op jit(solution)/shard_map/ppermute | solution.py:387
  32.2 40.7 %collective-permute-start.7 = (bf16[192,4096]{1,0:T(8,128)(2,1)}, bf16[192,4096]{1,0:T(8,128)(2,1)}, u32[]{:S(2)}, u32[]{:S(2)}) collective-permute-start(bf16[192,4096]{1,0:T(8,128)(2,1)} %bitcast.3.refs_8_), channel_id=1, source_target_pairs={{0,1},{1,0},{2,3},{3,2},{4,5},{5,4},{6,7},{7,6},{8,9},{9,8},{10,11... | collective-permute-start | bytes 4718600 | tf_op jit(solution)/shard_map/ppermute | solution.py:387
  35.6 7.1 %copy-start.3 = (bf16[192,1024]{1,0:T(8,128)(2,1)}, bf16[192,1024]{1,0:T(8,128)(2,1)S(1)}, u32[]{:S(2)}) copy-start(bf16[192,1024]{1,0:T(8,128)(2,1)S(1)} %collective-permute-done.10.refs_3_) | copy-start | bytes 1179652
  42.7 0.7 copy-start.4
  42.7 0.9 copy-start.5
  45.6 43.1 %copy-start = (bf16[4,192,1024]{2,1,0:T(8,128)(2,1)}, bf16[4,192,1024]{2,1,0:T(8,128)(2,1)S(1)}, u32[]{:S(2)}) copy-start(bf16[4,192,1024]{2,1,0:T(8,128)(2,1)S(1)} %shard_map.82.own_ref) | copy-start | bytes 4718596
  45.6 43.1 %collective-permute-start.11 = (bf16[4,192,1024]{2,1,0:T(8,128)(2,1)S(1)}, bf16[4,192,1024]{2,1,0:T(8,128)(2,1)S(1)}, u32[]{:S(2)}, u32[]{:S(2)}) collective-permute-start(bf16[4,192,1024]{2,1,0:T(8,128)(2,1)S(1)} %shard_map.82.own_ref), channel_id=1, source_target_pairs={{0,1},{1,0},{2,3},{3,2},{4,5},{5,4},{6,7},{7,6},{8,9},{9,8},{10,11... | collective-permute-start | bytes 4718600 | tf_op jit(solution)/shard_map/ppermute | solution.py:387
  62.6 13.0 %collective-permute-start = (bf16[128,1024]{1,0:T(8,128)(2,1)S(1)}, bf16[128,1024]{1,0:T(8,128)(2,1)S(1)}, u32[]{:S(2)}, u32[]{:S(2)}) collective-permute-start(bf16[128,1024]{1,0:T(8,128)(2,1)S(1)} %get-tuple-element.21.refs_0_), channel_id=1, source_target_pairs={{0,6},{2,4},{4,2},{6,0},{1,7},{3,5},{5,3},{7,1},{8,14},{10,12},{12... | collective-permute-start | bytes 786440 | tf_op jit(solution)/shard_map/ppermute | solution.py:384
  67.0 11.1 %collective-permute-start.2 = (bf16[128,1024]{1,0:T(8,128)(2,1)S(1)}, bf16[128,1024]{1,0:T(8,128)(2,1)S(1)}, u32[]{:S(2)}, u32[]{:S(2)}) collective-permute-start(bf16[128,1024]{1,0:T(8,128)(2,1)S(1)} %get-tuple-element.22.refs_1_), channel_id=1, source_target_pairs={{0,2},{2,0},{4,6},{6,4},{1,3},{3,1},{5,7},{7,5},{8,10},{10,8},{12,... | collective-permute-start | bytes 786440 | tf_op jit(solution)/shard_map/ppermute | solution.py:384
  69.1 14.6 %collective-permute-start.4 = (bf16[128,1024]{1,0:T(8,128)(2,1)S(1)}, bf16[128,1024]{1,0:T(8,128)(2,1)S(1)}, u32[]{:S(2)}, u32[]{:S(2)}) collective-permute-start(bf16[128,1024]{1,0:T(8,128)(2,1)S(1)} %get-tuple-element.21.refs_0_), channel_id=1, source_target_pairs={{0,2},{2,0},{4,6},{6,4},{1,3},{3,1},{5,7},{7,5},{8,10},{10,8},{12,... | collective-permute-start | bytes 786440 | tf_op jit(solution)/shard_map/ppermute | solution.py:384
  72.9 11.2 %collective-permute-start.5 = (bf16[128,1024]{1,0:T(8,128)(2,1)S(1)}, bf16[128,1024]{1,0:T(8,128)(2,1)S(1)}, u32[]{:S(2)}, u32[]{:S(2)}) collective-permute-start(bf16[128,1024]{1,0:T(8,128)(2,1)S(1)} %get-tuple-element.22.refs_1_), channel_id=1, source_target_pairs={{0,6},{2,4},{4,2},{6,0},{1,7},{3,5},{5,3},{7,1},{8,14},{10,12},{12... | collective-permute-start | bytes 786440 | tf_op jit(solution)/shard_map/ppermute | solution.py:384
  75.6 16.7 %collective-permute-start.1 = (bf16[128,1024]{1,0:T(8,128)(2,1)S(1)}, bf16[128,1024]{1,0:T(8,128)(2,1)S(1)}, u32[]{:S(2)}, u32[]{:S(2)}) collective-permute-start(bf16[128,1024]{1,0:T(8,128)(2,1)S(1)} %collective-permute-done.refs_4_), channel_id=1, source_target_pairs={{0,2},{2,0},{4,6},{6,4},{1,3},{3,1},{5,7},{7,5},{8,10},{10,8},{12,... | collective-permute-start | bytes 786440 | tf_op jit(solution)/shard_map/ppermute | solution.py:384
  78.1 14.2 %collective-permute-start.3 = (bf16[128,1024]{1,0:T(8,128)(2,1)S(1)}, bf16[128,1024]{1,0:T(8,128)(2,1)S(1)}, u32[]{:S(2)}, u32[]{:S(2)}) collective-permute-start(bf16[128,1024]{1,0:T(8,128)(2,1)S(1)} %collective-permute-done.2.refs_3_), channel_id=1, source_target_pairs={{0,6},{2,4},{4,2},{6,0},{1,7},{3,5},{5,3},{7,1},{8,14},{10,12},{12... | collective-permute-start | bytes 786440 | tf_op jit(solution)/shard_map/ppermute | solution.py:384
  88.7 1.2 copy-start.2
  108.6 13.7 %all-to-all-start.2 = ((bf16[8,64,512]{2,1,0:T(8,128)(2,1)}), bf16[8,64,512]{2,1,0:T(8,128)(2,1)S(1)}, u32[]{:S(2)}, u32[]{:S(2)}) async-start(bf16[8,64,512]{2,1,0:T(8,128)(2,1)} %get-tuple-element.32), calls=%async_computation.2 | async-start | bytes 1048576 | tf_op jit(solution)/shard_map/all_to_all | solution.py:448
  112.1 3.1 %collective-permute-start.12 = (f32[8,128]{1,0:T(8,128)S(1)}, f32[8,128]{1,0:T(8,128)S(1)}, u32[]{:S(2)}, u32[]{:S(2)}) collective-permute-start(f32[8,128]{1,0:T(8,128)S(1)} %get-tuple-element.33), channel_id=1, source_target_pairs={{0,1},{1,0},{2,3},{3,2},{4,5},{5,4},{6,7},{7,6},{8,9},{9,8},{10,11... | collective-permute-start | bytes 12296 | tf_op jit(solution)/shard_map/ppermute | solution.py:387
